TPU v7x, 256 devices: a whole 4x4x8 slice. The times are simulated.
256 devices in a mesh: mem: 4 (over x), cell: 64 (over y, z, core).
Axes of the slice: x: 4, y: 4, z: 8, core: 2. Of those that a mesh axis runs over, the one named last changes fastest.
Arguments:
- state: bfloat16 [131072, 40, 120], P('cell', 'mem'), may hold values from -6 to 6
- vertical_weight: bfloat16 [65536, 120], P('cell'), may hold values from -0.5 to 0.5
- horizontal_weight: float32 [65536, 4], P('cell'), may hold values from 0.05 to 0.45
- obs_slot: int32 [65536, 4], P('cell'), may hold values from 0 to 4095, as said below
- request_cell: int32 [64, 4096], P('cell'), may hold values from 0 to 2047
- obs_value: float32 [65536], P('cell'), may hold values from -6 to 6
- obs_error: float32 [65536], P('cell'), may hold values from 0.5 to 2
- obs_region: int32 [65536], P('cell'), may hold values from 0 to 511, as said below
Outputs:
- cov_matrix: float32 [512, 40, 40], P('cell', 'mem')
- innovation_proj: float32 [512, 40], P('cell', 'mem')
Inputs may be any that keep to these rules, and one draw needn't show every extreme that they name: `obs_slot`: within one owner's 1024 observations all 4096 slots differ, so every slot is used: 1024 ask the owner's own patch and 768 each of the four patches at distance 1 and 2. `obs_region`: an observation's region is one of the 8 regions of its owner's patch or of the patches just before or after it (indices wrap); patch p holds regions p * 8 to p * 8 + 7.
All inputs are finite; a program needn't handle non-finite values.
Results may differ from a plain program's by a relative error of at most 0.0003.
Values may be sent and summed in bfloat16 or wider, within the bound.
No kernel may reach another device: no remote copies, remote signals or barrier semaphores. Data moves between devices by JAX's collectives and lax.ppermute only.
A program may use at most 128 MiB of HBM per device.

v0:
```python
import jax
import jax.numpy as jnp
from jax import lax
from jax.experimental import pallas as pl
from jax.experimental.pallas import tpu as pltpu
from jax.sharding import PartitionSpec as P

REG_DEV = 8
HALO_MOVES = (-2, -1, 1, 2)
TILE = 256
F32 = jnp.float32
BF16 = jnp.bfloat16
NT = (((1,), (1,)), ((), ()))
VMEM = pl.BlockSpec(memory_space=pltpu.VMEM)
SMEM = pl.BlockSpec(memory_space=pltpu.SMEM)


def passed_along(x, axis, by):
    devices = lax.axis_size(axis)
    return lax.ppermute(x, axis, [(i, (i + by) % devices) for i in range(devices)])


def row_stride(cells):
    return cells + 4


def slot_owner(slot_ref):
    neigh, obs = slot_ref.shape
    tops = neigh * obs // 128
    o = lax.broadcasted_iota(jnp.int32, (1, obs), 1)
    upper, lower = (o >> 5).astype(F32), (o & 31).astype(F32)
    row_top = lax.broadcasted_iota(jnp.int32, (tops, obs), 0)
    row_low = lax.broadcasted_iota(jnp.int32, (128, obs), 0)
    total = jnp.zeros((2 * tops, 128), F32)
    for k in range(neigh):
        s = slot_ref[k : k + 1, :]
        hit = row_top == (s >> 7)
        lhs = jnp.concatenate(
            [jnp.where(hit, upper, 0.0), jnp.where(hit, lower, 0.0)], axis=0
        ).astype(BF16)
        rhs = jnp.where(row_low == (s & 127), 1.0, 0.0).astype(BF16)
        total += lax.dot_general(lhs, rhs, NT, preferred_element_type=F32)
    return (32.0 * total[:tops] + total[tops:]).astype(jnp.int32)


def slot_weights(inv_ref, table_ref, vw_ref, tile):
    levels, obs = vw_ref.shape
    key = jnp.concatenate([inv_ref[2 * tile : 2 * tile + 1, :], inv_ref[2 * tile + 1 : 2 * tile + 2, :]], axis=1)
    ids = lax.broadcasted_iota(jnp.int32, (obs, TILE), 0)
    pick = jnp.where(ids == key, 1.0, 0.0).astype(BF16)
    w = jnp.dot(vw_ref[...], pick, preferred_element_type=F32)
    cells = table_ref[0:1, tile * TILE : (tile + 1) * TILE]
    sub = lax.broadcasted_iota(jnp.int32, (128 - levels, TILE), 0)
    extra = jnp.where(sub == 0, (cells >> 3).astype(F32), jnp.where(sub == 1, (cells & 7).astype(F32), 0.0))
    return jnp.concatenate([w, extra], axis=0).astype(BF16)


def ask_kernel(slot_ref, table_ref, vw_ref, inv_ref, *out_refs):
    obs = vw_ref.shape[1]
    inv_ref[...] = slot_owner(slot_ref)
    tile = obs // TILE
    for out in out_refs:
        for part in range(out.shape[1] // TILE):
            out[:, part * TILE : (part + 1) * TILE] = slot_weights(inv_ref, table_ref, vw_ref, tile)
            tile += 1


def answer_tile(cell_of, w, turned_ref, cells_dim):
    S = row_stride(cells_dim)
    half = TILE // 2
    lane = lax.broadcasted_iota(jnp.int32, (8, TILE), 1) & (half - 1)
    sub = lax.broadcasted_iota(jnp.int32, (8, 128), 0)
    wide = lax.broadcasted_iota(jnp.int32, (128, TILE), 1)
    zero = jnp.zeros_like(w)
    rhs = jnp.concatenate([jnp.where(wide < half, w, zero), jnp.where(wide < half, zero, w)], axis=0)
    first, second = [], []
    for h in range(2):
        a_rows, b_rows = [], []
        for q in range(half // 4):
            got = None
            for j in range(4):
                c = cell_of(h * half + 4 * q + j)
                a_rows.append(turned_ref[pl.ds(c, 8, stride=S), :])
                b = turned_ref[pl.ds(c + (8 - 2 * j) * S, 8, stride=S), :]
                got = b if got is None else jnp.where(sub >= 2 * j, b, got)
            b_rows.append(got)
        first.append(jnp.concatenate(a_rows, axis=0).astype(BF16))
        second.append(jnp.concatenate(b_rows, axis=0).astype(BF16))
    lhs_a = jnp.concatenate(first, axis=1)
    lhs_b = jnp.concatenate(second, axis=1)
    d_a = jnp.dot(lhs_a, rhs, preferred_element_type=F32)
    d_b = jnp.dot(lhs_b, rhs, preferred_element_type=F32)
    out_a = jnp.zeros((8, TILE), F32)
    for r in range(half):
        out_a = jnp.where(lane == r, d_a[8 * r : 8 * r + 8, :], out_a)
    out_b = jnp.zeros((8, TILE), F32)
    near = lane - (lax.broadcasted_iota(jnp.int32, (8, TILE), 0) >> 1)
    for q in range(half // 4):
        out_b = jnp.where(near == 4 * q, d_b[8 * q : 8 * q + 8, :], out_b)
    return jnp.concatenate([out_a, out_b], axis=0)


def own_kernel(state_ref, cell_ref, inv_ref, table_ref, vw_ref, turned_ref, eq_ref):
    members, levels, cells = state_ref.shape
    S = row_stride(cells)
    r = lax.broadcasted_iota(jnp.int32, (TILE, TILE), 0)
    eye = jnp.where(r == lax.broadcasted_iota(jnp.int32, (TILE, TILE), 1), 1.0, 0.0).astype(BF16)
    pad = jnp.zeros((TILE, 128 - levels), F32)
    for m in range(members):
        for part in range(cells // TILE):
            block = state_ref[m, :, part * TILE : (part + 1) * TILE]
            flat = lax.dot_general(eye, block, NT, preferred_element_type=F32)
            turned_ref[m * S + part * TILE : m * S + (part + 1) * TILE, :] = jnp.concatenate([flat, pad], axis=1)
    keep = lax.broadcasted_iota(jnp.int32, (128, TILE), 0) < levels
    for tile in range(eq_ref.shape[1] // TILE):
        w = slot_weights(inv_ref, table_ref, vw_ref, tile)
        w = jnp.where(keep, w, jnp.zeros_like(w))
        eq_ref[:, tile * TILE : (tile + 1) * TILE] = answer_tile(
            lambda i: cell_ref[0, tile * TILE + i], w, turned_ref, cells
        )


def halo_kernel(levels, cells, turned_ref, w_ref, eq_ref, words, scalars, sem):
    tail = w_ref[112:128, :].astype(F32)
    row = levels - 112
    words[...] = (8.0 * tail[row : row + 1, :] + tail[row + 1 : row + 2, :]).astype(jnp.int32)
    copy = pltpu.make_async_copy(words, scalars, sem)
    copy.start()
    copy.wait()
    keep = lax.broadcasted_iota(jnp.int32, (128, TILE), 0) < levels

    def step(tile, carry):
        at = pl.multiple_of(tile * TILE, TILE)
        w = w_ref[:, pl.ds(at, TILE)]
        w = jnp.where(keep, w, jnp.zeros_like(w))
        eq_ref[:, pl.ds(at, TILE)] = answer_tile(lambda i: scalars[0, at + i], w, turned_ref, cells)
        return carry

    lax.fori_loop(0, eq_ref.shape[1] // TILE, step, 0)


def combine_kernel(slot_ref, hw_ref, *refs):
    out_ref = refs[-1]
    neigh, obs = slot_ref.shape
    sub = lax.broadcasted_iota(jnp.int32, (8, 128), 0)
    tops, pairs = [], []
    for ref in refs[:-1]:
        for part in range(ref.shape[1] // 128):
            tops.append(ref[0:8, part * 128 : (part + 1) * 128])
            x = ref[8:16, part * 128 : (part + 1) * 128]
            x = x + pltpu.roll(x, 4, 0)
            pairs.append(x + pltpu.roll(x, 2, 0))
    quads = []
    for q in range(len(pairs) // 4):
        x = pairs[4 * q]
        for j in range(1, 4):
            x = jnp.where(sub >= 2 * j, pairs[4 * q + j], x)
        quads.append(x)
    for block in range(obs // 128):
        at = slice(block * 128, (block + 1) * 128)
        a_sum = jnp.zeros((8, 128), F32)
        b_sum = jnp.zeros((8, 128), F32)
        for k in range(neigh):
            s = jnp.broadcast_to(slot_ref[k : k + 1, at], (8, 128))
            low, top = s & 127, s >> 7
            a = jnp.zeros((8, 128), F32)
            for i, x in enumerate(tops):
                a = jnp.where(top == i, jnp.take_along_axis(x, low, axis=1, mode="promise_in_bounds"), a)
            b = jnp.zeros((8, 128), F32)
            top4 = top >> 2
            for i, x in enumerate(quads):
                b = jnp.where(top4 == i, jnp.take_along_axis(x, low, axis=1, mode="promise_in_bounds"), b)
            b = jnp.where((top & 3) == (sub >> 1), b, 0.0)
            h = hw_ref[k : k + 1, at]
            a_sum += a * h
            b_sum += b * h
        b_sum = b_sum + pltpu.roll(b_sum, 4, 0)
        b_sum = b_sum + pltpu.roll(b_sum, 2, 0)
        out_ref[0:8, at] = a_sum
        out_ref[8:16, at] = jnp.where(sub < 2, b_sum, 0.0)


def split(x):
    top = x.astype(BF16)
    return top, (x - top.astype(F32)).astype(BF16)


def cov_kernel(members, own_ref, r1_ref, r2_ref, r3_ref, value_ref, error_ref, rel_ref, mid_ref, prev_ref, next_ref):
    mem_dev = members // 4
    obs = own_ref.shape[1]
    blocks = [own_ref[...], r1_ref[...], r2_ref[...], r3_ref[...]]
    total = blocks[0] + blocks[1] + blocks[2] + blocks[3]
    mean = jnp.sum(total, axis=0, keepdims=True) * (1.0 / members)
    err = error_ref[...]
    inverse = 1.0 / (err * err)
    innov = (value_ref[...] - mean) * inverse
    row = lax.broadcasted_iota(jnp.int32, (16, obs), 0)
    spread = [jnp.where(row < mem_dev, x - mean, 0.0) for x in blocks]
    right = [x * inverse for x in spread]
    right[0] = jnp.where(row == mem_dev, innov, right[0])
    r_top, r_low = split(jnp.concatenate(right, axis=0))
    rel = rel_ref[...]
    region = lax.broadcasted_iota(jnp.int32, (REG_DEV, obs), 0)
    own = spread[0]
    own_low = own - own.astype(BF16).astype(F32)
    for g, out_ref in ((0, prev_ref), (2, next_ref), (1, mid_ref)):
        mask = rel == region + g * REG_DEV
        l_top = jnp.concatenate([jnp.where(mask, own[m : m + 1, :], 0.0) for m in range(mem_dev)], axis=0).astype(BF16)
        l_low = jnp.concatenate([jnp.where(mask, own_low[m : m + 1, :], 0.0) for m in range(mem_dev)], axis=0).astype(BF16)
        d = lax.dot_general(l_top, r_top, NT, preferred_element_type=F32)
        d += lax.dot_general(l_top, r_low, NT, preferred_element_type=F32)
        d += lax.dot_general(l_low, r_top, NT, preferred_element_type=F32)
        out_ref[...] = d


def final_kernel(mem_ref, mid_ref, a_ref, b_ref, cov_ref, proj_ref):
    mem_dev, regions, members = cov_ref.shape
    d = mid_ref[...] + a_ref[...] + b_ref[...]
    width = d.shape[1]
    i = lax.broadcasted_iota(jnp.int32, (width, members), 0)
    j = lax.broadcasted_iota(jnp.int32, (width, members), 1)
    block = (mem_ref[0] + 4 - (i >> 4)) & 3
    place = jnp.where(((i & 15) < mem_dev) & (block * mem_dev + (i & 15) == j), 1.0, 0.0)
    cov = jnp.dot(d, place, precision=lax.Precision.HIGHEST, preferred_element_type=F32)
    lane = lax.broadcasted_iota(jnp.int32, (regions, mem_dev), 1)
    proj = jnp.zeros((regions, mem_dev), F32)
    for m in range(mem_dev):
        cov_ref[m] = cov[m * regions : (m + 1) * regions, :]
        proj = jnp.where(lane == m, d[m * regions : (m + 1) * regions, mem_dev : mem_dev + 1], proj)
    proj_ref[...] = proj


def on_device(state, vertical_weight, horizontal_weight, obs_slot, request_cell, obs_value, obs_error, obs_region):
    patches = lax.axis_size("cell")
    here = lax.axis_index("cell")
    cells, mem_dev, levels = state.shape
    members = mem_dev * lax.axis_size("mem")
    obs, neigh = obs_slot.shape
    halo = 3 * obs // 4
    state_t = jnp.transpose(state, (1, 2, 0))
    vw_t, hw_t, slot_t = vertical_weight.T, horizontal_weight.T, obs_slot.T
    params = pltpu.CompilerParams(vmem_limit_bytes=40 * 1024 * 1024)

    inv, *asks = pl.pallas_call(
        ask_kernel,
        out_shape=[jax.ShapeDtypeStruct((neigh * obs // 128, 128), jnp.int32)]
        + [jax.ShapeDtypeStruct((128, halo), BF16)] * 4,
        in_specs=[VMEM] * 3,
        out_specs=[VMEM] * 5,
        compiler_params=params,
        name="ask",
    )(slot_t, request_cell, vw_t)
    arrived = [passed_along(w, "cell", by) for w, by in zip(asks, HALO_MOVES)]
    turned, eq_own = pl.pallas_call(
        own_kernel,
        out_shape=[
            jax.ShapeDtypeStruct((16 * row_stride(cells), 128), F32),
            jax.ShapeDtypeStruct((16, obs), F32),
        ],
        in_specs=[VMEM, SMEM, VMEM, VMEM, VMEM],
        out_specs=[VMEM] * 2,
        compiler_params=params,
        cost_estimate=pl.CostEstimate(flops=8_000_000_000, bytes_accessed=10_000_000, transcendentals=0),
        name="own",
    )(state_t, request_cell, inv, request_cell, vw_t)
    answer = pl.pallas_call(
        lambda *refs: halo_kernel(levels, cells, *refs),
        out_shape=jax.ShapeDtypeStruct((16, halo), F32),
        in_specs=[VMEM] * 2,
        out_specs=VMEM,
        scratch_shapes=[
            pltpu.VMEM((1, halo), jnp.int32),
            pltpu.SMEM((1, halo), jnp.int32),
            pltpu.SemaphoreType.DMA,
        ],
        compiler_params=params,
        cost_estimate=pl.CostEstimate(flops=2_000_000_000, bytes_accessed=1_000_000, transcendentals=0),
        name="answer",
    )
    back = [passed_along(answer(turned, w), "cell", -by) for w, by in zip(arrived, HALO_MOVES)]
    own = pl.pallas_call(
        combine_kernel,
        out_shape=jax.ShapeDtypeStruct((16, obs), F32),
        in_specs=[VMEM] * 7,
        out_specs=VMEM,
        compiler_params=params,
        name="combine",
    )(slot_t, hw_t, eq_own, *back)
    others = [passed_along(own, "mem", by) for by in (1, 2, 3)]
    rel = jnp.mod(obs_region - (here - 1) * REG_DEV, patches * REG_DEV)
    wide = 4 * 16
    mid, to_prev, to_next = pl.pallas_call(
        lambda *refs: cov_kernel(members, *refs),
        out_shape=[jax.ShapeDtypeStruct((mem_dev * REG_DEV, wide), F32)] * 3,
        in_specs=[VMEM] * 7,
        out_specs=[VMEM] * 3,
        compiler_params=params,
        name="cov",
    )(own, *others, obs_value.reshape(1, obs), obs_error.reshape(1, obs), rel.reshape(1, obs))
    from_prev = passed_along(to_next, "cell", 1)
    from_next = passed_along(to_prev, "cell", -1)
    cov, proj = pl.pallas_call(
        final_kernel,
        out_shape=[
            jax.ShapeDtypeStruct((mem_dev, REG_DEV, members), F32),
            jax.ShapeDtypeStruct((REG_DEV, mem_dev), F32),
        ],
        in_specs=[SMEM, VMEM, VMEM, VMEM],
        out_specs=[VMEM] * 2,
        compiler_params=params,
        name="final",
    )(lax.axis_index("mem").reshape(1).astype(jnp.int32), mid, from_prev, from_next)
    return (jnp.transpose(cov, (1, 0, 2)), proj)


def solution(mesh):
    in_specs = (
        P("cell", "mem", None),
        P("cell", None),
        P("cell", None),
        P("cell", None),
        P("cell", None),
        P("cell"),
        P("cell"),
        P("cell"),
    )
    out_specs = (P("cell", "mem", None), P("cell", "mem"))
    return jax.shard_map(
        on_device, mesh=mesh, in_specs=in_specs, out_specs=out_specs, check_vma=False
    )
```

profile of v0, /device:TPU:4, one launch (start us, length us, event | category | flops | bytes accessed | tf_op | source)
XLA Modules:
  0.0 88.4 jit_solution(10013641730634959401)
XLA Ops:
  0.6 0.0 copy-start
  0.6 0.9 %copy-done = bf16[1024,120]{0,1:T(8,128)(2,1)S(1)} copy-done((bf16[1024,120]{0,1:T(8,128)(2,1)S(1)}, bf16[1024,120]{0,1:T(8,128)(2,1)}, u32[]{:S(2)}) %copy-start) | copy-done | bytes 245784
  1.6 0.0 copy-start.2
  1.6 0.7 copy-done.2
  2.3 0.0 copy-start.4
  2.3 0.7 copy-done.4
  3.0 2.0 %ask.1 = (s32[32,128]{1,0:T(8,128)S(1)}, bf16[128,768]{1,0:T(8,128)(2,1)S(1)}, bf16[128,768]{1,0:T(8,128)(2,1)S(1)}, bf16[128,768]{1,0:T(8,128)(2,1)S(1)}, bf16[128,768]{1,0:T(8,128)(2,1)S(1)}) custom-call(s32[4,1024]{1,0:T(4,128)S(1)} %bitcast.11, s32[1,4096]{1,0:T(1,128)S(1)} %copy-done.4, bf16[120,1024]{1,0:T(8,128)(2,1)S(1)} %bitcast.9), custom_call_target="tpu_custom_call" | custom-call | tf_op jit(solution)/shard_map/ask/pallas_call | solution.py:244
  5.0 8.4 %collective-permute-start = (bf16[128,768]{1,0:T(8,128)(2,1)S(1)}, bf16[128,768]{1,0:T(8,128)(2,1)S(1)}, u32[]{:S(2)}, u32[]{:S(2)}) collective-permute-start(bf16[128,768]{1,0:T(8,128)(2,1)S(1)} %get-tuple-element.17), channel_id=1, source_target_pairs={{0,62},{1,63},{2,0},{3,1},{4,2},{5,3},{6,4},{7,5},{8,6},{9,7},{10,... | collective-permute-start | bytes 589832 | tf_op jit(solution)/shard_map/ppermute | solution.py:20
  13.4 0.2 collective-permute-start.2
  13.6 0.3 collective-permute-start.4
  13.9 0.7 collective-permute-start.6
  14.6 0.0 copy-start.1
  14.6 0.9 %copy-done.1 = bf16[1024,120]{0,1:T(8,128)(2,1)S(1)} copy-done((bf16[1024,120]{0,1:T(8,128)(2,1)S(1)}, bf16[1024,120]{0,1:T(8,128)(2,1)}, u32[]{:S(2)}) %copy-start.1) | copy-done | bytes 245784
  15.5 0.0 copy-start.5
  15.5 0.7 copy-done.5
  16.2 0.0 copy-start.9
  16.2 2.4 %copy-done.9 = bf16[2048,10,120]{0,2,1:T(8,128)(2,1)S(1)} copy-done((bf16[2048,10,120]{0,2,1:T(8,128)(2,1)S(1)}, bf16[2048,10,120]{0,2,1:T(8,128)(2,1)}, u32[]{:S(2)}) %copy-start.9) | copy-done | bytes 4915224
  18.6 11.4 %own.1 = (f32[32832,128]{1,0:T(8,128)}, f32[16,1024]{1,0:T(8,128)S(1)}) custom-call(bf16[10,120,2048]{2,1,0:T(8,128)(2,1)S(1)} %bitcast.17, s32[1,4096]{1,0:T(1,128)S(1)} %copy-done.5, s32[32,128]{1,0:T(8,128)S(1)} %get-tuple-element.14.inv_ref, s32[1,4096]{1,0:T(1,128)S(1)} %copy-done.5, bf16[120,1024]{1,0:T(8,128)(2,1)S(1)} %bitcast.10), custom_call_target="tpu_custom_call" | custom-call | flops 8000000000 | bytes 10000000 | tf_op jit(solution)/shard_map/own/pallas_call | solution.py:254
  30.0 0.0 collective-permute-done.refs_1_
  30.0 7.8 %answer.4 = f32[16,768]{1,0:T(8,128)S(1)} custom-call(f32[32832,128]{1,0:T(8,128)} %get-tuple-element.16.refs_0_, bf16[128,768]{1,0:T(8,128)(2,1)S(1)} %collective-permute-done.refs_1_), custom_call_target="tpu_custom_call" | custom-call | flops 2000000000 | bytes 1000000 | tf_op jit(solution)/shard_map/answer/pallas_call | solution.py:280
  37.9 0.1 collective-permute-start.1
  37.9 0.0 collective-permute-done.2.refs_1_
  38.0 7.8 %answer.5 = f32[16,768]{1,0:T(8,128)S(1)} custom-call(f32[32832,128]{1,0:T(8,128)} %get-tuple-element.16.refs_0_, bf16[128,768]{1,0:T(8,128)(2,1)S(1)} %collective-permute-done.2.refs_1_), custom_call_target="tpu_custom_call" | custom-call | flops 2000000000 | bytes 1000000 | tf_op jit(solution)/shard_map/answer/pallas_call | solution.py:280
  45.8 0.0 copy-start.3
  45.8 0.0 copy-start.6
  45.8 0.0 copy-start.10
  45.8 0.0 copy-start.7
  45.8 0.0 copy-start.8
  45.8 0.4 collective-permute-start.3
  46.2 0.0 collective-permute-done.4.refs_1_
  46.2 7.8 %answer.6 = f32[16,768]{1,0:T(8,128)S(1)} custom-call(f32[32832,128]{1,0:T(8,128)} %get-tuple-element.16.refs_0_, bf16[128,768]{1,0:T(8,128)(2,1)S(1)} %collective-permute-done.4.refs_1_), custom_call_target="tpu_custom_call" | custom-call | flops 2000000000 | bytes 1000000 | tf_op jit(solution)/shard_map/answer/pallas_call | solution.py:280
  54.0 5.0 %collective-permute-start.5 = (f32[16,768]{1,0:T(8,128)S(1)}, f32[16,768]{1,0:T(8,128)S(1)}, u32[]{:S(2)}, u32[]{:S(2)}) collective-permute-start(f32[16,768]{1,0:T(8,128)S(1)} %answer.6), channel_id=1, source_target_pairs={{0,63},{1,0},{2,1},{3,2},{4,3},{5,4},{6,5},{7,6},{8,7},{9,8},{10,9... | collective-permute-start | bytes 147464 | tf_op jit(solution)/shard_map/ppermute | solution.py:20
  59.1 0.0 collective-permute-done.6.refs_1_
  59.1 7.8 %answer.7 = f32[16,768]{1,0:T(8,128)S(1)} custom-call(f32[32832,128]{1,0:T(8,128)} %get-tuple-element.16.refs_0_, bf16[128,768]{1,0:T(8,128)(2,1)S(1)} %collective-permute-done.6.refs_1_), custom_call_target="tpu_custom_call" | custom-call | flops 2000000000 | bytes 1000000 | tf_op jit(solution)/shard_map/answer/pallas_call | solution.py:280
  66.9 2.1 %collective-permute-start.7 = (f32[16,768]{1,0:T(8,128)S(1)}, f32[16,768]{1,0:T(8,128)S(1)}, u32[]{:S(2)}, u32[]{:S(2)}) collective-permute-start(f32[16,768]{1,0:T(8,128)S(1)} %answer.7), channel_id=1, source_target_pairs={{0,62},{1,63},{2,0},{3,1},{4,2},{5,3},{6,4},{7,5},{8,6},{9,7},{10,... | collective-permute-start | bytes 147464 | tf_op jit(solution)/shard_map/ppermute | solution.py:20
  69.0 0.0 collective-permute-done.1.refs_1_
  69.0 0.0 collective-permute-done.3.refs_2_
  69.0 0.0 collective-permute-done.5.refs_3_
  69.0 2.1 %collective-permute-done.7.refs_4_ = f32[16,768]{1,0:T(8,128)S(1)} collective-permute-done((f32[16,768]{1,0:T(8,128)S(1)}, f32[16,768]{1,0:T(8,128)S(1)}, u32[]{:S(2)}, u32[]{:S(2)}) %collective-permute-start.7) | collective-permute-done | bytes 49184 | tf_op jit(solution)/shard_map/ppermute | solution.py:20
  71.1 0.0 copy-done.3
  71.1 0.0 copy-done.6
  71.1 1.5 %combine.1.refs_0_ = f32[16,1024]{1,0:T(8,128)S(1)} custom-call(s32[4,1024]{1,0:T(4,128)S(1)} %bitcast.12, f32[4,1024]{1,0:T(4,128)S(1)} %bitcast.14, f32[16,1024]{1,0:T(8,128)S(1)} %get-tuple-element.15.refs_0_, f32[16,768]{1,0:T(8,128)S(1)} %collective-permute-done.1.refs_1_, f32[16,768]{1,0:T(8,128)S(1)} %collective-permute-done.3.refs_2_, ...), custom_call_target="tpu_custom_call" | custom-call | tf_op jit(solution)/shard_map/combine/pallas_call | solution.py:281
  72.6 0.6 collective-permute-start.10
  73.2 2.7 %collective-permute-start.9 = (f32[16,1024]{1,0:T(8,128)S(1)}, f32[16,1024]{1,0:T(8,128)S(1)}, u32[]{:S(2)}, u32[]{:S(2)}) collective-permute-start(f32[16,1024]{1,0:T(8,128)S(1)} %combine.1.refs_0_), channel_id=1, source_target_pairs={{0,128},{64,192},{128,0},{192,64},{1,129},{65,193},{129,1},{193,65... | collective-permute-start | bytes 196616 | tf_op jit(solution)/shard_map/ppermute | solution.py:20
  75.9 0.0 collective-permute-start.8
  76.0 0.0 copy-done.10
  76.0 1.0 %collective-permute-done.10.refs_3_ = f32[16,1024]{1,0:T(8,128)S(1)} collective-permute-done((f32[16,1024]{1,0:T(8,128)S(1)}, f32[16,1024]{1,0:T(8,128)S(1)}, u32[]{:S(2)}, u32[]{:S(2)}) %collective-permute-start.10) | collective-permute-done | bytes 65568 | tf_op jit(solution)/shard_map/ppermute | solution.py:20
  76.9 2.0 %collective-permute-done.9.refs_2_ = f32[16,1024]{1,0:T(8,128)S(1)} collective-permute-done((f32[16,1024]{1,0:T(8,128)S(1)}, f32[16,1024]{1,0:T(8,128)S(1)}, u32[]{:S(2)}, u32[]{:S(2)}) %collective-permute-start.9) | collective-permute-done | bytes 65568 | tf_op jit(solution)/shard_map/ppermute | solution.py:20
  79.0 1.2 %collective-permute-done.8.refs_1_ = f32[16,1024]{1,0:T(8,128)S(1)} collective-permute-done((f32[16,1024]{1,0:T(8,128)S(1)}, f32[16,1024]{1,0:T(8,128)S(1)}, u32[]{:S(2)}, u32[]{:S(2)}) %collective-permute-start.8) | collective-permute-done | bytes 65568 | tf_op jit(solution)/shard_map/ppermute | solution.py:20
  80.2 0.0 copy-done.7
  80.2 0.0 copy-done.8
  80.2 0.6 cov.1
  80.8 0.1 collective-permute-start.11
  80.9 5.1 %collective-permute-start.12 = (f32[80,64]{1,0:T(8,128)S(1)}, f32[80,64]{1,0:T(8,128)S(1)}, u32[]{:S(2)}, u32[]{:S(2)}) collective-permute-start(f32[80,64]{1,0:T(8,128)S(1)} %get-tuple-element.23), channel_id=1, source_target_pairs={{0,63},{1,0},{2,1},{3,2},{4,3},{5,4},{6,5},{7,6},{8,7},{9,8},{10,9... | collective-permute-start | bytes 61448 | tf_op jit(solution)/shard_map/ppermute | solution.py:20
  85.9 1.7 %collective-permute-done.11.a_ref = f32[80,64]{1,0:T(8,128)S(1)} collective-permute-done((f32[80,64]{1,0:T(8,128)S(1)}, f32[80,64]{1,0:T(8,128)S(1)}, u32[]{:S(2)}, u32[]{:S(2)}) %collective-permute-start.11) | collective-permute-done | bytes 20512 | tf_op jit(solution)/shard_map/ppermute | solution.py:20
  87.6 0.0 collective-permute-done.12.b_ref
  87.6 0.8 final.1
  (1 shorter events, 0.0 us)
Async XLA Ops:
  0.6 0.9 %copy-start = (bf16[1024,120]{0,1:T(8,128)(2,1)S(1)}, bf16[1024,120]{0,1:T(8,128)(2,1)}, u32[]{:S(2)}) copy-start(bf16[1024,120]{0,1:T(8,128)(2,1)} %param.9) | copy-start | bytes 737284
  1.6 0.7 copy-start.2
  2.3 0.7 copy-start.4
  5.0 25.0 %collective-permute-start = (bf16[128,768]{1,0:T(8,128)(2,1)S(1)}, bf16[128,768]{1,0:T(8,128)(2,1)S(1)}, u32[]{:S(2)}, u32[]{:S(2)}) collective-permute-start(bf16[128,768]{1,0:T(8,128)(2,1)S(1)} %get-tuple-element.17), channel_id=1, source_target_pairs={{0,62},{1,63},{2,0},{3,1},{4,2},{5,3},{6,4},{7,5},{8,6},{9,7},{10,... | collective-permute-start | bytes 589832 | tf_op jit(solution)/shard_map/ppermute | solution.py:20
  13.4 24.6 %collective-permute-start.2 = (bf16[128,768]{1,0:T(8,128)(2,1)S(1)}, bf16[128,768]{1,0:T(8,128)(2,1)S(1)}, u32[]{:S(2)}, u32[]{:S(2)}) collective-permute-start(bf16[128,768]{1,0:T(8,128)(2,1)S(1)} %get-tuple-element.18), channel_id=1, source_target_pairs={{0,63},{1,0},{2,1},{3,2},{4,3},{5,4},{6,5},{7,6},{8,7},{9,8},{10,9... | collective-permute-start | bytes 589832 | tf_op jit(solution)/shard_map/ppermute | solution.py:20
  13.6 32.7 %collective-permute-start.4 = (bf16[128,768]{1,0:T(8,128)(2,1)S(1)}, bf16[128,768]{1,0:T(8,128)(2,1)S(1)}, u32[]{:S(2)}, u32[]{:S(2)}) collective-permute-start(bf16[128,768]{1,0:T(8,128)(2,1)S(1)} %get-tuple-element.19), channel_id=1, source_target_pairs={{0,1},{1,2},{2,3},{3,4},{4,5},{5,6},{6,7},{7,8},{8,9},{9,10},{10,1... | collective-permute-start | bytes 589832 | tf_op jit(solution)/shard_map/ppermute | solution.py:20
  13.9 45.2 %collective-permute-start.6 = (bf16[128,768]{1,0:T(8,128)(2,1)S(1)}, bf16[128,768]{1,0:T(8,128)(2,1)S(1)}, u32[]{:S(2)}, u32[]{:S(2)}) collective-permute-start(bf16[128,768]{1,0:T(8,128)(2,1)S(1)} %get-tuple-element.20), channel_id=1, source_target_pairs={{0,2},{1,3},{2,4},{3,5},{4,6},{5,7},{6,8},{7,9},{8,10},{9,11},{10,... | collective-permute-start | bytes 589832 | tf_op jit(solution)/shard_map/ppermute | solution.py:20
  14.6 0.9 %copy-start.1 = (bf16[1024,120]{0,1:T(8,128)(2,1)S(1)}, bf16[1024,120]{0,1:T(8,128)(2,1)}, u32[]{:S(2)}) copy-start(bf16[1024,120]{0,1:T(8,128)(2,1)} %param.9) | copy-start | bytes 737284
  15.5 0.7 copy-start.5
  16.2 2.4 %copy-start.9 = (bf16[2048,10,120]{0,2,1:T(8,128)(2,1)S(1)}, bf16[2048,10,120]{0,2,1:T(8,128)(2,1)}, u32[]{:S(2)}) copy-start(bf16[2048,10,120]{0,2,1:T(8,128)(2,1)} %param.8) | copy-start | bytes 14745604
  37.9 31.1 %collective-permute-start.1 = (f32[16,768]{1,0:T(8,128)S(1)}, f32[16,768]{1,0:T(8,128)S(1)}, u32[]{:S(2)}, u32[]{:S(2)}) collective-permute-start(f32[16,768]{1,0:T(8,128)S(1)} %answer.4), channel_id=1, source_target_pairs={{0,2},{1,3},{2,4},{3,5},{4,6},{5,7},{6,8},{7,9},{8,10},{9,11},{10,... | collective-permute-start | bytes 147464 | tf_op jit(solution)/shard_map/ppermute | solution.py:20
  45.8 25.3 %copy-start.3 = (s32[1024,4]{0,1:T(4,128)S(1)}, s32[1024,4]{0,1:T(4,128)}, u32[]{:S(2)}) copy-start(s32[1024,4]{0,1:T(4,128)} %param.11) | copy-start | bytes 49156
  45.8 25.3 %copy-start.6 = (f32[1024,4]{0,1:T(4,128)S(1)}, f32[1024,4]{0,1:T(4,128)}, u32[]{:S(2)}) copy-start(f32[1024,4]{0,1:T(4,128)} %param.10) | copy-start | bytes 49156
  45.8 30.1 %copy-start.10 = (s32[1024]{0:T(1024)S(1)}, s32[1024]{0:T(1024)}, u32[]{:S(2)}) copy-start(s32[1024]{0:T(1024)} %param.15) | copy-start | bytes 12292
  45.8 34.4 %copy-start.7 = (f32[1024]{0:T(1024)S(1)}, f32[1024]{0:T(1024)}, u32[]{:S(2)}) copy-start(f32[1024]{0:T(1024)} %param.13) | copy-start | bytes 12292
  45.8 34.4 %copy-start.8 = (f32[1024]{0:T(1024)S(1)}, f32[1024]{0:T(1024)}, u32[]{:S(2)}) copy-start(f32[1024]{0:T(1024)} %param.14) | copy-start | bytes 12292
  45.8 23.1 %collective-permute-start.3 = (f32[16,768]{1,0:T(8,128)S(1)}, f32[16,768]{1,0:T(8,128)S(1)}, u32[]{:S(2)}, u32[]{:S(2)}) collective-permute-start(f32[16,768]{1,0:T(8,128)S(1)} %answer.5), channel_id=1, source_target_pairs={{0,1},{1,2},{2,3},{3,4},{4,5},{5,6},{6,7},{7,8},{8,9},{9,10},{10,1... | collective-permute-start | bytes 147464 | tf_op jit(solution)/shard_map/ppermute | solution.py:20
  54.0 14.9 %collective-permute-start.5 = (f32[16,768]{1,0:T(8,128)S(1)}, f32[16,768]{1,0:T(8,128)S(1)}, u32[]{:S(2)}, u32[]{:S(2)}) collective-permute-start(f32[16,768]{1,0:T(8,128)S(1)} %answer.6), channel_id=1, source_target_pairs={{0,63},{1,0},{2,1},{3,2},{4,3},{5,4},{6,5},{7,6},{8,7},{9,8},{10,9... | collective-permute-start | bytes 147464 | tf_op jit(solution)/shard_map/ppermute | solution.py:20
  66.9 4.2 %collective-permute-start.7 = (f32[16,768]{1,0:T(8,128)S(1)}, f32[16,768]{1,0:T(8,128)S(1)}, u32[]{:S(2)}, u32[]{:S(2)}) collective-permute-start(f32[16,768]{1,0:T(8,128)S(1)} %answer.7), channel_id=1, source_target_pairs={{0,62},{1,63},{2,0},{3,1},{4,2},{5,3},{6,4},{7,5},{8,6},{9,7},{10,... | collective-permute-start | bytes 147464 | tf_op jit(solution)/shard_map/ppermute | solution.py:20
  72.6 4.3 %collective-permute-start.10 = (f32[16,1024]{1,0:T(8,128)S(1)}, f32[16,1024]{1,0:T(8,128)S(1)}, u32[]{:S(2)}, u32[]{:S(2)}) collective-permute-start(f32[16,1024]{1,0:T(8,128)S(1)} %combine.1.refs_0_), channel_id=1, source_target_pairs={{0,192},{64,0},{128,64},{192,128},{1,193},{65,1},{129,65},{193,129... | collective-permute-start | bytes 196616 | tf_op jit(solution)/shard_map/ppermute | solution.py:20
  73.2 5.8 %collective-permute-start.9 = (f32[16,1024]{1,0:T(8,128)S(1)}, f32[16,1024]{1,0:T(8,128)S(1)}, u32[]{:S(2)}, u32[]{:S(2)}) collective-permute-start(f32[16,1024]{1,0:T(8,128)S(1)} %combine.1.refs_0_), channel_id=1, source_target_pairs={{0,128},{64,192},{128,0},{192,64},{1,129},{65,193},{129,1},{193,65... | collective-permute-start | bytes 196616 | tf_op jit(solution)/shard_map/ppermute | solution.py:20
  75.9 4.3 %collective-permute-start.8 = (f32[16,1024]{1,0:T(8,128)S(1)}, f32[16,1024]{1,0:T(8,128)S(1)}, u32[]{:S(2)}, u32[]{:S(2)}) collective-permute-start(f32[16,1024]{1,0:T(8,128)S(1)} %combine.1.refs_0_), channel_id=1, source_target_pairs={{0,64},{64,128},{128,192},{192,0},{1,65},{65,129},{129,193},{193,1... | collective-permute-start | bytes 196616 | tf_op jit(solution)/shard_map/ppermute | solution.py:20
  80.8 6.8 %collective-permute-start.11 = (f32[80,64]{1,0:T(8,128)S(1)}, f32[80,64]{1,0:T(8,128)S(1)}, u32[]{:S(2)}, u32[]{:S(2)}) collective-permute-start(f32[80,64]{1,0:T(8,128)S(1)} %get-tuple-element.22), channel_id=1, source_target_pairs={{0,1},{1,2},{2,3},{3,4},{4,5},{5,6},{6,7},{7,8},{8,9},{9,10},{10,1... | collective-permute-start | bytes 61448 | tf_op jit(solution)/shard_map/ppermute | solution.py:20
  80.9 6.7 %collective-permute-start.12 = (f32[80,64]{1,0:T(8,128)S(1)}, f32[80,64]{1,0:T(8,128)S(1)}, u32[]{:S(2)}, u32[]{:S(2)}) collective-permute-start(f32[80,64]{1,0:T(8,128)S(1)} %get-tuple-element.23), channel_id=1, source_target_pairs={{0,63},{1,0},{2,1},{3,2},{4,3},{5,4},{6,5},{7,6},{8,7},{9,8},{10,9... | collective-permute-start | bytes 61448 | tf_op jit(solution)/shard_map/ppermute | solution.py:20
where the time goes:
time: 88.9 us; the launch traced here: 88.4 us
  Pallas kernels  47.5 us (53%)
  starting transfers between devices  25.6 us (29%)
  waiting for transfers between devices  8.03 us (9%)
  local copies, waits for them, and re-layouts  6.46 us (7%)
    pallas_call x4, Pallas kernels, on_device(): answer(turned, w)  31.3 us
    ppermute x13, starting transfers between devices, passed_along(): lax.ppermute(x, axis, [(i, (i + by) % devices) for i in range(devices)])  25.6 us
    pallas_call x1, Pallas kernels, on_device(): pl.pallas_call(own_kernel, out_shape=[jax.ShapeDtypeStruct((16 * row_stri...  11.4 us
    ppermute x13, waiting for transfers between devices, passed_along(): lax.ppermute(x, axis, [(i, (i + by) % devices) for i in range(devices)])  8.03 us
    unnamed x22, local copies, waits for them, and re-layouts  6.46 us
    pallas_call x1, Pallas kernels, on_device(): pl.pallas_call(ask_kernel, out_shape=[jax.ShapeDtypeStruct((neigh * obs /...  1.99 us
  transfers between devices with their start and end apart: 13, of which 5 were waited for; matrix products, arithmetic and copies ran while one was open for 0% of the time, Pallas kernels for 48%

commit v1 on v0

--- a/solution.py
+++ b/solution.py
@@ -12,6 +12,7 @@
 BF16 = jnp.bfloat16
 NT = (((1,), (1,)), ((), ()))
 VMEM = pl.BlockSpec(memory_space=pltpu.VMEM)
+ANY = pl.BlockSpec(memory_space=pltpu.HBM)
 SMEM = pl.BlockSpec(memory_space=pltpu.SMEM)
 
 
@@ -43,25 +44,37 @@
     return (32.0 * total[:tops] + total[tops:]).astype(jnp.int32)
 
 
-def slot_weights(inv_ref, table_ref, vw_ref, tile):
+def slot_weights(inv_ref, vw_ref, tile, table_ref=None):
     levels, obs = vw_ref.shape
     key = jnp.concatenate([inv_ref[2 * tile : 2 * tile + 1, :], inv_ref[2 * tile + 1 : 2 * tile + 2, :]], axis=1)
     ids = lax.broadcasted_iota(jnp.int32, (obs, TILE), 0)
     pick = jnp.where(ids == key, 1.0, 0.0).astype(BF16)
     w = jnp.dot(vw_ref[...], pick, preferred_element_type=F32)
-    cells = table_ref[0:1, tile * TILE : (tile + 1) * TILE]
-    sub = lax.broadcasted_iota(jnp.int32, (128 - levels, TILE), 0)
-    extra = jnp.where(sub == 0, (cells >> 3).astype(F32), jnp.where(sub == 1, (cells & 7).astype(F32), 0.0))
+    extra = jnp.zeros((128 - levels, TILE), F32)
+    if table_ref is not None:
+        cells = table_ref[0:1, tile * TILE : (tile + 1) * TILE]
+        sub = lax.broadcasted_iota(jnp.int32, (128 - levels, TILE), 0)
+        extra = jnp.where(sub == 0, (cells >> 3).astype(F32), jnp.where(sub == 1, (cells & 7).astype(F32), extra))
     return jnp.concatenate([w, extra], axis=0).astype(BF16)
 
 
-def ask_kernel(slot_ref, table_ref, vw_ref, inv_ref, *out_refs):
+def ask_kernel(slot_hbm, table_hbm, vw_hbm, inv_ref, vw_ref, *refs):
+    *out_refs, slot_ref, table_ref, sems = refs
+    copies = [
+        pltpu.make_async_copy(src, dst, sems.at[i])
+        for i, (src, dst) in enumerate(((slot_hbm, slot_ref), (vw_hbm, vw_ref), (table_hbm, table_ref)))
+    ]
+    for copy in copies:
+        copy.start()
     obs = vw_ref.shape[1]
+    copies[0].wait()
     inv_ref[...] = slot_owner(slot_ref)
+    copies[1].wait()
+    copies[2].wait()
     tile = obs // TILE
     for out in out_refs:
         for part in range(out.shape[1] // TILE):
-            out[:, part * TILE : (part + 1) * TILE] = slot_weights(inv_ref, table_ref, vw_ref, tile)
+            out[:, part * TILE : (part + 1) * TILE] = slot_weights(inv_ref, vw_ref, tile, table_ref)
             tile += 1
 
 
@@ -100,21 +113,26 @@
     return jnp.concatenate([out_a, out_b], axis=0)
 
 
-def own_kernel(state_ref, cell_ref, inv_ref, table_ref, vw_ref, turned_ref, eq_ref):
+def own_kernel(state_hbm, table_hbm, inv_ref, vw_ref, turned_ref, eq_ref, state_ref, cell_ref, sems, cell_sem):
     members, levels, cells = state_ref.shape
+    copies = [pltpu.make_async_copy(state_hbm.at[m], state_ref.at[m], sems.at[m]) for m in range(members)]
+    for copy in copies:
+        copy.start()
+    cell_copy = pltpu.make_async_copy(table_hbm.at[:, pl.ds(0, eq_ref.shape[1])], cell_ref, cell_sem)
+    cell_copy.start()
     S = row_stride(cells)
     r = lax.broadcasted_iota(jnp.int32, (TILE, TILE), 0)
     eye = jnp.where(r == lax.broadcasted_iota(jnp.int32, (TILE, TILE), 1), 1.0, 0.0).astype(BF16)
     pad = jnp.zeros((TILE, 128 - levels), F32)
     for m in range(members):
+        copies[m].wait()
         for part in range(cells // TILE):
             block = state_ref[m, :, part * TILE : (part + 1) * TILE]
             flat = lax.dot_general(eye, block, NT, preferred_element_type=F32)
             turned_ref[m * S + part * TILE : m * S + (part + 1) * TILE, :] = jnp.concatenate([flat, pad], axis=1)
-    keep = lax.broadcasted_iota(jnp.int32, (128, TILE), 0) < levels
+    cell_copy.wait()
     for tile in range(eq_ref.shape[1] // TILE):
-        w = slot_weights(inv_ref, table_ref, vw_ref, tile)
-        w = jnp.where(keep, w, jnp.zeros_like(w))
+        w = slot_weights(inv_ref, vw_ref, tile)
         eq_ref[:, tile * TILE : (tile + 1) * TILE] = answer_tile(
             lambda i: cell_ref[0, tile * TILE + i], w, turned_ref, cells
         )
@@ -239,30 +257,45 @@
     halo = 3 * obs // 4
     state_t = jnp.transpose(state, (1, 2, 0))
     vw_t, hw_t, slot_t = vertical_weight.T, horizontal_weight.T, obs_slot.T
-    params = pltpu.CompilerParams(vmem_limit_bytes=40 * 1024 * 1024)
-
-    inv, *asks = pl.pallas_call(
+    far = lambda x: pltpu.with_memory_space_constraint(x, pltpu.HBM)
+    params = pltpu.CompilerParams(vmem_limit_bytes=16 * 1024 * 1024)
+
+    inv, vw_near, *asks = pl.pallas_call(
         ask_kernel,
-        out_shape=[jax.ShapeDtypeStruct((neigh * obs // 128, 128), jnp.int32)]
+        out_shape=[
+            jax.ShapeDtypeStruct((neigh * obs // 128, 128), jnp.int32),
+            jax.ShapeDtypeStruct((levels, obs), BF16),
+        ]
         + [jax.ShapeDtypeStruct((128, halo), BF16)] * 4,
-        in_specs=[VMEM] * 3,
-        out_specs=[VMEM] * 5,
+        in_specs=[ANY] * 3,
+        out_specs=[VMEM] * 6,
+        scratch_shapes=[
+            pltpu.VMEM((neigh, obs), jnp.int32),
+            pltpu.VMEM((1, neigh * obs), jnp.int32),
+            pltpu.SemaphoreType.DMA((3,)),
+        ],
         compiler_params=params,
         name="ask",
-    )(slot_t, request_cell, vw_t)
+    )(far(slot_t), far(request_cell), far(vw_t))
     arrived = [passed_along(w, "cell", by) for w, by in zip(asks, HALO_MOVES)]
     turned, eq_own = pl.pallas_call(
         own_kernel,
         out_shape=[
-            jax.ShapeDtypeStruct((16 * row_stride(cells), 128), F32),
+            pltpu.VMEM((16 * row_stride(cells), 128), F32),
             jax.ShapeDtypeStruct((16, obs), F32),
         ],
-        in_specs=[VMEM, SMEM, VMEM, VMEM, VMEM],
+        in_specs=[ANY, ANY, VMEM, VMEM],
         out_specs=[VMEM] * 2,
+        scratch_shapes=[
+            pltpu.VMEM((mem_dev, levels, cells), BF16),
+            pltpu.SMEM((1, obs), jnp.int32),
+            pltpu.SemaphoreType.DMA((mem_dev,)),
+            pltpu.SemaphoreType.DMA,
+        ],
         compiler_params=params,
         cost_estimate=pl.CostEstimate(flops=8_000_000_000, bytes_accessed=10_000_000, transcendentals=0),
         name="own",
-    )(state_t, request_cell, inv, request_cell, vw_t)
+    )(far(state_t), far(request_cell), inv, vw_near)
     answer = pl.pallas_call(
         lambda *refs: halo_kernel(levels, cells, *refs),
         out_shape=jax.ShapeDtypeStruct((16, halo), F32),

time: 88.9 us -> 58.8 us (0.66)
  the two profiles are of different devices: /device:TPU:4 before, /device:TPU:6 now
where the time goes in v1:
time: 58.8 us; the launch traced here: 58.7 us
  starting transfers between devices  21.9 us (37%)
  Pallas kernels  21.4 us (36%)
  waiting for transfers between devices  14.6 us (25%)
  between operations  0.78 us (1%)
    ppermute x13, starting transfers between devices, passed_along(): lax.ppermute(x, axis, [(i, (i + by) % devices) for i in range(devices)])  21.9 us
    ppermute x13, waiting for transfers between devices, passed_along(): lax.ppermute(x, axis, [(i, (i + by) % devices) for i in range(devices)])  14.6 us
    pallas_call x4, Pallas kernels, on_device(): answer(turned, w)  8.06 us
    pallas_call x1, Pallas kernels, on_device(): pl.pallas_call(own_kernel, out_shape=[pltpu.VMEM((16 * row_stride(cells),...  7.73 us
    pallas_call x1, Pallas kernels, on_device(): pl.pallas_call(ask_kernel, out_shape=[jax.ShapeDtypeStruct((neigh * obs /...  2.74 us
    pallas_call x1, Pallas kernels, on_device(): pl.pallas_call(combine_kernel, out_shape=jax.ShapeDtypeStruct((16, obs),...  1.52 us
  transfers between devices with their start and end apart: 13, of which 6 were waited for; matrix products, arithmetic and copies ran while one was open for 0% of the time, Pallas kernels for 27%

profile of v1, /device:TPU:6, one launch (start us, length us, event | category | flops | bytes accessed | tf_op | source)
XLA Modules:
  0.0 58.7 jit_solution(14284140371453943691)
XLA Ops:
  0.6 2.7 %ask.1 = (s32[32,128]{1,0:T(8,128)S(1)}, bf16[120,1024]{1,0:T(8,128)(2,1)S(1)}, bf16[128,768]{1,0:T(8,128)(2,1)S(1)}, bf16[128,768]{1,0:T(8,128)(2,1)S(1)}, bf16...) custom-call(s32[4,1024]{1,0:T(4,128)} %bitcast.9, s32[1,4096]{1,0:T(1,128)} %table_hbm.3, bf16[120,1024]{1,0:T(8,128)(2,1)} %bitcast.15), custom_call_target="tpu_custom_call" | custom-call | tf_op jit(solution)/shard_map/ask/pallas_call | solution.py:263
  3.4 2.0 %collective-permute-start.6 = (bf16[128,768]{1,0:T(8,128)(2,1)S(1)}, bf16[128,768]{1,0:T(8,128)(2,1)S(1)}, u32[]{:S(2)}, u32[]{:S(2)}) collective-permute-start(bf16[128,768]{1,0:T(8,128)(2,1)S(1)} %get-tuple-element.22), channel_id=1, source_target_pairs={{0,2},{1,3},{2,4},{3,5},{4,6},{5,7},{6,8},{7,9},{8,10},{9,11},{10,... | collective-permute-start | bytes 589832 | tf_op jit(solution)/shard_map/ppermute | solution.py:21
  5.4 0.0 collective-permute-start.4
  5.4 6.0 %collective-permute-start.2 = (bf16[128,768]{1,0:T(8,128)(2,1)S(1)}, bf16[128,768]{1,0:T(8,128)(2,1)S(1)}, u32[]{:S(2)}, u32[]{:S(2)}) collective-permute-start(bf16[128,768]{1,0:T(8,128)(2,1)S(1)} %get-tuple-element.20), channel_id=1, source_target_pairs={{0,63},{1,0},{2,1},{3,2},{4,3},{5,4},{6,5},{7,6},{8,7},{9,8},{10,9... | collective-permute-start | bytes 589832 | tf_op jit(solution)/shard_map/ppermute | solution.py:21
  11.4 2.2 %collective-permute-start = (bf16[128,768]{1,0:T(8,128)(2,1)S(1)}, bf16[128,768]{1,0:T(8,128)(2,1)S(1)}, u32[]{:S(2)}, u32[]{:S(2)}) collective-permute-start(bf16[128,768]{1,0:T(8,128)(2,1)S(1)} %get-tuple-element.19), channel_id=1, source_target_pairs={{0,62},{1,63},{2,0},{3,1},{4,2},{5,3},{6,4},{7,5},{8,6},{9,7},{10,... | collective-permute-start | bytes 589832 | tf_op jit(solution)/shard_map/ppermute | solution.py:21
  13.6 7.7 %own.1 = (f32[32832,128]{1,0:T(8,128)S(1)}, f32[16,1024]{1,0:T(8,128)S(1)}) custom-call(bf16[10,120,2048]{2,1,0:T(8,128)(2,1)} %bitcast.16, s32[1,4096]{1,0:T(1,128)} %table_hbm.3, s32[32,128]{1,0:T(8,128)S(1)} %get-tuple-element.15.inv_ref, bf16[120,1024]{1,0:T(8,128)(2,1)S(1)} %get-tuple-element.16.vw_ref), custom_call_target="tpu_custom_call" | custom-call | flops 8000000000 | bytes 10000000 | tf_op jit(solution)/shard_map/own/pallas_call | solution.py:281
  21.3 0.0 collective-permute-done.6.refs_1_
  21.3 2.0 %answer.7 = f32[16,768]{1,0:T(8,128)S(1)} custom-call(f32[32832,128]{1,0:T(8,128)S(1)} %get-tuple-element.18.refs_0_, bf16[128,768]{1,0:T(8,128)(2,1)S(1)} %collective-permute-done.6.refs_1_), custom_call_target="tpu_custom_call" | custom-call | flops 2000000000 | bytes 1000000 | tf_op jit(solution)/shard_map/answer/pallas_call | solution.py:313
  23.4 2.0 %collective-permute-start.7 = (f32[16,768]{1,0:T(8,128)S(1)}, f32[16,768]{1,0:T(8,128)S(1)}, u32[]{:S(2)}, u32[]{:S(2)}) collective-permute-start(f32[16,768]{1,0:T(8,128)S(1)} %answer.7), channel_id=1, source_target_pairs={{0,62},{1,63},{2,0},{3,1},{4,2},{5,3},{6,4},{7,5},{8,6},{9,7},{10,... | collective-permute-start | bytes 147464 | tf_op jit(solution)/shard_map/ppermute | solution.py:21
  25.4 0.0 collective-permute-done.4.refs_1_
  25.4 2.0 %answer.6 = f32[16,768]{1,0:T(8,128)S(1)} custom-call(f32[32832,128]{1,0:T(8,128)S(1)} %get-tuple-element.18.refs_0_, bf16[128,768]{1,0:T(8,128)(2,1)S(1)} %collective-permute-done.4.refs_1_), custom_call_target="tpu_custom_call" | custom-call | flops 2000000000 | bytes 1000000 | tf_op jit(solution)/shard_map/answer/pallas_call | solution.py:313
  27.4 0.0 copy-start
  27.4 0.0 copy-start.1
  27.4 0.0 copy-start.4
  27.5 0.0 copy-start.2
  27.5 0.0 copy-start.3
  27.5 0.3 collective-permute-start.5
  27.8 0.0 collective-permute-done.2.refs_1_
  27.8 2.0 %answer.5 = f32[16,768]{1,0:T(8,128)S(1)} custom-call(f32[32832,128]{1,0:T(8,128)S(1)} %get-tuple-element.18.refs_0_, bf16[128,768]{1,0:T(8,128)(2,1)S(1)} %collective-permute-done.2.refs_1_), custom_call_target="tpu_custom_call" | custom-call | flops 2000000000 | bytes 1000000 | tf_op jit(solution)/shard_map/answer/pallas_call | solution.py:313
  29.8 0.6 collective-permute-start.3
  30.4 0.0 collective-permute-done.refs_1_
  30.4 2.0 %answer.4 = f32[16,768]{1,0:T(8,128)S(1)} custom-call(f32[32832,128]{1,0:T(8,128)S(1)} %get-tuple-element.18.refs_0_, bf16[128,768]{1,0:T(8,128)(2,1)S(1)} %collective-permute-done.refs_1_), custom_call_target="tpu_custom_call" | custom-call | flops 2000000000 | bytes 1000000 | tf_op jit(solution)/shard_map/answer/pallas_call | solution.py:313
  32.4 0.2 collective-permute-start.1
  32.6 0.0 collective-permute-done.7.refs_4_
  32.6 0.0 collective-permute-done.5.refs_3_
  32.6 4.1 %collective-permute-done.3.refs_2_ = f32[16,768]{1,0:T(8,128)S(1)} collective-permute-done((f32[16,768]{1,0:T(8,128)S(1)}, f32[16,768]{1,0:T(8,128)S(1)}, u32[]{:S(2)}, u32[]{:S(2)}) %collective-permute-start.3) | collective-permute-done | bytes 49184 | tf_op jit(solution)/shard_map/ppermute | solution.py:21
  36.7 3.2 %collective-permute-done.1.refs_1_ = f32[16,768]{1,0:T(8,128)S(1)} collective-permute-done((f32[16,768]{1,0:T(8,128)S(1)}, f32[16,768]{1,0:T(8,128)S(1)}, u32[]{:S(2)}, u32[]{:S(2)}) %collective-permute-start.1) | collective-permute-done | bytes 49184 | tf_op jit(solution)/shard_map/ppermute | solution.py:21
  39.9 0.0 copy-done
  39.9 0.0 copy-done.1
  39.9 1.5 %combine.1.refs_0_ = f32[16,1024]{1,0:T(8,128)S(1)} custom-call(s32[4,1024]{1,0:T(4,128)S(1)} %bitcast.10, f32[4,1024]{1,0:T(4,128)S(1)} %bitcast.12, f32[16,1024]{1,0:T(8,128)S(1)} %get-tuple-element.17.refs_0_, f32[16,768]{1,0:T(8,128)S(1)} %collective-permute-done.1.refs_1_, f32[16,768]{1,0:T(8,128)S(1)} %collective-permute-done.3.refs_2_, ...), custom_call_target="tpu_custom_call" | custom-call | tf_op jit(solution)/shard_map/combine/pallas_call | solution.py:314
  41.4 0.9 %collective-permute-start.10 = (f32[16,1024]{1,0:T(8,128)S(1)}, f32[16,1024]{1,0:T(8,128)S(1)}, u32[]{:S(2)}, u32[]{:S(2)}) collective-permute-start(f32[16,1024]{1,0:T(8,128)S(1)} %combine.1.refs_0_), channel_id=1, source_target_pairs={{0,192},{64,0},{128,64},{192,128},{1,193},{65,1},{129,65},{193,129... | collective-permute-start | bytes 196616 | tf_op jit(solution)/shard_map/ppermute | solution.py:21
  42.3 2.4 %collective-permute-start.8 = (f32[16,1024]{1,0:T(8,128)S(1)}, f32[16,1024]{1,0:T(8,128)S(1)}, u32[]{:S(2)}, u32[]{:S(2)}) collective-permute-start(f32[16,1024]{1,0:T(8,128)S(1)} %combine.1.refs_0_), channel_id=1, source_target_pairs={{0,64},{64,128},{128,192},{192,0},{1,65},{65,129},{129,193},{193,1... | collective-permute-start | bytes 196616 | tf_op jit(solution)/shard_map/ppermute | solution.py:21
  44.7 0.2 collective-permute-start.9
  44.9 0.0 copy-done.4
  44.9 2.0 %collective-permute-done.10.refs_3_ = f32[16,1024]{1,0:T(8,128)S(1)} collective-permute-done((f32[16,1024]{1,0:T(8,128)S(1)}, f32[16,1024]{1,0:T(8,128)S(1)}, u32[]{:S(2)}, u32[]{:S(2)}) %collective-permute-start.10) | collective-permute-done | bytes 65568 | tf_op jit(solution)/shard_map/ppermute | solution.py:21
  47.0 0.3 collective-permute-done.8.refs_1_
  47.2 3.3 %collective-permute-done.9.refs_2_ = f32[16,1024]{1,0:T(8,128)S(1)} collective-permute-done((f32[16,1024]{1,0:T(8,128)S(1)}, f32[16,1024]{1,0:T(8,128)S(1)}, u32[]{:S(2)}, u32[]{:S(2)}) %collective-permute-start.9) | collective-permute-done | bytes 65568 | tf_op jit(solution)/shard_map/ppermute | solution.py:21
  50.5 0.0 copy-done.2
  50.5 0.0 copy-done.3
  50.5 0.6 cov.1
  51.1 0.1 collective-permute-start.11
  51.2 5.1 %collective-permute-start.12 = (f32[80,64]{1,0:T(8,128)S(1)}, f32[80,64]{1,0:T(8,128)S(1)}, u32[]{:S(2)}, u32[]{:S(2)}) collective-permute-start(f32[80,64]{1,0:T(8,128)S(1)} %get-tuple-element.25), channel_id=1, source_target_pairs={{0,63},{1,0},{2,1},{3,2},{4,3},{5,4},{6,5},{7,6},{8,7},{9,8},{10,9... | collective-permute-start | bytes 61448 | tf_op jit(solution)/shard_map/ppermute | solution.py:21
  56.2 1.7 %collective-permute-done.11.a_ref = f32[80,64]{1,0:T(8,128)S(1)} collective-permute-done((f32[80,64]{1,0:T(8,128)S(1)}, f32[80,64]{1,0:T(8,128)S(1)}, u32[]{:S(2)}, u32[]{:S(2)}) %collective-permute-start.11) | collective-permute-done | bytes 20512 | tf_op jit(solution)/shard_map/ppermute | solution.py:21
  57.9 0.0 collective-permute-done.12.b_ref
  57.9 0.8 %final.1 = (f32[10,8,40]{2,1,0:T(8,128)}, f32[8,10]{1,0:T(8,128)}) custom-call(s32[1]{0:T(128)} %bitcast.mem_ref, f32[80,64]{1,0:T(8,128)S(1)} %get-tuple-element.23.mid_ref, f32[80,64]{1,0:T(8,128)S(1)} %collective-permute-done.11.a_ref, f32[80,64]{1,0:T(8,128)S(1)} %collective-permute-done.12.b_ref), custom_call_target="tpu_custom_call" | custom-call | tf_op jit(solution)/shard_map/final/pallas_call | solution.py:335
  (1 shorter events, 0.0 us)
Async XLA Ops:
  3.4 18.0 %collective-permute-start.6 = (bf16[128,768]{1,0:T(8,128)(2,1)S(1)}, bf16[128,768]{1,0:T(8,128)(2,1)S(1)}, u32[]{:S(2)}, u32[]{:S(2)}) collective-permute-start(bf16[128,768]{1,0:T(8,128)(2,1)S(1)} %get-tuple-element.22), channel_id=1, source_target_pairs={{0,2},{1,3},{2,4},{3,5},{4,6},{5,7},{6,8},{7,9},{8,10},{9,11},{10,... | collective-permute-start | bytes 589832 | tf_op jit(solution)/shard_map/ppermute | solution.py:21
  5.4 20.0 %collective-permute-start.4 = (bf16[128,768]{1,0:T(8,128)(2,1)S(1)}, bf16[128,768]{1,0:T(8,128)(2,1)S(1)}, u32[]{:S(2)}, u32[]{:S(2)}) collective-permute-start(bf16[128,768]{1,0:T(8,128)(2,1)S(1)} %get-tuple-element.21), channel_id=1, source_target_pairs={{0,1},{1,2},{2,3},{3,4},{4,5},{5,6},{6,7},{7,8},{8,9},{9,10},{10,1... | collective-permute-start | bytes 589832 | tf_op jit(solution)/shard_map/ppermute | solution.py:21
  5.4 22.4 %collective-permute-start.2 = (bf16[128,768]{1,0:T(8,128)(2,1)S(1)}, bf16[128,768]{1,0:T(8,128)(2,1)S(1)}, u32[]{:S(2)}, u32[]{:S(2)}) collective-permute-start(bf16[128,768]{1,0:T(8,128)(2,1)S(1)} %get-tuple-element.20), channel_id=1, source_target_pairs={{0,63},{1,0},{2,1},{3,2},{4,3},{5,4},{6,5},{7,6},{8,7},{9,8},{10,9... | collective-permute-start | bytes 589832 | tf_op jit(solution)/shard_map/ppermute | solution.py:21
  11.4 19.0 %collective-permute-start = (bf16[128,768]{1,0:T(8,128)(2,1)S(1)}, bf16[128,768]{1,0:T(8,128)(2,1)S(1)}, u32[]{:S(2)}, u32[]{:S(2)}) collective-permute-start(bf16[128,768]{1,0:T(8,128)(2,1)S(1)} %get-tuple-element.19), channel_id=1, source_target_pairs={{0,62},{1,63},{2,0},{3,1},{4,2},{5,3},{6,4},{7,5},{8,6},{9,7},{10,... | collective-permute-start | bytes 589832 | tf_op jit(solution)/shard_map/ppermute | solution.py:21
  23.4 9.2 %collective-permute-start.7 = (f32[16,768]{1,0:T(8,128)S(1)}, f32[16,768]{1,0:T(8,128)S(1)}, u32[]{:S(2)}, u32[]{:S(2)}) collective-permute-start(f32[16,768]{1,0:T(8,128)S(1)} %answer.7), channel_id=1, source_target_pairs={{0,62},{1,63},{2,0},{3,1},{4,2},{5,3},{6,4},{7,5},{8,6},{9,7},{10,... | collective-permute-start | bytes 147464 | tf_op jit(solution)/shard_map/ppermute | solution.py:21
  27.4 12.5 %copy-start = (s32[1024,4]{0,1:T(4,128)S(1)}, s32[1024,4]{0,1:T(4,128)}, u32[]{:S(2)}) copy-start(s32[1024,4]{0,1:T(4,128)} %param.11) | copy-start | bytes 49156
  27.4 12.4 %copy-start.1 = (f32[1024,4]{0,1:T(4,128)S(1)}, f32[1024,4]{0,1:T(4,128)}, u32[]{:S(2)}) copy-start(f32[1024,4]{0,1:T(4,128)} %param.10) | copy-start | bytes 49156
  27.4 17.5 %copy-start.4 = (s32[1024]{0:T(1024)S(1)}, s32[1024]{0:T(1024)}, u32[]{:S(2)}) copy-start(s32[1024]{0:T(1024)} %param.15) | copy-start | bytes 12292
  27.5 23.0 %copy-start.2 = (f32[1024]{0:T(1024)S(1)}, f32[1024]{0:T(1024)}, u32[]{:S(2)}) copy-start(f32[1024]{0:T(1024)} %param.13) | copy-start | bytes 12292
  27.5 23.0 %copy-start.3 = (f32[1024]{0:T(1024)S(1)}, f32[1024]{0:T(1024)}, u32[]{:S(2)}) copy-start(f32[1024]{0:T(1024)} %param.14) | copy-start | bytes 12292
  27.5 5.1 %collective-permute-start.5 = (f32[16,768]{1,0:T(8,128)S(1)}, f32[16,768]{1,0:T(8,128)S(1)}, u32[]{:S(2)}, u32[]{:S(2)}) collective-permute-start(f32[16,768]{1,0:T(8,128)S(1)} %answer.6), channel_id=1, source_target_pairs={{0,63},{1,0},{2,1},{3,2},{4,3},{5,4},{6,5},{7,6},{8,7},{9,8},{10,9... | collective-permute-start | bytes 147464 | tf_op jit(solution)/shard_map/ppermute | solution.py:21
  29.8 6.9 %collective-permute-start.3 = (f32[16,768]{1,0:T(8,128)S(1)}, f32[16,768]{1,0:T(8,128)S(1)}, u32[]{:S(2)}, u32[]{:S(2)}) collective-permute-start(f32[16,768]{1,0:T(8,128)S(1)} %answer.5), channel_id=1, source_target_pairs={{0,1},{1,2},{2,3},{3,4},{4,5},{5,6},{6,7},{7,8},{8,9},{9,10},{10,1... | collective-permute-start | bytes 147464 | tf_op jit(solution)/shard_map/ppermute | solution.py:21
  32.4 7.5 %collective-permute-start.1 = (f32[16,768]{1,0:T(8,128)S(1)}, f32[16,768]{1,0:T(8,128)S(1)}, u32[]{:S(2)}, u32[]{:S(2)}) collective-permute-start(f32[16,768]{1,0:T(8,128)S(1)} %answer.4), channel_id=1, source_target_pairs={{0,2},{1,3},{2,4},{3,5},{4,6},{5,7},{6,8},{7,9},{8,10},{9,11},{10,... | collective-permute-start | bytes 147464 | tf_op jit(solution)/shard_map/ppermute | solution.py:21
  41.4 5.6 %collective-permute-start.10 = (f32[16,1024]{1,0:T(8,128)S(1)}, f32[16,1024]{1,0:T(8,128)S(1)}, u32[]{:S(2)}, u32[]{:S(2)}) collective-permute-start(f32[16,1024]{1,0:T(8,128)S(1)} %combine.1.refs_0_), channel_id=1, source_target_pairs={{0,192},{64,0},{128,64},{192,128},{1,193},{65,1},{129,65},{193,129... | collective-permute-start | bytes 196616 | tf_op jit(solution)/shard_map/ppermute | solution.py:21
  42.3 4.9 %collective-permute-start.8 = (f32[16,1024]{1,0:T(8,128)S(1)}, f32[16,1024]{1,0:T(8,128)S(1)}, u32[]{:S(2)}, u32[]{:S(2)}) collective-permute-start(f32[16,1024]{1,0:T(8,128)S(1)} %combine.1.refs_0_), channel_id=1, source_target_pairs={{0,64},{64,128},{128,192},{192,0},{1,65},{65,129},{129,193},{193,1... | collective-permute-start | bytes 196616 | tf_op jit(solution)/shard_map/ppermute | solution.py:21
  44.7 5.8 %collective-permute-start.9 = (f32[16,1024]{1,0:T(8,128)S(1)}, f32[16,1024]{1,0:T(8,128)S(1)}, u32[]{:S(2)}, u32[]{:S(2)}) collective-permute-start(f32[16,1024]{1,0:T(8,128)S(1)} %combine.1.refs_0_), channel_id=1, source_target_pairs={{0,128},{64,192},{128,0},{192,64},{1,129},{65,193},{129,1},{193,65... | collective-permute-start | bytes 196616 | tf_op jit(solution)/shard_map/ppermute | solution.py:21
  51.1 6.8 %collective-permute-start.11 = (f32[80,64]{1,0:T(8,128)S(1)}, f32[80,64]{1,0:T(8,128)S(1)}, u32[]{:S(2)}, u32[]{:S(2)}) collective-permute-start(f32[80,64]{1,0:T(8,128)S(1)} %get-tuple-element.24), channel_id=1, source_target_pairs={{0,1},{1,2},{2,3},{3,4},{4,5},{5,6},{6,7},{7,8},{8,9},{9,10},{10,1... | collective-permute-start | bytes 61448 | tf_op jit(solution)/shard_map/ppermute | solution.py:21
  51.2 6.7 %collective-permute-start.12 = (f32[80,64]{1,0:T(8,128)S(1)}, f32[80,64]{1,0:T(8,128)S(1)}, u32[]{:S(2)}, u32[]{:S(2)}) collective-permute-start(f32[80,64]{1,0:T(8,128)S(1)} %get-tuple-element.25), channel_id=1, source_target_pairs={{0,63},{1,0},{2,1},{3,2},{4,3},{5,4},{6,5},{7,6},{8,7},{9,8},{10,9... | collective-permute-start | bytes 61448 | tf_op jit(solution)/shard_map/ppermute | solution.py:21

commit v2 on v0

v2 whole, which is shorter than its diff:
```python
import jax
import jax.numpy as jnp
from jax import lax
from jax.experimental import pallas as pl
from jax.experimental.pallas import tpu as pltpu
from jax.sharding import PartitionSpec as P

REG_DEV = 8
HALO_MOVES = (-2, -1, 1, 2)
TILE = 256
F32 = jnp.float32
BF16 = jnp.bfloat16
NT = (((1,), (1,)), ((), ()))
VMEM = pl.BlockSpec(memory_space=pltpu.VMEM)
ANY = pl.BlockSpec(memory_space=pltpu.HBM)
SMEM = pl.BlockSpec(memory_space=pltpu.SMEM)


def passed_along(x, axis, by):
    devices = lax.axis_size(axis)
    return lax.ppermute(x, axis, [(i, (i + by) % devices) for i in range(devices)])


def row_stride(cells):
    return cells + 4


def member_row(cells, m):
    return m * row_stride(cells) + (m >= 8)


def slot_owner(slot_ref):
    neigh, obs = slot_ref.shape
    tops = neigh * obs // 128
    o = lax.broadcasted_iota(jnp.int32, (1, obs), 1)
    upper, lower = (o >> 5).astype(F32), (o & 31).astype(F32)
    row_top = lax.broadcasted_iota(jnp.int32, (tops, obs), 0)
    row_low = lax.broadcasted_iota(jnp.int32, (128, obs), 0)
    total = jnp.zeros((2 * tops, 128), F32)
    for k in range(neigh):
        s = slot_ref[k : k + 1, :]
        hit = row_top == (s >> 7)
        lhs = jnp.concatenate(
            [jnp.where(hit, upper, 0.0), jnp.where(hit, lower, 0.0)], axis=0
        ).astype(BF16)
        rhs = jnp.where(row_low == (s & 127), 1.0, 0.0).astype(BF16)
        total += lax.dot_general(lhs, rhs, NT, preferred_element_type=F32)
    return (32.0 * total[:tops] + total[tops:]).astype(jnp.int32)


def slot_weights(inv_ref, vw_ref, tile, table_ref=None):
    levels, obs = vw_ref.shape
    key = jnp.concatenate([inv_ref[2 * tile : 2 * tile + 1, :], inv_ref[2 * tile + 1 : 2 * tile + 2, :]], axis=1)
    ids = lax.broadcasted_iota(jnp.int32, (obs, TILE), 0)
    pick = jnp.where(ids == key, 1.0, 0.0).astype(BF16)
    w = jnp.dot(vw_ref[...], pick, preferred_element_type=F32)
    extra = jnp.zeros((128 - levels, TILE), F32)
    if table_ref is not None:
        cells = table_ref[0:1, tile * TILE : (tile + 1) * TILE]
        sub = lax.broadcasted_iota(jnp.int32, (128 - levels, TILE), 0)
        extra = jnp.where(sub == 0, (cells >> 3).astype(F32), jnp.where(sub == 1, (cells & 7).astype(F32), extra))
    return jnp.concatenate([w, extra], axis=0).astype(BF16)


def ask_far_kernel(slot_hbm, table_hbm, vw_hbm, state_hbm, inv_ref, vw_ref, table_ref, state_ref, *refs):
    *out_refs, slot_ref, sems = refs
    members, levels, cells = state_hbm.shape
    pairs = (
        (slot_hbm, slot_ref),
        (vw_hbm, vw_ref),
        (table_hbm, table_ref),
        (state_hbm, state_ref.at[:, pl.ds(0, levels), :]),
    )
    copies = [pltpu.make_async_copy(src, dst, sems.at[i]) for i, (src, dst) in enumerate(pairs)]
    for copy in copies:
        copy.start()
    copies[0].wait()
    inv_ref[...] = slot_owner(slot_ref)
    copies[1].wait()
    copies[2].wait()
    halo_weights(inv_ref, vw_ref, table_ref, out_refs, (0, 3))
    copies[3].wait()
    for m in range(members):
        state_ref[m, levels:, :] = jnp.zeros((state_ref.shape[1] - levels, cells), BF16)


def ask_near_kernel(inv_ref, vw_ref, table_ref, own_ref, *out_refs):
    halo_weights(inv_ref, vw_ref, table_ref, out_refs, (1, 2))
    for tile in range(own_ref.shape[1] // TILE):
        own_ref[:, tile * TILE : (tile + 1) * TILE] = slot_weights(inv_ref, vw_ref, tile)


def halo_weights(inv_ref, vw_ref, table_ref, out_refs, numbers):
    obs = vw_ref.shape[1]
    for out, number in zip(out_refs, numbers):
        count = out.shape[1] // TILE
        for part in range(count):
            tile = obs // TILE + number * count + part
            out[:, part * TILE : (part + 1) * TILE] = slot_weights(inv_ref, vw_ref, tile, table_ref)


def answer_tile(cell_of, w, turned_ref, cells_dim):
    S, rest = row_stride(cells_dim), member_row(cells_dim, 8)
    half = TILE // 2
    lane = lax.broadcasted_iota(jnp.int32, (8, TILE), 1) & (half - 1)
    wide = lax.broadcasted_iota(jnp.int32, (128, TILE), 1)
    zero = jnp.zeros_like(w)
    rhs = jnp.concatenate([jnp.where(wide < half, w, zero), jnp.where(wide < half, zero, w)], axis=0)
    first, second = [], []
    for h in range(2):
        a_rows, b_rows = [], []
        for q in range(half // 4):
            for j in range(4):
                c = cell_of(h * half + 4 * q + j)
                a_rows.append(turned_ref[pl.ds(c, 8, stride=S), :])
                b_rows.append(turned_ref[pl.ds(c + rest, 2, stride=S), :])
        first.append(jnp.concatenate(a_rows, axis=0).astype(BF16))
        second.append(jnp.concatenate(b_rows, axis=0).astype(BF16))
    lhs_a = jnp.concatenate(first, axis=1)
    lhs_b = jnp.concatenate(second, axis=1)
    d_a = jnp.dot(lhs_a, rhs, preferred_element_type=F32)
    d_b = jnp.dot(lhs_b, rhs, preferred_element_type=F32)
    out_a = jnp.zeros((8, TILE), F32)
    for r in range(half):
        out_a = jnp.where(lane == r, d_a[8 * r : 8 * r + 8, :], out_a)
    out_b = jnp.zeros((8, TILE), F32)
    near = lane - (lax.broadcasted_iota(jnp.int32, (8, TILE), 0) >> 1)
    for q in range(half // 4):
        out_b = jnp.where(near == 4 * q, d_b[8 * q : 8 * q + 8, :], out_b)
    return jnp.concatenate([out_a, out_b], axis=0)


def own_kernel(state_ref, table_hbm, w_ref, turned_ref, eq_ref, cell_ref, cell_sem):
    members, levels, cells = state_ref.shape
    copy = pltpu.make_async_copy(table_hbm.at[:, pl.ds(0, eq_ref.shape[1])], cell_ref, cell_sem)
    copy.start()
    r = lax.broadcasted_iota(jnp.int32, (TILE, TILE), 0)
    eye = jnp.where(r == lax.broadcasted_iota(jnp.int32, (TILE, TILE), 1), 1.0, 0.0).astype(BF16)
    for m in range(0, members, 2):
        for part in range(cells // TILE):
            at = slice(part * TILE, (part + 1) * TILE)
            block = jnp.concatenate([state_ref[m, :, at], state_ref[m + 1, :, at]], axis=0)
            flat = lax.dot_general(eye, block, NT, preferred_element_type=F32)
            for i in range(2):
                low = member_row(cells, m + i) + part * TILE
                turned_ref[low : low + TILE, :] = flat[:, i * 128 : (i + 1) * 128]
    copy.wait()
    for tile in range(eq_ref.shape[1] // TILE):
        at = slice(tile * TILE, (tile + 1) * TILE)
        eq_ref[:, at] = answer_tile(lambda i: cell_ref[0, tile * TILE + i], w_ref[:, at], turned_ref, cells)


def answer_kernel(levels, cells, turned_ref, *refs):
    count = len(refs) // 4
    w_refs, eq_refs = refs[:count], refs[count : 2 * count]
    words, scalars, sems = refs[2 * count : 3 * count], refs[3 * count : 4 * count], refs[-1]
    copies = []
    for i in range(count):
        tail = w_refs[i][112:128, :].astype(F32)
        row = levels - 112
        words[i][...] = (8.0 * tail[row : row + 1, :] + tail[row + 1 : row + 2, :]).astype(jnp.int32)
        copies.append(pltpu.make_async_copy(words[i], scalars[i], sems.at[i]))
        copies[-1].start()
    keep = lax.broadcasted_iota(jnp.int32, (128, TILE), 0) < levels
    for copy in copies:
        copy.wait()
    for i in range(count):
        for tile in range(eq_refs[i].shape[1] // TILE):
            at = slice(tile * TILE, (tile + 1) * TILE)
            w = w_refs[i][:, at]
            w = jnp.where(keep, w, jnp.zeros_like(w))
            eq_refs[i][:, at] = answer_tile(lambda j: scalars[i][0, tile * TILE + j], w, turned_ref, cells)


def combine_kernel(firsts, slot_ref, hw_ref, *refs):
    *eq_refs, out_ref = refs
    before = eq_refs.pop(0) if len(eq_refs) > len(firsts) else None
    neigh, obs = slot_ref.shape
    sub = lax.broadcasted_iota(jnp.int32, (8, 128), 0)
    tops, pairs = {}, {}
    for first, ref in zip(firsts, eq_refs):
        for part in range(ref.shape[1] // 128):
            tops[first + part] = ref[0:8, part * 128 : (part + 1) * 128]
            x = ref[8:16, part * 128 : (part + 1) * 128]
            x = x + pltpu.roll(x, 4, 0)
            pairs[first + part] = x + pltpu.roll(x, 2, 0)
    quads = {}
    for q in sorted({i // 4 for i in pairs}):
        x = jnp.zeros((8, 128), F32)
        for j in range(4):
            if 4 * q + j in pairs:
                x = jnp.where(sub >> 1 == j, pairs[4 * q + j], x)
        quads[q] = x
    last = None
    for block in range(obs // 128):
        at = slice(block * 128, (block + 1) * 128)
        a_sum = jnp.zeros((8, 128), F32)
        b_sum = jnp.zeros((8, 128), F32)
        for k in range(neigh):
            s = jnp.broadcast_to(slot_ref[k : k + 1, at], (8, 128))
            low, top = s & 127, s >> 7
            a = jnp.zeros((8, 128), F32)
            for i, x in tops.items():
                a = jnp.where(top == i, jnp.take_along_axis(x, low, axis=1, mode="promise_in_bounds"), a)
            b = jnp.zeros((8, 128), F32)
            top4 = top >> 2
            for i, x in quads.items():
                b = jnp.where(top4 == i, jnp.take_along_axis(x, low, axis=1, mode="promise_in_bounds"), b)
            b = jnp.where((top & 3) == (sub >> 1), b, 0.0)
            h = hw_ref[k : k + 1, at]
            a_sum += a * h
            b_sum += b * h
        b_sum = b_sum + pltpu.roll(b_sum, 4, 0)
        b_sum = b_sum + pltpu.roll(b_sum, 2, 0)
        if before is not None:
            a_sum += before[:, at]
        out_ref[:, at] = a_sum
        last = b_sum if block % 4 == 0 else jnp.where(sub >> 1 >= block % 4, b_sum, last)
        if block % 4 == 3:
            low = obs + block // 4 * 128
            if before is not None:
                last += before[:, low : low + 128]
            out_ref[:, low : low + 128] = last


def unpacked(ref, obs):
    sub = lax.broadcasted_iota(jnp.int32, (8, 128), 0)
    rest = []
    for block in range(obs // 128):
        low = obs + block // 4 * 128
        x = ref[:, low : low + 128]
        if block % 4:
            x = pltpu.roll(x, 8 - 2 * (block % 4), 0)
        rest.append(jnp.where(sub < 2, x, 0.0))
    return jnp.concatenate([ref[:, :obs], jnp.concatenate(rest, axis=1)], axis=0)


def split(x):
    top = x.astype(BF16)
    return top, (x - top.astype(F32)).astype(BF16)


def cov_kernel(members, own_ref, r1_ref, r2_ref, r3_ref, value_ref, error_ref, region_ref, mid_ref, prev_ref, next_ref):
    mem_dev = members // 4
    obs = region_ref.shape[1]
    blocks = [unpacked(ref, obs) for ref in (own_ref, r1_ref, r2_ref, r3_ref)]
    total = blocks[0] + blocks[1] + blocks[2] + blocks[3]
    mean = jnp.sum(total, axis=0, keepdims=True) * (1.0 / members)
    err = error_ref[...]
    inverse = 1.0 / (err * err)
    innov = (value_ref[...] - mean) * inverse
    row = lax.broadcasted_iota(jnp.int32, (16, obs), 0)
    spread = [jnp.where(row < mem_dev, x - mean, 0.0) for x in blocks]
    right = [x * inverse for x in spread]
    right[0] = jnp.where(row == mem_dev, innov, right[0])
    r_top, r_low = split(jnp.concatenate(right, axis=0))
    regions = lax.axis_size("cell") * REG_DEV
    rel = region_ref[...] - (lax.axis_index("cell") - 1) * REG_DEV
    rel = jnp.where(rel < 0, rel + regions, rel)
    rel = jnp.where(rel >= regions, rel - regions, rel)
    region = lax.broadcasted_iota(jnp.int32, (REG_DEV, obs), 0)
    own = spread[0]
    own_low = own - own.astype(BF16).astype(F32)
    for g, out_ref in ((0, prev_ref), (2, next_ref), (1, mid_ref)):
        mask = rel == region + g * REG_DEV
        l_top = jnp.concatenate([jnp.where(mask, own[m : m + 1, :], 0.0) for m in range(mem_dev)], axis=0).astype(BF16)
        l_low = jnp.concatenate([jnp.where(mask, own_low[m : m + 1, :], 0.0) for m in range(mem_dev)], axis=0).astype(BF16)
        d = lax.dot_general(l_top, r_top, NT, preferred_element_type=F32)
        d += lax.dot_general(l_top, r_low, NT, preferred_element_type=F32)
        d += lax.dot_general(l_low, r_top, NT, preferred_element_type=F32)
        out_ref[...] = d


def final_kernel(mid_ref, a_ref, b_ref, cov_ref, proj_ref):
    mem_dev, regions, members = cov_ref.shape
    d = mid_ref[...] + a_ref[...] + b_ref[...]
    width = d.shape[1]
    i = lax.broadcasted_iota(jnp.int32, (width, members), 0)
    j = lax.broadcasted_iota(jnp.int32, (width, members), 1)
    block = (lax.axis_index("mem") + 4 - (i >> 4)) & 3
    place = jnp.where(((i & 15) < mem_dev) & (block * mem_dev + (i & 15) == j), 1.0, 0.0)
    cov = jnp.dot(d, place, precision=lax.Precision.HIGHEST, preferred_element_type=F32)
    lane = lax.broadcasted_iota(jnp.int32, (regions, mem_dev), 1)
    proj = jnp.zeros((regions, mem_dev), F32)
    for m in range(mem_dev):
        cov_ref[m] = cov[m * regions : (m + 1) * regions, :]
        proj = jnp.where(lane == m, d[m * regions : (m + 1) * regions, mem_dev : mem_dev + 1], proj)
    proj_ref[...] = proj


def on_device(state, vertical_weight, horizontal_weight, obs_slot, request_cell, obs_value, obs_error, obs_region):
    cells, mem_dev, levels = state.shape
    members = mem_dev * lax.axis_size("mem")
    obs, neigh = obs_slot.shape
    halo = 3 * obs // 4
    state_t = jnp.transpose(state, (1, 2, 0))
    vw_t, hw_t, slot_t = vertical_weight.T, horizontal_weight.T, obs_slot.T
    far = lambda x: pltpu.with_memory_space_constraint(x, pltpu.HBM)
    params = pltpu.CompilerParams(vmem_limit_bytes=16 * 1024 * 1024)

    w_shape = jax.ShapeDtypeStruct((128, halo), BF16)
    inv, vw_near, table, state_near, ask_m2, ask_p2 = pl.pallas_call(
        ask_far_kernel,
        out_shape=[
            pltpu.VMEM((neigh * obs // 128, 128), jnp.int32),
            pltpu.VMEM((levels, obs), BF16),
            pltpu.VMEM((1, neigh * obs), jnp.int32),
            pltpu.VMEM((mem_dev, 128, cells), BF16),
            w_shape,
            w_shape,
        ],
        in_specs=[ANY] * 4,
        out_specs=[VMEM] * 6,
        scratch_shapes=[pltpu.VMEM((neigh, obs), jnp.int32), pltpu.SemaphoreType.DMA((4,))],
        compiler_params=params,
        cost_estimate=pl.CostEstimate(flops=2_000_000_000, bytes_accessed=6_000_000, transcendentals=0),
        name="ask_far",
    )(far(slot_t), far(request_cell), far(vw_t), far(state_t))
    w_m2, w_p2 = passed_along(ask_m2, "cell", -2), passed_along(ask_p2, "cell", 2)
    w_own, ask_m1, ask_p1 = pl.pallas_call(
        ask_near_kernel,
        out_shape=[pltpu.VMEM((128, obs), BF16), w_shape, w_shape],
        in_specs=[VMEM] * 3,
        out_specs=[VMEM] * 3,
        compiler_params=params,
        cost_estimate=pl.CostEstimate(flops=2_000_000_000, bytes_accessed=1_000_000, transcendentals=0),
        name="ask_near",
    )(inv, vw_near, table)
    w_m1, w_p1 = passed_along(ask_m1, "cell", -1), passed_along(ask_p1, "cell", 1)
    turned, eq_own = pl.pallas_call(
        own_kernel,
        out_shape=[
            pltpu.VMEM((mem_dev * row_stride(cells), 128), F32),
            pltpu.VMEM((16, obs), F32),
        ],
        in_specs=[VMEM, ANY, VMEM],
        out_specs=[VMEM] * 2,
        scratch_shapes=[pltpu.SMEM((1, obs), jnp.int32), pltpu.SemaphoreType.DMA],
        compiler_params=params,
        cost_estimate=pl.CostEstimate(flops=8_000_000_000, bytes_accessed=10_000_000, transcendentals=0),
        name="own",
    )(state_near, far(request_cell), w_own)
    turned = pltpu.with_memory_space_constraint(turned, pltpu.VMEM)
    answer = pl.pallas_call(
        lambda *refs: answer_kernel(levels, cells, *refs),
        out_shape=[jax.ShapeDtypeStruct((16, halo), F32)] * 2,
        in_specs=[VMEM] * 3,
        out_specs=[VMEM] * 2,
        scratch_shapes=[pltpu.VMEM((1, halo), jnp.int32)] * 2
        + [pltpu.SMEM((1, halo), jnp.int32)] * 2
        + [pltpu.SemaphoreType.DMA((2,))],
        compiler_params=params,
        cost_estimate=pl.CostEstimate(flops=4_000_000_000, bytes_accessed=1_000_000, transcendentals=0),
        name="answer",
    )
    eq_m2, eq_p2 = answer(turned, w_m2, w_p2)
    eq_m2, eq_p2 = passed_along(eq_m2, "cell", 2), passed_along(eq_p2, "cell", -2)
    eq_m1, eq_p1 = answer(turned, w_m1, w_p1)
    eq_m1, eq_p1 = passed_along(eq_m1, "cell", 1), passed_along(eq_p1, "cell", -1)

    def combine(tables, *before):
        firsts = [obs // 128 + n * halo // 128 if n >= 0 else 0 for n, _ in tables]
        return pl.pallas_call(
            lambda *refs: combine_kernel(firsts, *refs),
            out_shape=jax.ShapeDtypeStruct((8, obs + obs // 4), F32),
            in_specs=[VMEM] * (2 + len(before) + len(tables)),
            out_specs=VMEM,
            compiler_params=params,
            cost_estimate=pl.CostEstimate(flops=1_000_000_000, bytes_accessed=1_000_000, transcendentals=0),
            name="combine",
        )(slot_t, hw_t, *before, *(x for _, x in tables))

    own = combine([(-1, eq_own), (0, eq_m2), (3, eq_p2)])
    own = combine([(1, eq_m1), (2, eq_p1)], own)
    others = [passed_along(own, "mem", by) for by in (1, 2, 3)]
    wide = 4 * 16
    mid, to_prev, to_next = pl.pallas_call(
        lambda *refs: cov_kernel(members, *refs),
        out_shape=[jax.ShapeDtypeStruct((mem_dev * REG_DEV, wide), F32)] * 3,
        in_specs=[VMEM] * 7,
        out_specs=[VMEM] * 3,
        compiler_params=params,
        name="cov",
    )(own, *others, obs_value.reshape(1, obs), obs_error.reshape(1, obs), obs_region.reshape(1, obs))
    from_prev = passed_along(to_next, "cell", 1)
    from_next = passed_along(to_prev, "cell", -1)
    cov, proj = pl.pallas_call(
        final_kernel,
        out_shape=[
            jax.ShapeDtypeStruct((mem_dev, REG_DEV, members), F32),
            jax.ShapeDtypeStruct((REG_DEV, mem_dev), F32),
        ],
        in_specs=[VMEM] * 3,
        out_specs=[VMEM] * 2,
        compiler_params=params,
        name="final",
    )(mid, from_prev, from_next)
    return (jnp.transpose(cov, (1, 0, 2)), proj)


def solution(mesh):
    in_specs = (
        P("cell", "mem", None),
        P("cell", None),
        P("cell", None),
        P("cell", None),
        P("cell", None),
        P("cell"),
        P("cell"),
        P("cell"),
    )
    out_specs = (P("cell", "mem", None), P("cell", "mem"))
    return jax.shard_map(
        on_device, mesh=mesh, in_specs=in_specs, out_specs=out_specs, check_vma=False
    )
```

time: 88.9 us -> 55.1 us (0.62)
  Pallas kernels: 47.5 us -> 14.4 us
  local copies, waits for them, and re-layouts: 6.46 us -> 0.03 us
  starting transfers between devices: 25.6 us -> 31.7 us
    pallas_call x7, Pallas kernels: 46.2 us -> 13 us  [the longest x1 2.84 us: on_device(): pl.pallas_call(own_kernel, out_shape=[pltpu.VMEM((mem_dev * row_stride(ce...]
    unnamed x22 -> x10, local copies, waits for them, and re-layouts: 6.46 us -> 0.03 us
    ppermute x13, starting transfers between devices: 25.6 us -> 31.7 us  [passed_along(): lax.ppermute(x, axis, [(i, (i + by) % devices) for i in range(devices)])]
  transfers between devices with their start and end apart: 13 -> 13, of which waited for: 5 -> 6; matrix products, arithmetic and copies ran while one was open for 0% -> 0% of each run, Pallas kernels for 48% -> 18%
where the time goes in v2:
time: 55.1 us; the launch traced here: 55 us
  starting transfers between devices  31.7 us (58%)
  Pallas kernels  14.4 us (26%)
  waiting for transfers between devices  8.02 us (15%)
  between operations  0.78 us (1%)
    ppermute x13, starting transfers between devices, passed_along(): lax.ppermute(x, axis, [(i, (i + by) % devices) for i in range(devices)])  31.7 us
    ppermute x13, waiting for transfers between devices, passed_along(): lax.ppermute(x, axis, [(i, (i + by) % devices) for i in range(devices)])  8.02 us
    pallas_call x1, Pallas kernels, on_device(): pl.pallas_call(own_kernel, out_shape=[pltpu.VMEM((mem_dev * row_stride(ce...  2.84 us
    pallas_call x1, Pallas kernels, on_device(): pl.pallas_call(ask_far_kernel, out_shape=[pltpu.VMEM((neigh * obs // 128,...  2.63 us
    pallas_call x1, Pallas kernels, on_device(): eq_m2, eq_p2 = answer(turned, w_m2, w_p2)  2.46 us
    pallas_call x1, Pallas kernels, on_device(): eq_m1, eq_p1 = answer(turned, w_m1, w_p1)  2.46 us
    pallas_call x2, Pallas kernels, combine(): pl.pallas_call(lambda *refs: combine_kernel(firsts, *refs), out_shape=jax...  1.76 us
  transfers between devices with their start and end apart: 13, of which 6 were waited for; matrix products, arithmetic and copies ran while one was open for 0% of the time, Pallas kernels for 18%

profile of v2, /device:TPU:4, one launch (start us, length us, event | category | flops | bytes accessed | tf_op | source)
XLA Modules:
  0.0 55.0 jit_solution(2338818495480791537)
XLA Ops:
  0.6 2.6 %ask_far.1 = (s32[32,128]{1,0:T(8,128)S(1)}, bf16[120,1024]{1,0:T(8,128)(2,1)S(1)}, s32[1,4096]{1,0:T(1,128)S(1)}, bf16[10,128,2048]{2,1,0:T(8,128)(2,1)S(1)}, b...) custom-call(s32[4,1024]{1,0:T(4,128)} %bitcast.11, s32[1,4096]{1,0:T(1,128)} %table_hbm.3, ...), custom_call_target="tpu_custom_call" | custom-call | flops 2000000000 | bytes 6000000 | tf_op jit(solution)/shard_map/ask_far/pallas_call | solution.py:302
  3.3 8.4 %collective-permute-start = (bf16[128,768]{1,0:T(8,128)(2,1)S(1)}, bf16[128,768]{1,0:T(8,128)(2,1)S(1)}, u32[]{:S(2)}, u32[]{:S(2)}) collective-permute-start(bf16[128,768]{1,0:T(8,128)(2,1)S(1)} %get-tuple-element.29), channel_id=1, source_target_pairs={{0,62},{1,63},{2,0},{3,1},{4,2},{5,3},{6,4},{7,5},{8,6},{9,7},{10,... | collective-permute-start | bytes 589832 | tf_op jit(solution)/shard_map/ppermute | solution.py:21
  11.6 0.0 collective-permute-start.1
  11.7 0.9 %ask_near.1 = (bf16[128,1024]{1,0:T(8,128)(2,1)S(1)}, bf16[128,768]{1,0:T(8,128)(2,1)S(1)}, bf16[128,768]{1,0:T(8,128)(2,1)S(1)}) custom-call(s32[32,128]{1,0:T(8,128)S(1)} %get-tuple-element.23.inv_ref, bf16[120,1024]{1,0:T(8,128)(2,1)S(1)} %get-tuple-element.24.vw_ref, s32[1,4096]{1,0:T(1,128)S(1)} %get-tuple-element.25.table_ref), custom_call_target="tpu_custom_call" | custom-call | flops 2000000000 | bytes 1000000 | tf_op jit(solution)/shard_map/ask_near/pallas_call | solution.py:320
  12.5 4.3 %collective-permute-start.4 = (bf16[128,768]{1,0:T(8,128)(2,1)S(1)}, bf16[128,768]{1,0:T(8,128)(2,1)S(1)}, u32[]{:S(2)}, u32[]{:S(2)}) collective-permute-start(bf16[128,768]{1,0:T(8,128)(2,1)S(1)} %get-tuple-element.33), channel_id=1, source_target_pairs={{0,63},{1,0},{2,1},{3,2},{4,3},{5,4},{6,5},{7,6},{8,7},{9,8},{10,9... | collective-permute-start | bytes 589832 | tf_op jit(solution)/shard_map/ppermute | solution.py:21
  16.8 0.0 collective-permute-start.5
  16.8 2.8 %own.1 = (f32[20520,128]{1,0:T(8,128)S(1)}, f32[16,1024]{1,0:T(8,128)S(1)}) custom-call(bf16[10,128,2048]{2,1,0:T(8,128)(2,1)S(1)} %get-tuple-element.22.state_ref, s32[1,4096]{1,0:T(1,128)} %table_hbm.3, bf16[128,1024]{1,0:T(8,128)(2,1)S(1)} %get-tuple-element.26.w_ref), custom_call_target="tpu_custom_call" | custom-call | flops 8000000000 | bytes 10000000 | tf_op jit(solution)/shard_map/own/pallas_call | solution.py:330
  19.7 0.0 collective-permute-done.refs_1_
  19.7 1.6 %collective-permute-done.1.refs_2_ = bf16[128,768]{1,0:T(8,128)(2,1)S(1)} collective-permute-done((bf16[128,768]{1,0:T(8,128)(2,1)S(1)}, bf16[128,768]{1,0:T(8,128)(2,1)S(1)}, u32[]{:S(2)}, u32[]{:S(2)}) %collective-permute-start.1) | collective-permute-done | bytes 196640 | tf_op jit(solution)/shard_map/ppermute | solution.py:21
  21.3 2.5 %answer.2 = (f32[16,768]{1,0:T(8,128)S(1)}, f32[16,768]{1,0:T(8,128)S(1)}) custom-call(f32[20520,128]{1,0:T(8,128)S(1)} %get-tuple-element.28.refs_0_, bf16[128,768]{1,0:T(8,128)(2,1)S(1)} %collective-permute-done.refs_1_, bf16[128,768]{1,0:T(8,128)(2,1)S(1)} %collective-permute-done.1.refs_2_), custom_call_target="tpu_custom_call" | custom-call | flops 4000000000 | bytes 1000000 | tf_op jit(solution)/shard_map/answer/pallas_call | solution.py:356
  23.8 0.1 collective-permute-start.2
  23.9 0.0 copy-start.3
  23.9 0.0 copy-start.4
  23.9 5.3 %collective-permute-start.3 = (f32[16,768]{1,0:T(8,128)S(1)}, f32[16,768]{1,0:T(8,128)S(1)}, u32[]{:S(2)}, u32[]{:S(2)}) collective-permute-start(f32[16,768]{1,0:T(8,128)S(1)} %get-tuple-element.32), channel_id=1, source_target_pairs={{0,62},{1,63},{2,0},{3,1},{4,2},{5,3},{6,4},{7,5},{8,6},{9,7},{10,... | collective-permute-start | bytes 147464 | tf_op jit(solution)/shard_map/ppermute | solution.py:21
  29.2 0.0 collective-permute-done.4.refs_1_
  29.2 0.0 collective-permute-done.5.refs_2_
  29.2 2.5 %answer.3 = (f32[16,768]{1,0:T(8,128)S(1)}, f32[16,768]{1,0:T(8,128)S(1)}) custom-call(f32[20520,128]{1,0:T(8,128)S(1)} %get-tuple-element.28.refs_0_, bf16[128,768]{1,0:T(8,128)(2,1)S(1)} %collective-permute-done.4.refs_1_, bf16[128,768]{1,0:T(8,128)(2,1)S(1)} %collective-permute-done.5.refs_2_), custom_call_target="tpu_custom_call" | custom-call | flops 4000000000 | bytes 1000000 | tf_op jit(solution)/shard_map/answer/pallas_call | solution.py:358
  31.7 0.0 copy-start
  31.7 0.0 copy-start.1
  31.7 0.0 copy-start.2
  31.7 0.1 collective-permute-start.6
  31.8 5.1 %collective-permute-start.7 = (f32[16,768]{1,0:T(8,128)S(1)}, f32[16,768]{1,0:T(8,128)S(1)}, u32[]{:S(2)}, u32[]{:S(2)}) collective-permute-start(f32[16,768]{1,0:T(8,128)S(1)} %get-tuple-element.36), channel_id=1, source_target_pairs={{0,63},{1,0},{2,1},{3,2},{4,3},{5,4},{6,5},{7,6},{8,7},{9,8},{10,9... | collective-permute-start | bytes 147464 | tf_op jit(solution)/shard_map/ppermute | solution.py:21
  36.9 0.0 collective-permute-done.2.refs_3_
  36.9 0.0 collective-permute-done.3.refs_4_
  36.9 0.0 copy-done.3
  36.9 0.0 copy-done.4
  36.9 1.0 %combine.2.refs_2_ = f32[8,1280]{1,0:T(8,128)S(1)} custom-call(s32[4,1024]{1,0:T(4,128)S(1)} %bitcast.12, f32[4,1024]{1,0:T(4,128)S(1)} %bitcast.14, f32[16,1024]{1,0:T(8,128)S(1)} %get-tuple-element.27.refs_2_, f32[16,768]{1,0:T(8,128)S(1)} %collective-permute-done.2.refs_3_, f32[16,768]{1,0:T(8,128)S(1)} %collective-permute-done.3.refs_4_), custom_call_target="tpu_custom_call" | custom-call | flops 1000000000 | bytes 1000000 | tf_op jit(solution)/shard_map/combine/pallas_call | solution.py:363
  38.0 0.7 %collective-permute-done.6.refs_3_ = f32[16,768]{1,0:T(8,128)S(1)} collective-permute-done((f32[16,768]{1,0:T(8,128)S(1)}, f32[16,768]{1,0:T(8,128)S(1)}, u32[]{:S(2)}, u32[]{:S(2)}) %collective-permute-start.6) | collective-permute-done | bytes 49184 | tf_op jit(solution)/shard_map/ppermute | solution.py:21
  38.7 0.0 collective-permute-done.7.refs_4_
  38.7 0.7 %combine.3.refs_0_ = f32[8,1280]{1,0:T(8,128)S(1)} custom-call(s32[4,1024]{1,0:T(4,128)S(1)} %bitcast.13, f32[4,1024]{1,0:T(4,128)S(1)} %bitcast.15, f32[8,1280]{1,0:T(8,128)S(1)} %combine.2.refs_2_, f32[16,768]{1,0:T(8,128)S(1)} %collective-permute-done.6.refs_3_, f32[16,768]{1,0:T(8,128)S(1)} %collective-permute-done.7.refs_4_), custom_call_target="tpu_custom_call" | custom-call | flops 1000000000 | bytes 1000000 | tf_op jit(solution)/shard_map/combine/pallas_call | solution.py:363
  39.4 0.6 %collective-permute-start.10 = (f32[8,1280]{1,0:T(8,128)S(1)}, f32[8,1280]{1,0:T(8,128)S(1)}, u32[]{:S(2)}, u32[]{:S(2)}) collective-permute-start(f32[8,1280]{1,0:T(8,128)S(1)} %combine.3.refs_0_), channel_id=1, source_target_pairs={{0,192},{64,0},{128,64},{192,128},{1,193},{65,1},{129,65},{193,129... | collective-permute-start | bytes 122888 | tf_op jit(solution)/shard_map/ppermute | solution.py:21
  40.0 2.7 %collective-permute-start.9 = (f32[8,1280]{1,0:T(8,128)S(1)}, f32[8,1280]{1,0:T(8,128)S(1)}, u32[]{:S(2)}, u32[]{:S(2)}) collective-permute-start(f32[8,1280]{1,0:T(8,128)S(1)} %combine.3.refs_0_), channel_id=1, source_target_pairs={{0,128},{64,192},{128,0},{192,64},{1,129},{65,193},{129,1},{193,65... | collective-permute-start | bytes 122888 | tf_op jit(solution)/shard_map/ppermute | solution.py:21
  42.7 0.0 collective-permute-start.8
  42.7 0.7 %collective-permute-done.10.refs_3_ = f32[8,1280]{1,0:T(8,128)S(1)} collective-permute-done((f32[8,1280]{1,0:T(8,128)S(1)}, f32[8,1280]{1,0:T(8,128)S(1)}, u32[]{:S(2)}, u32[]{:S(2)}) %collective-permute-start.10) | collective-permute-done | bytes 40992 | tf_op jit(solution)/shard_map/ppermute | solution.py:21
  43.5 2.0 %collective-permute-done.9.refs_2_ = f32[8,1280]{1,0:T(8,128)S(1)} collective-permute-done((f32[8,1280]{1,0:T(8,128)S(1)}, f32[8,1280]{1,0:T(8,128)S(1)}, u32[]{:S(2)}, u32[]{:S(2)}) %collective-permute-start.9) | collective-permute-done | bytes 40992 | tf_op jit(solution)/shard_map/ppermute | solution.py:21
  45.5 1.2 %collective-permute-done.8.refs_1_ = f32[8,1280]{1,0:T(8,128)S(1)} collective-permute-done((f32[8,1280]{1,0:T(8,128)S(1)}, f32[8,1280]{1,0:T(8,128)S(1)}, u32[]{:S(2)}, u32[]{:S(2)}) %collective-permute-start.8) | collective-permute-done | bytes 40992 | tf_op jit(solution)/shard_map/ppermute | solution.py:21
  46.7 0.0 copy-done
  46.7 0.0 copy-done.1
  46.7 0.0 copy-done.2
  46.7 0.6 %cov.1 = (f32[80,64]{1,0:T(8,128)S(1)}, f32[80,64]{1,0:T(8,128)S(1)}, f32[80,64]{1,0:T(8,128)S(1)}) custom-call(f32[8,1280]{1,0:T(8,128)S(1)} %combine.3.refs_0_, f32[8,1280]{1,0:T(8,128)S(1)} %collective-permute-done.8.refs_1_, f32[8,1280]{1,0:T(8,128)S(1)} %collective-permute-done.9.refs_2_, f32[8,1280]{1,0:T(8,128)S(1)} %collective-permute-done.10.refs_3_, ...), custom_call_target="tpu_custom_call" | custom-call | tf_op jit(solution)/shard_map/cov/pallas_call | solution.py:377
  47.3 0.1 collective-permute-start.11
  47.4 5.1 %collective-permute-start.12 = (f32[80,64]{1,0:T(8,128)S(1)}, f32[80,64]{1,0:T(8,128)S(1)}, u32[]{:S(2)}, u32[]{:S(2)}) collective-permute-start(f32[80,64]{1,0:T(8,128)S(1)} %get-tuple-element.39), channel_id=1, source_target_pairs={{0,63},{1,0},{2,1},{3,2},{4,3},{5,4},{6,5},{7,6},{8,7},{9,8},{10,9... | collective-permute-start | bytes 61448 | tf_op jit(solution)/shard_map/ppermute | solution.py:21
  52.5 1.7 %collective-permute-done.11.a_ref = f32[80,64]{1,0:T(8,128)S(1)} collective-permute-done((f32[80,64]{1,0:T(8,128)S(1)}, f32[80,64]{1,0:T(8,128)S(1)}, u32[]{:S(2)}, u32[]{:S(2)}) %collective-permute-start.11) | collective-permute-done | bytes 20512 | tf_op jit(solution)/shard_map/ppermute | solution.py:21
  54.1 0.0 collective-permute-done.12.b_ref
  54.2 0.8 %final.1 = (f32[10,8,40]{2,1,0:T(8,128)}, f32[8,10]{1,0:T(8,128)}) custom-call(f32[80,64]{1,0:T(8,128)S(1)} %get-tuple-element.37.mid_ref, f32[80,64]{1,0:T(8,128)S(1)} %collective-permute-done.11.a_ref, f32[80,64]{1,0:T(8,128)S(1)} %collective-permute-done.12.b_ref), custom_call_target="tpu_custom_call" | custom-call | tf_op jit(solution)/shard_map/final/pallas_call | solution.py:387
Async XLA Ops:
  3.3 16.4 %collective-permute-start = (bf16[128,768]{1,0:T(8,128)(2,1)S(1)}, bf16[128,768]{1,0:T(8,128)(2,1)S(1)}, u32[]{:S(2)}, u32[]{:S(2)}) collective-permute-start(bf16[128,768]{1,0:T(8,128)(2,1)S(1)} %get-tuple-element.29), channel_id=1, source_target_pairs={{0,62},{1,63},{2,0},{3,1},{4,2},{5,3},{6,4},{7,5},{8,6},{9,7},{10,... | collective-permute-start | bytes 589832 | tf_op jit(solution)/shard_map/ppermute | solution.py:21
  11.6 9.7 %collective-permute-start.1 = (bf16[128,768]{1,0:T(8,128)(2,1)S(1)}, bf16[128,768]{1,0:T(8,128)(2,1)S(1)}, u32[]{:S(2)}, u32[]{:S(2)}) collective-permute-start(bf16[128,768]{1,0:T(8,128)(2,1)S(1)} %get-tuple-element.30), channel_id=1, source_target_pairs={{0,2},{1,3},{2,4},{3,5},{4,6},{5,7},{6,8},{7,9},{8,10},{9,11},{10,... | collective-permute-start | bytes 589832 | tf_op jit(solution)/shard_map/ppermute | solution.py:21
  12.5 16.7 %collective-permute-start.4 = (bf16[128,768]{1,0:T(8,128)(2,1)S(1)}, bf16[128,768]{1,0:T(8,128)(2,1)S(1)}, u32[]{:S(2)}, u32[]{:S(2)}) collective-permute-start(bf16[128,768]{1,0:T(8,128)(2,1)S(1)} %get-tuple-element.33), channel_id=1, source_target_pairs={{0,63},{1,0},{2,1},{3,2},{4,3},{5,4},{6,5},{7,6},{8,7},{9,8},{10,9... | collective-permute-start | bytes 589832 | tf_op jit(solution)/shard_map/ppermute | solution.py:21
  16.8 12.4 %collective-permute-start.5 = (bf16[128,768]{1,0:T(8,128)(2,1)S(1)}, bf16[128,768]{1,0:T(8,128)(2,1)S(1)}, u32[]{:S(2)}, u32[]{:S(2)}) collective-permute-start(bf16[128,768]{1,0:T(8,128)(2,1)S(1)} %get-tuple-element.34), channel_id=1, source_target_pairs={{0,1},{1,2},{2,3},{3,4},{4,5},{5,6},{6,7},{7,8},{8,9},{9,10},{10,1... | collective-permute-start | bytes 589832 | tf_op jit(solution)/shard_map/ppermute | solution.py:21
  23.8 13.1 %collective-permute-start.2 = (f32[16,768]{1,0:T(8,128)S(1)}, f32[16,768]{1,0:T(8,128)S(1)}, u32[]{:S(2)}, u32[]{:S(2)}) collective-permute-start(f32[16,768]{1,0:T(8,128)S(1)} %get-tuple-element.31), channel_id=1, source_target_pairs={{0,2},{1,3},{2,4},{3,5},{4,6},{5,7},{6,8},{7,9},{8,10},{9,11},{10,... | collective-permute-start | bytes 147464 | tf_op jit(solution)/shard_map/ppermute | solution.py:21
  23.9 13.0 %copy-start.3 = (s32[1024,4]{0,1:T(4,128)S(1)}, s32[1024,4]{0,1:T(4,128)}, u32[]{:S(2)}) copy-start(s32[1024,4]{0,1:T(4,128)} %param.11) | copy-start | bytes 49156
  23.9 13.0 %copy-start.4 = (f32[1024,4]{0,1:T(4,128)S(1)}, f32[1024,4]{0,1:T(4,128)}, u32[]{:S(2)}) copy-start(f32[1024,4]{0,1:T(4,128)} %param.10) | copy-start | bytes 49156
  23.9 13.0 %collective-permute-start.3 = (f32[16,768]{1,0:T(8,128)S(1)}, f32[16,768]{1,0:T(8,128)S(1)}, u32[]{:S(2)}, u32[]{:S(2)}) collective-permute-start(f32[16,768]{1,0:T(8,128)S(1)} %get-tuple-element.32), channel_id=1, source_target_pairs={{0,62},{1,63},{2,0},{3,1},{4,2},{5,3},{6,4},{7,5},{8,6},{9,7},{10,... | collective-permute-start | bytes 147464 | tf_op jit(solution)/shard_map/ppermute | solution.py:21
  31.7 15.0 %copy-start = (f32[1024]{0:T(1024)S(1)}, f32[1024]{0:T(1024)}, u32[]{:S(2)}) copy-start(f32[1024]{0:T(1024)} %param.13) | copy-start | bytes 12292
  31.7 15.0 %copy-start.1 = (f32[1024]{0:T(1024)S(1)}, f32[1024]{0:T(1024)}, u32[]{:S(2)}) copy-start(f32[1024]{0:T(1024)} %param.14) | copy-start | bytes 12292
  31.7 15.0 %copy-start.2 = (s32[1024]{0:T(1024)S(1)}, s32[1024]{0:T(1024)}, u32[]{:S(2)}) copy-start(s32[1024]{0:T(1024)} %param.15) | copy-start | bytes 12292
  31.7 6.9 %collective-permute-start.6 = (f32[16,768]{1,0:T(8,128)S(1)}, f32[16,768]{1,0:T(8,128)S(1)}, u32[]{:S(2)}, u32[]{:S(2)}) collective-permute-start(f32[16,768]{1,0:T(8,128)S(1)} %get-tuple-element.35), channel_id=1, source_target_pairs={{0,1},{1,2},{2,3},{3,4},{4,5},{5,6},{6,7},{7,8},{8,9},{9,10},{10,1... | collective-permute-start | bytes 147464 | tf_op jit(solution)/shard_map/ppermute | solution.py:21
  31.8 6.8 %collective-permute-start.7 = (f32[16,768]{1,0:T(8,128)S(1)}, f32[16,768]{1,0:T(8,128)S(1)}, u32[]{:S(2)}, u32[]{:S(2)}) collective-permute-start(f32[16,768]{1,0:T(8,128)S(1)} %get-tuple-element.36), channel_id=1, source_target_pairs={{0,63},{1,0},{2,1},{3,2},{4,3},{5,4},{6,5},{7,6},{8,7},{9,8},{10,9... | collective-permute-start | bytes 147464 | tf_op jit(solution)/shard_map/ppermute | solution.py:21
  39.4 4.1 %collective-permute-start.10 = (f32[8,1280]{1,0:T(8,128)S(1)}, f32[8,1280]{1,0:T(8,128)S(1)}, u32[]{:S(2)}, u32[]{:S(2)}) collective-permute-start(f32[8,1280]{1,0:T(8,128)S(1)} %combine.3.refs_0_), channel_id=1, source_target_pairs={{0,192},{64,0},{128,64},{192,128},{1,193},{65,1},{129,65},{193,129... | collective-permute-start | bytes 122888 | tf_op jit(solution)/shard_map/ppermute | solution.py:21
  40.0 5.5 %collective-permute-start.9 = (f32[8,1280]{1,0:T(8,128)S(1)}, f32[8,1280]{1,0:T(8,128)S(1)}, u32[]{:S(2)}, u32[]{:S(2)}) collective-permute-start(f32[8,1280]{1,0:T(8,128)S(1)} %combine.3.refs_0_), channel_id=1, source_target_pairs={{0,128},{64,192},{128,0},{192,64},{1,129},{65,193},{129,1},{193,65... | collective-permute-start | bytes 122888 | tf_op jit(solution)/shard_map/ppermute | solution.py:21
  42.7 4.0 %collective-permute-start.8 = (f32[8,1280]{1,0:T(8,128)S(1)}, f32[8,1280]{1,0:T(8,128)S(1)}, u32[]{:S(2)}, u32[]{:S(2)}) collective-permute-start(f32[8,1280]{1,0:T(8,128)S(1)} %combine.3.refs_0_), channel_id=1, source_target_pairs={{0,64},{64,128},{128,192},{192,0},{1,65},{65,129},{129,193},{193,1... | collective-permute-start | bytes 122888 | tf_op jit(solution)/shard_map/ppermute | solution.py:21
  47.3 6.8 %collective-permute-start.11 = (f32[80,64]{1,0:T(8,128)S(1)}, f32[80,64]{1,0:T(8,128)S(1)}, u32[]{:S(2)}, u32[]{:S(2)}) collective-permute-start(f32[80,64]{1,0:T(8,128)S(1)} %get-tuple-element.38), channel_id=1, source_target_pairs={{0,1},{1,2},{2,3},{3,4},{4,5},{5,6},{6,7},{7,8},{8,9},{9,10},{10,1... | collective-permute-start | bytes 61448 | tf_op jit(solution)/shard_map/ppermute | solution.py:21
  47.4 6.7 %collective-permute-start.12 = (f32[80,64]{1,0:T(8,128)S(1)}, f32[80,64]{1,0:T(8,128)S(1)}, u32[]{:S(2)}, u32[]{:S(2)}) collective-permute-start(f32[80,64]{1,0:T(8,128)S(1)} %get-tuple-element.39), channel_id=1, source_target_pairs={{0,63},{1,0},{2,1},{3,2},{4,3},{5,4},{6,5},{7,6},{8,7},{9,8},{10,9... | collective-permute-start | bytes 61448 | tf_op jit(solution)/shard_map/ppermute | solution.py:21

commit v3 on v2

--- a/solution.py
+++ b/solution.py
@@ -62,7 +62,7 @@
     return jnp.concatenate([w, extra], axis=0).astype(BF16)
 
 
-def ask_far_kernel(slot_hbm, table_hbm, vw_hbm, state_hbm, inv_ref, vw_ref, table_ref, state_ref, *refs):
+def ask_low_kernel(slot_hbm, table_hbm, vw_hbm, state_hbm, inv_ref, vw_ref, table_ref, state_ref, *refs):
     *out_refs, slot_ref, sems = refs
     members, levels, cells = state_hbm.shape
     pairs = (
@@ -78,14 +78,14 @@
     inv_ref[...] = slot_owner(slot_ref)
     copies[1].wait()
     copies[2].wait()
-    halo_weights(inv_ref, vw_ref, table_ref, out_refs, (0, 3))
+    halo_weights(inv_ref, vw_ref, table_ref, out_refs, (0, 1))
     copies[3].wait()
     for m in range(members):
         state_ref[m, levels:, :] = jnp.zeros((state_ref.shape[1] - levels, cells), BF16)
 
 
-def ask_near_kernel(inv_ref, vw_ref, table_ref, own_ref, *out_refs):
-    halo_weights(inv_ref, vw_ref, table_ref, out_refs, (1, 2))
+def ask_high_kernel(inv_ref, vw_ref, table_ref, own_ref, *out_refs):
+    halo_weights(inv_ref, vw_ref, table_ref, out_refs, (2, 3))
     for tile in range(own_ref.shape[1] // TILE):
         own_ref[:, tile * TILE : (tile + 1) * TILE] = slot_weights(inv_ref, vw_ref, tile)
 
@@ -299,8 +299,8 @@
     params = pltpu.CompilerParams(vmem_limit_bytes=16 * 1024 * 1024)
 
     w_shape = jax.ShapeDtypeStruct((128, halo), BF16)
-    inv, vw_near, table, state_near, ask_m2, ask_p2 = pl.pallas_call(
-        ask_far_kernel,
+    inv, vw_near, table, state_near, ask_m2, ask_m1 = pl.pallas_call(
+        ask_low_kernel,
         out_shape=[
             pltpu.VMEM((neigh * obs // 128, 128), jnp.int32),
             pltpu.VMEM((levels, obs), BF16),
@@ -314,19 +314,19 @@
         scratch_shapes=[pltpu.VMEM((neigh, obs), jnp.int32), pltpu.SemaphoreType.DMA((4,))],
         compiler_params=params,
         cost_estimate=pl.CostEstimate(flops=2_000_000_000, bytes_accessed=6_000_000, transcendentals=0),
-        name="ask_far",
+        name="ask_low",
     )(far(slot_t), far(request_cell), far(vw_t), far(state_t))
-    w_m2, w_p2 = passed_along(ask_m2, "cell", -2), passed_along(ask_p2, "cell", 2)
-    w_own, ask_m1, ask_p1 = pl.pallas_call(
-        ask_near_kernel,
+    w_m2, w_m1 = passed_along(ask_m2, "cell", -2), passed_along(ask_m1, "cell", -1)
+    w_own, ask_p1, ask_p2 = pl.pallas_call(
+        ask_high_kernel,
         out_shape=[pltpu.VMEM((128, obs), BF16), w_shape, w_shape],
         in_specs=[VMEM] * 3,
         out_specs=[VMEM] * 3,
         compiler_params=params,
         cost_estimate=pl.CostEstimate(flops=2_000_000_000, bytes_accessed=1_000_000, transcendentals=0),
-        name="ask_near",
+        name="ask_high",
     )(inv, vw_near, table)
-    w_m1, w_p1 = passed_along(ask_m1, "cell", -1), passed_along(ask_p1, "cell", 1)
+    w_p1, w_p2 = passed_along(ask_p1, "cell", 1), passed_along(ask_p2, "cell", 2)
     turned, eq_own = pl.pallas_call(
         own_kernel,
         out_shape=[
@@ -353,10 +353,10 @@
         cost_estimate=pl.CostEstimate(flops=4_000_000_000, bytes_accessed=1_000_000, transcendentals=0),
         name="answer",
     )
-    eq_m2, eq_p2 = answer(turned, w_m2, w_p2)
-    eq_m2, eq_p2 = passed_along(eq_m2, "cell", 2), passed_along(eq_p2, "cell", -2)
-    eq_m1, eq_p1 = answer(turned, w_m1, w_p1)
-    eq_m1, eq_p1 = passed_along(eq_m1, "cell", 1), passed_along(eq_p1, "cell", -1)
+    eq_m2, eq_m1 = answer(turned, w_m2, w_m1)
+    eq_m2, eq_m1 = passed_along(eq_m2, "cell", 2), passed_along(eq_m1, "cell", 1)
+    eq_p1, eq_p2 = answer(turned, w_p1, w_p2)
+    eq_p1, eq_p2 = passed_along(eq_p1, "cell", -1), passed_along(eq_p2, "cell", -2)
 
     def combine(tables, *before):
         firsts = [obs // 128 + n * halo // 128 if n >= 0 else 0 for n, _ in tables]
@@ -370,8 +370,8 @@
             name="combine",
         )(slot_t, hw_t, *before, *(x for _, x in tables))
 
-    own = combine([(-1, eq_own), (0, eq_m2), (3, eq_p2)])
-    own = combine([(1, eq_m1), (2, eq_p1)], own)
+    own = combine([(-1, eq_own), (0, eq_m2), (1, eq_m1)])
+    own = combine([(2, eq_p1), (3, eq_p2)], own)
     others = [passed_along(own, "mem", by) for by in (1, 2, 3)]
     wide = 4 * 16
     mid, to_prev, to_next = pl.pallas_call(

time: 55.1 us -> 49.2 us (0.89)
  starting transfers between devices: 31.7 us -> 22 us
  waiting for transfers between devices: 8.02 us -> 11.8 us
    ppermute x13, starting transfers between devices: 31.7 us -> 22 us  [passed_along(): lax.ppermute(x, axis, [(i, (i + by) % devices) for i in range(devices)])]
    ppermute x13, waiting for transfers between devices: 8.02 us -> 11.8 us  [passed_along(): lax.ppermute(x, axis, [(i, (i + by) % devices) for i in range(devices)])]
  transfers between devices with their start and end apart: 13 -> 13, of which waited for: 6 -> 8; matrix products, arithmetic and copies ran while one was open for 0% -> 0% of each run, Pallas kernels for 18% -> 20%
where the time goes in v3:
time: 49.2 us; the launch traced here: 49 us
  starting transfers between devices  22 us (45%)
  Pallas kernels  14.4 us (29%)
  waiting for transfers between devices  11.8 us (24%)
  between operations  0.79 us (2%)
    ppermute x13, starting transfers between devices, passed_along(): lax.ppermute(x, axis, [(i, (i + by) % devices) for i in range(devices)])  22 us
    ppermute x13, waiting for transfers between devices, passed_along(): lax.ppermute(x, axis, [(i, (i + by) % devices) for i in range(devices)])  11.8 us
    pallas_call x1, Pallas kernels, on_device(): pl.pallas_call(own_kernel, out_shape=[pltpu.VMEM((mem_dev * row_stride(ce...  2.85 us
    pallas_call x1, Pallas kernels, on_device(): pl.pallas_call(ask_low_kernel, out_shape=[pltpu.VMEM((neigh * obs // 128,...  2.63 us
    pallas_call x1, Pallas kernels, on_device(): eq_p1, eq_p2 = answer(turned, w_p1, w_p2)  2.47 us
    pallas_call x1, Pallas kernels, on_device(): eq_m2, eq_m1 = answer(turned, w_m2, w_m1)  2.47 us
    pallas_call x2, Pallas kernels, combine(): pl.pallas_call(lambda *refs: combine_kernel(firsts, *refs), out_shape=jax...  1.69 us
  transfers between devices with their start and end apart: 13, of which 8 were waited for; matrix products, arithmetic and copies ran while one was open for 0% of the time, Pallas kernels for 20%

profile of v3, /device:TPU:4, one launch (start us, length us, event | category | flops | bytes accessed | tf_op | source)
XLA Modules:
  0.0 49.0 jit_solution(2088248081858388940)
XLA Ops:
  0.6 2.6 %ask_low.1 = (s32[32,128]{1,0:T(8,128)S(1)}, bf16[120,1024]{1,0:T(8,128)(2,1)S(1)}, s32[1,4096]{1,0:T(1,128)S(1)}, bf16[10,128,2048]{2,1,0:T(8,128)(2,1)S(1)}, b...) custom-call(s32[4,1024]{1,0:T(4,128)} %bitcast.11, s32[1,4096]{1,0:T(1,128)} %table_hbm.3, ...), custom_call_target="tpu_custom_call" | custom-call | flops 2000000000 | bytes 6000000 | tf_op jit(solution)/shard_map/ask_low/pallas_call | solution.py:302
  3.3 8.4 %collective-permute-start = (bf16[128,768]{1,0:T(8,128)(2,1)S(1)}, bf16[128,768]{1,0:T(8,128)(2,1)S(1)}, u32[]{:S(2)}, u32[]{:S(2)}) collective-permute-start(bf16[128,768]{1,0:T(8,128)(2,1)S(1)} %get-tuple-element.29), channel_id=1, source_target_pairs={{0,62},{1,63},{2,0},{3,1},{4,2},{5,3},{6,4},{7,5},{8,6},{9,7},{10,... | collective-permute-start | bytes 589832 | tf_op jit(solution)/shard_map/ppermute | solution.py:21
  11.6 0.2 collective-permute-start.1
  11.8 0.9 %ask_high.1 = (bf16[128,1024]{1,0:T(8,128)(2,1)S(1)}, bf16[128,768]{1,0:T(8,128)(2,1)S(1)}, bf16[128,768]{1,0:T(8,128)(2,1)S(1)}) custom-call(s32[32,128]{1,0:T(8,128)S(1)} %get-tuple-element.23.inv_ref, bf16[120,1024]{1,0:T(8,128)(2,1)S(1)} %get-tuple-element.24.vw_ref, s32[1,4096]{1,0:T(1,128)S(1)} %get-tuple-element.25.table_ref), custom_call_target="tpu_custom_call" | custom-call | flops 2000000000 | bytes 1000000 | tf_op jit(solution)/shard_map/ask_high/pallas_call | solution.py:320
  12.7 0.4 collective-permute-start.4
  13.1 0.8 %collective-permute-start.5 = (bf16[128,768]{1,0:T(8,128)(2,1)S(1)}, bf16[128,768]{1,0:T(8,128)(2,1)S(1)}, u32[]{:S(2)}, u32[]{:S(2)}) collective-permute-start(bf16[128,768]{1,0:T(8,128)(2,1)S(1)} %get-tuple-element.34), channel_id=1, source_target_pairs={{0,2},{1,3},{2,4},{3,5},{4,6},{5,7},{6,8},{7,9},{8,10},{9,11},{10,... | collective-permute-start | bytes 589832 | tf_op jit(solution)/shard_map/ppermute | solution.py:21
  13.9 2.9 %own.1 = (f32[20520,128]{1,0:T(8,128)S(1)}, f32[16,1024]{1,0:T(8,128)S(1)}) custom-call(bf16[10,128,2048]{2,1,0:T(8,128)(2,1)S(1)} %get-tuple-element.22.state_ref, s32[1,4096]{1,0:T(1,128)} %table_hbm.3, bf16[128,1024]{1,0:T(8,128)(2,1)S(1)} %get-tuple-element.26.w_ref), custom_call_target="tpu_custom_call" | custom-call | flops 8000000000 | bytes 10000000 | tf_op jit(solution)/shard_map/own/pallas_call | solution.py:330
  16.7 0.0 collective-permute-done.refs_1_
  16.8 1.2 %collective-permute-done.1.refs_2_ = bf16[128,768]{1,0:T(8,128)(2,1)S(1)} collective-permute-done((bf16[128,768]{1,0:T(8,128)(2,1)S(1)}, bf16[128,768]{1,0:T(8,128)(2,1)S(1)}, u32[]{:S(2)}, u32[]{:S(2)}) %collective-permute-start.1) | collective-permute-done | bytes 196640 | tf_op jit(solution)/shard_map/ppermute | solution.py:21
  17.9 2.5 %answer.2 = (f32[16,768]{1,0:T(8,128)S(1)}, f32[16,768]{1,0:T(8,128)S(1)}) custom-call(f32[20520,128]{1,0:T(8,128)S(1)} %get-tuple-element.28.refs_0_, bf16[128,768]{1,0:T(8,128)(2,1)S(1)} %collective-permute-done.refs_1_, bf16[128,768]{1,0:T(8,128)(2,1)S(1)} %collective-permute-done.1.refs_2_), custom_call_target="tpu_custom_call" | custom-call | flops 4000000000 | bytes 1000000 | tf_op jit(solution)/shard_map/answer/pallas_call | solution.py:356
  20.4 0.1 collective-permute-start.2
  20.5 0.0 copy-start.3
  20.5 0.0 copy-start.4
  20.5 0.3 collective-permute-start.3
  20.8 1.6 %collective-permute-done.4.refs_1_ = bf16[128,768]{1,0:T(8,128)(2,1)S(1)} collective-permute-done((bf16[128,768]{1,0:T(8,128)(2,1)S(1)}, bf16[128,768]{1,0:T(8,128)(2,1)S(1)}, u32[]{:S(2)}, u32[]{:S(2)}) %collective-permute-start.4) | collective-permute-done | bytes 196640 | tf_op jit(solution)/shard_map/ppermute | solution.py:21
  22.4 1.8 %collective-permute-done.5.refs_2_ = bf16[128,768]{1,0:T(8,128)(2,1)S(1)} collective-permute-done((bf16[128,768]{1,0:T(8,128)(2,1)S(1)}, bf16[128,768]{1,0:T(8,128)(2,1)S(1)}, u32[]{:S(2)}, u32[]{:S(2)}) %collective-permute-start.5) | collective-permute-done | bytes 196640 | tf_op jit(solution)/shard_map/ppermute | solution.py:21
  24.2 2.5 %answer.3 = (f32[16,768]{1,0:T(8,128)S(1)}, f32[16,768]{1,0:T(8,128)S(1)}) custom-call(f32[20520,128]{1,0:T(8,128)S(1)} %get-tuple-element.28.refs_0_, bf16[128,768]{1,0:T(8,128)(2,1)S(1)} %collective-permute-done.4.refs_1_, bf16[128,768]{1,0:T(8,128)(2,1)S(1)} %collective-permute-done.5.refs_2_), custom_call_target="tpu_custom_call" | custom-call | flops 4000000000 | bytes 1000000 | tf_op jit(solution)/shard_map/answer/pallas_call | solution.py:358
  26.7 0.0 copy-start
  26.7 0.0 copy-start.1
  26.7 0.0 copy-start.2
  26.7 1.9 %collective-permute-start.6 = (f32[16,768]{1,0:T(8,128)S(1)}, f32[16,768]{1,0:T(8,128)S(1)}, u32[]{:S(2)}, u32[]{:S(2)}) collective-permute-start(f32[16,768]{1,0:T(8,128)S(1)} %get-tuple-element.35), channel_id=1, source_target_pairs={{0,63},{1,0},{2,1},{3,2},{4,3},{5,4},{6,5},{7,6},{8,7},{9,8},{10,9... | collective-permute-start | bytes 147464 | tf_op jit(solution)/shard_map/ppermute | solution.py:21
  28.6 1.6 %collective-permute-start.7 = (f32[16,768]{1,0:T(8,128)S(1)}, f32[16,768]{1,0:T(8,128)S(1)}, u32[]{:S(2)}, u32[]{:S(2)}) collective-permute-start(f32[16,768]{1,0:T(8,128)S(1)} %get-tuple-element.36), channel_id=1, source_target_pairs={{0,62},{1,63},{2,0},{3,1},{4,2},{5,3},{6,4},{7,5},{8,6},{9,7},{10,... | collective-permute-start | bytes 147464 | tf_op jit(solution)/shard_map/ppermute | solution.py:21
  30.2 0.0 collective-permute-done.2.refs_3_
  30.2 0.0 collective-permute-done.3.refs_4_
  30.2 0.0 copy-done.3
  30.2 0.0 copy-done.4
  30.2 1.0 %combine.2.refs_2_ = f32[8,1280]{1,0:T(8,128)S(1)} custom-call(s32[4,1024]{1,0:T(4,128)S(1)} %bitcast.12, f32[4,1024]{1,0:T(4,128)S(1)} %bitcast.14, f32[16,1024]{1,0:T(8,128)S(1)} %get-tuple-element.27.refs_2_, f32[16,768]{1,0:T(8,128)S(1)} %collective-permute-done.2.refs_3_, f32[16,768]{1,0:T(8,128)S(1)} %collective-permute-done.3.refs_4_), custom_call_target="tpu_custom_call" | custom-call | flops 1000000000 | bytes 1000000 | tf_op jit(solution)/shard_map/combine/pallas_call | solution.py:363
  31.2 0.0 collective-permute-done.6.refs_3_
  31.2 1.5 %collective-permute-done.7.refs_4_ = f32[16,768]{1,0:T(8,128)S(1)} collective-permute-done((f32[16,768]{1,0:T(8,128)S(1)}, f32[16,768]{1,0:T(8,128)S(1)}, u32[]{:S(2)}, u32[]{:S(2)}) %collective-permute-start.7) | collective-permute-done | bytes 49184 | tf_op jit(solution)/shard_map/ppermute | solution.py:21
  32.7 0.7 %combine.3.refs_0_ = f32[8,1280]{1,0:T(8,128)S(1)} custom-call(s32[4,1024]{1,0:T(4,128)S(1)} %bitcast.13, f32[4,1024]{1,0:T(4,128)S(1)} %bitcast.15, f32[8,1280]{1,0:T(8,128)S(1)} %combine.2.refs_2_, f32[16,768]{1,0:T(8,128)S(1)} %collective-permute-done.6.refs_3_, f32[16,768]{1,0:T(8,128)S(1)} %collective-permute-done.7.refs_4_), custom_call_target="tpu_custom_call" | custom-call | flops 1000000000 | bytes 1000000 | tf_op jit(solution)/shard_map/combine/pallas_call | solution.py:363
  33.4 0.6 %collective-permute-start.10 = (f32[8,1280]{1,0:T(8,128)S(1)}, f32[8,1280]{1,0:T(8,128)S(1)}, u32[]{:S(2)}, u32[]{:S(2)}) collective-permute-start(f32[8,1280]{1,0:T(8,128)S(1)} %combine.3.refs_0_), channel_id=1, source_target_pairs={{0,192},{64,0},{128,64},{192,128},{1,193},{65,1},{129,65},{193,129... | collective-permute-start | bytes 122888 | tf_op jit(solution)/shard_map/ppermute | solution.py:21
  34.0 2.7 %collective-permute-start.9 = (f32[8,1280]{1,0:T(8,128)S(1)}, f32[8,1280]{1,0:T(8,128)S(1)}, u32[]{:S(2)}, u32[]{:S(2)}) collective-permute-start(f32[8,1280]{1,0:T(8,128)S(1)} %combine.3.refs_0_), channel_id=1, source_target_pairs={{0,128},{64,192},{128,0},{192,64},{1,129},{65,193},{129,1},{193,65... | collective-permute-start | bytes 122888 | tf_op jit(solution)/shard_map/ppermute | solution.py:21
  36.7 0.0 collective-permute-start.8
  36.7 0.7 %collective-permute-done.10.refs_3_ = f32[8,1280]{1,0:T(8,128)S(1)} collective-permute-done((f32[8,1280]{1,0:T(8,128)S(1)}, f32[8,1280]{1,0:T(8,128)S(1)}, u32[]{:S(2)}, u32[]{:S(2)}) %collective-permute-start.10) | collective-permute-done | bytes 40992 | tf_op jit(solution)/shard_map/ppermute | solution.py:21
  37.5 2.0 %collective-permute-done.9.refs_2_ = f32[8,1280]{1,0:T(8,128)S(1)} collective-permute-done((f32[8,1280]{1,0:T(8,128)S(1)}, f32[8,1280]{1,0:T(8,128)S(1)}, u32[]{:S(2)}, u32[]{:S(2)}) %collective-permute-start.9) | collective-permute-done | bytes 40992 | tf_op jit(solution)/shard_map/ppermute | solution.py:21
  39.5 1.2 %collective-permute-done.8.refs_1_ = f32[8,1280]{1,0:T(8,128)S(1)} collective-permute-done((f32[8,1280]{1,0:T(8,128)S(1)}, f32[8,1280]{1,0:T(8,128)S(1)}, u32[]{:S(2)}, u32[]{:S(2)}) %collective-permute-start.8) | collective-permute-done | bytes 40992 | tf_op jit(solution)/shard_map/ppermute | solution.py:21
  40.7 0.0 copy-done
  40.7 0.0 copy-done.1
  40.7 0.0 copy-done.2
  40.7 0.6 %cov.1 = (f32[80,64]{1,0:T(8,128)S(1)}, f32[80,64]{1,0:T(8,128)S(1)}, f32[80,64]{1,0:T(8,128)S(1)}) custom-call(f32[8,1280]{1,0:T(8,128)S(1)} %combine.3.refs_0_, f32[8,1280]{1,0:T(8,128)S(1)} %collective-permute-done.8.refs_1_, f32[8,1280]{1,0:T(8,128)S(1)} %collective-permute-done.9.refs_2_, f32[8,1280]{1,0:T(8,128)S(1)} %collective-permute-done.10.refs_3_, ...), custom_call_target="tpu_custom_call" | custom-call | tf_op jit(solution)/shard_map/cov/pallas_call | solution.py:377
  41.3 0.1 collective-permute-start.11
  41.4 5.1 %collective-permute-start.12 = (f32[80,64]{1,0:T(8,128)S(1)}, f32[80,64]{1,0:T(8,128)S(1)}, u32[]{:S(2)}, u32[]{:S(2)}) collective-permute-start(f32[80,64]{1,0:T(8,128)S(1)} %get-tuple-element.39), channel_id=1, source_target_pairs={{0,63},{1,0},{2,1},{3,2},{4,3},{5,4},{6,5},{7,6},{8,7},{9,8},{10,9... | collective-permute-start | bytes 61448 | tf_op jit(solution)/shard_map/ppermute | solution.py:21
  46.5 1.7 %collective-permute-done.11.a_ref = f32[80,64]{1,0:T(8,128)S(1)} collective-permute-done((f32[80,64]{1,0:T(8,128)S(1)}, f32[80,64]{1,0:T(8,128)S(1)}, u32[]{:S(2)}, u32[]{:S(2)}) %collective-permute-start.11) | collective-permute-done | bytes 20512 | tf_op jit(solution)/shard_map/ppermute | solution.py:21
  48.2 0.0 collective-permute-done.12.b_ref
  48.2 0.8 %final.1 = (f32[10,8,40]{2,1,0:T(8,128)}, f32[8,10]{1,0:T(8,128)}) custom-call(f32[80,64]{1,0:T(8,128)S(1)} %get-tuple-element.37.mid_ref, f32[80,64]{1,0:T(8,128)S(1)} %collective-permute-done.11.a_ref, f32[80,64]{1,0:T(8,128)S(1)} %collective-permute-done.12.b_ref), custom_call_target="tpu_custom_call" | custom-call | tf_op jit(solution)/shard_map/final/pallas_call | solution.py:387
Async XLA Ops:
  3.3 13.5 %collective-permute-start = (bf16[128,768]{1,0:T(8,128)(2,1)S(1)}, bf16[128,768]{1,0:T(8,128)(2,1)S(1)}, u32[]{:S(2)}, u32[]{:S(2)}) collective-permute-start(bf16[128,768]{1,0:T(8,128)(2,1)S(1)} %get-tuple-element.29), channel_id=1, source_target_pairs={{0,62},{1,63},{2,0},{3,1},{4,2},{5,3},{6,4},{7,5},{8,6},{9,7},{10,... | collective-permute-start | bytes 589832 | tf_op jit(solution)/shard_map/ppermute | solution.py:21
  11.6 6.3 %collective-permute-start.1 = (bf16[128,768]{1,0:T(8,128)(2,1)S(1)}, bf16[128,768]{1,0:T(8,128)(2,1)S(1)}, u32[]{:S(2)}, u32[]{:S(2)}) collective-permute-start(bf16[128,768]{1,0:T(8,128)(2,1)S(1)} %get-tuple-element.30), channel_id=1, source_target_pairs={{0,63},{1,0},{2,1},{3,2},{4,3},{5,4},{6,5},{7,6},{8,7},{9,8},{10,9... | collective-permute-start | bytes 589832 | tf_op jit(solution)/shard_map/ppermute | solution.py:21
  12.7 9.7 %collective-permute-start.4 = (bf16[128,768]{1,0:T(8,128)(2,1)S(1)}, bf16[128,768]{1,0:T(8,128)(2,1)S(1)}, u32[]{:S(2)}, u32[]{:S(2)}) collective-permute-start(bf16[128,768]{1,0:T(8,128)(2,1)S(1)} %get-tuple-element.33), channel_id=1, source_target_pairs={{0,1},{1,2},{2,3},{3,4},{4,5},{5,6},{6,7},{7,8},{8,9},{9,10},{10,1... | collective-permute-start | bytes 589832 | tf_op jit(solution)/shard_map/ppermute | solution.py:21
  13.1 11.1 %collective-permute-start.5 = (bf16[128,768]{1,0:T(8,128)(2,1)S(1)}, bf16[128,768]{1,0:T(8,128)(2,1)S(1)}, u32[]{:S(2)}, u32[]{:S(2)}) collective-permute-start(bf16[128,768]{1,0:T(8,128)(2,1)S(1)} %get-tuple-element.34), channel_id=1, source_target_pairs={{0,2},{1,3},{2,4},{3,5},{4,6},{5,7},{6,8},{7,9},{8,10},{9,11},{10,... | collective-permute-start | bytes 589832 | tf_op jit(solution)/shard_map/ppermute | solution.py:21
  20.4 9.8 %collective-permute-start.2 = (f32[16,768]{1,0:T(8,128)S(1)}, f32[16,768]{1,0:T(8,128)S(1)}, u32[]{:S(2)}, u32[]{:S(2)}) collective-permute-start(f32[16,768]{1,0:T(8,128)S(1)} %get-tuple-element.31), channel_id=1, source_target_pairs={{0,2},{1,3},{2,4},{3,5},{4,6},{5,7},{6,8},{7,9},{8,10},{9,11},{10,... | collective-permute-start | bytes 147464 | tf_op jit(solution)/shard_map/ppermute | solution.py:21
  20.5 9.7 %copy-start.3 = (s32[1024,4]{0,1:T(4,128)S(1)}, s32[1024,4]{0,1:T(4,128)}, u32[]{:S(2)}) copy-start(s32[1024,4]{0,1:T(4,128)} %param.11) | copy-start | bytes 49156
  20.5 9.7 %copy-start.4 = (f32[1024,4]{0,1:T(4,128)S(1)}, f32[1024,4]{0,1:T(4,128)}, u32[]{:S(2)}) copy-start(f32[1024,4]{0,1:T(4,128)} %param.10) | copy-start | bytes 49156
  20.5 9.7 %collective-permute-start.3 = (f32[16,768]{1,0:T(8,128)S(1)}, f32[16,768]{1,0:T(8,128)S(1)}, u32[]{:S(2)}, u32[]{:S(2)}) collective-permute-start(f32[16,768]{1,0:T(8,128)S(1)} %get-tuple-element.32), channel_id=1, source_target_pairs={{0,1},{1,2},{2,3},{3,4},{4,5},{5,6},{6,7},{7,8},{8,9},{9,10},{10,1... | collective-permute-start | bytes 147464 | tf_op jit(solution)/shard_map/ppermute | solution.py:21
  26.7 14.0 %copy-start = (f32[1024]{0:T(1024)S(1)}, f32[1024]{0:T(1024)}, u32[]{:S(2)}) copy-start(f32[1024]{0:T(1024)} %param.13) | copy-start | bytes 12292
  26.7 14.0 %copy-start.1 = (f32[1024]{0:T(1024)S(1)}, f32[1024]{0:T(1024)}, u32[]{:S(2)}) copy-start(f32[1024]{0:T(1024)} %param.14) | copy-start | bytes 12292
  26.7 14.0 %copy-start.2 = (s32[1024]{0:T(1024)S(1)}, s32[1024]{0:T(1024)}, u32[]{:S(2)}) copy-start(s32[1024]{0:T(1024)} %param.15) | copy-start | bytes 12292
  26.7 4.5 %collective-permute-start.6 = (f32[16,768]{1,0:T(8,128)S(1)}, f32[16,768]{1,0:T(8,128)S(1)}, u32[]{:S(2)}, u32[]{:S(2)}) collective-permute-start(f32[16,768]{1,0:T(8,128)S(1)} %get-tuple-element.35), channel_id=1, source_target_pairs={{0,63},{1,0},{2,1},{3,2},{4,3},{5,4},{6,5},{7,6},{8,7},{9,8},{10,9... | collective-permute-start | bytes 147464 | tf_op jit(solution)/shard_map/ppermute | solution.py:21
  28.6 4.1 %collective-permute-start.7 = (f32[16,768]{1,0:T(8,128)S(1)}, f32[16,768]{1,0:T(8,128)S(1)}, u32[]{:S(2)}, u32[]{:S(2)}) collective-permute-start(f32[16,768]{1,0:T(8,128)S(1)} %get-tuple-element.36), channel_id=1, source_target_pairs={{0,62},{1,63},{2,0},{3,1},{4,2},{5,3},{6,4},{7,5},{8,6},{9,7},{10,... | collective-permute-start | bytes 147464 | tf_op jit(solution)/shard_map/ppermute | solution.py:21
  33.4 4.1 %collective-permute-start.10 = (f32[8,1280]{1,0:T(8,128)S(1)}, f32[8,1280]{1,0:T(8,128)S(1)}, u32[]{:S(2)}, u32[]{:S(2)}) collective-permute-start(f32[8,1280]{1,0:T(8,128)S(1)} %combine.3.refs_0_), channel_id=1, source_target_pairs={{0,192},{64,0},{128,64},{192,128},{1,193},{65,1},{129,65},{193,129... | collective-permute-start | bytes 122888 | tf_op jit(solution)/shard_map/ppermute | solution.py:21
  34.0 5.5 %collective-permute-start.9 = (f32[8,1280]{1,0:T(8,128)S(1)}, f32[8,1280]{1,0:T(8,128)S(1)}, u32[]{:S(2)}, u32[]{:S(2)}) collective-permute-start(f32[8,1280]{1,0:T(8,128)S(1)} %combine.3.refs_0_), channel_id=1, source_target_pairs={{0,128},{64,192},{128,0},{192,64},{1,129},{65,193},{129,1},{193,65... | collective-permute-start | bytes 122888 | tf_op jit(solution)/shard_map/ppermute | solution.py:21
  36.7 4.0 %collective-permute-start.8 = (f32[8,1280]{1,0:T(8,128)S(1)}, f32[8,1280]{1,0:T(8,128)S(1)}, u32[]{:S(2)}, u32[]{:S(2)}) collective-permute-start(f32[8,1280]{1,0:T(8,128)S(1)} %combine.3.refs_0_), channel_id=1, source_target_pairs={{0,64},{64,128},{128,192},{192,0},{1,65},{65,129},{129,193},{193,1... | collective-permute-start | bytes 122888 | tf_op jit(solution)/shard_map/ppermute | solution.py:21
  41.3 6.8 %collective-permute-start.11 = (f32[80,64]{1,0:T(8,128)S(1)}, f32[80,64]{1,0:T(8,128)S(1)}, u32[]{:S(2)}, u32[]{:S(2)}) collective-permute-start(f32[80,64]{1,0:T(8,128)S(1)} %get-tuple-element.38), channel_id=1, source_target_pairs={{0,1},{1,2},{2,3},{3,4},{4,5},{5,6},{6,7},{7,8},{8,9},{9,10},{10,1... | collective-permute-start | bytes 61448 | tf_op jit(solution)/shard_map/ppermute | solution.py:21
  41.4 6.7 %collective-permute-start.12 = (f32[80,64]{1,0:T(8,128)S(1)}, f32[80,64]{1,0:T(8,128)S(1)}, u32[]{:S(2)}, u32[]{:S(2)}) collective-permute-start(f32[80,64]{1,0:T(8,128)S(1)} %get-tuple-element.39), channel_id=1, source_target_pairs={{0,63},{1,0},{2,1},{3,2},{4,3},{5,4},{6,5},{7,6},{8,7},{9,8},{10,9... | collective-permute-start | bytes 61448 | tf_op jit(solution)/shard_map/ppermute | solution.py:21

commit v4 on v3

--- a/solution.py
+++ b/solution.py
@@ -6,7 +6,6 @@
 from jax.sharding import PartitionSpec as P
 
 REG_DEV = 8
-HALO_MOVES = (-2, -1, 1, 2)
 TILE = 256
 F32 = jnp.float32
 BF16 = jnp.bfloat16
@@ -19,6 +18,10 @@
 def passed_along(x, axis, by):
     devices = lax.axis_size(axis)
     return lax.ppermute(x, axis, [(i, (i + by) % devices) for i in range(devices)])
+
+
+def swapped(x, axis, mask):
+    return lax.ppermute(x, axis, [(i, i ^ mask) for i in range(lax.axis_size(axis))])
 
 
 def row_stride(cells):
@@ -62,15 +65,9 @@
     return jnp.concatenate([w, extra], axis=0).astype(BF16)
 
 
-def ask_low_kernel(slot_hbm, table_hbm, vw_hbm, state_hbm, inv_ref, vw_ref, table_ref, state_ref, *refs):
+def ask_low_kernel(slot_hbm, table_hbm, vw_hbm, inv_ref, vw_ref, table_ref, *refs):
     *out_refs, slot_ref, sems = refs
-    members, levels, cells = state_hbm.shape
-    pairs = (
-        (slot_hbm, slot_ref),
-        (vw_hbm, vw_ref),
-        (table_hbm, table_ref),
-        (state_hbm, state_ref.at[:, pl.ds(0, levels), :]),
-    )
+    pairs = ((slot_hbm, slot_ref), (vw_hbm, vw_ref), (table_hbm, table_ref))
     copies = [pltpu.make_async_copy(src, dst, sems.at[i]) for i, (src, dst) in enumerate(pairs)]
     for copy in copies:
         copy.start()
@@ -79,9 +76,6 @@
     copies[1].wait()
     copies[2].wait()
     halo_weights(inv_ref, vw_ref, table_ref, out_refs, (0, 1))
-    copies[3].wait()
-    for m in range(members):
-        state_ref[m, levels:, :] = jnp.zeros((state_ref.shape[1] - levels, cells), BF16)
 
 
 def ask_high_kernel(inv_ref, vw_ref, table_ref, own_ref, *out_refs):
@@ -102,41 +96,57 @@
 def answer_tile(cell_of, w, turned_ref, cells_dim):
     S, rest = row_stride(cells_dim), member_row(cells_dim, 8)
     half = TILE // 2
-    lane = lax.broadcasted_iota(jnp.int32, (8, TILE), 1) & (half - 1)
+    lane = lax.broadcasted_iota(jnp.int32, (8, 128), 1)
+    near = lane - (lax.broadcasted_iota(jnp.int32, (8, 128), 0) >> 1)
     wide = lax.broadcasted_iota(jnp.int32, (128, TILE), 1)
     zero = jnp.zeros_like(w)
     rhs = jnp.concatenate([jnp.where(wide < half, w, zero), jnp.where(wide < half, zero, w)], axis=0)
-    first, second = [], []
-    for h in range(2):
-        a_rows, b_rows = [], []
-        for q in range(half // 4):
-            for j in range(4):
-                c = cell_of(h * half + 4 * q + j)
+    parts = []
+    for o in range(half // 8):
+        sides = []
+        for h in range(2):
+            a_rows, b_rows = [], []
+            for j in range(8):
+                c = cell_of(h * half + 8 * o + j)
                 a_rows.append(turned_ref[pl.ds(c, 8, stride=S), :])
                 b_rows.append(turned_ref[pl.ds(c + rest, 2, stride=S), :])
-        first.append(jnp.concatenate(a_rows, axis=0).astype(BF16))
-        second.append(jnp.concatenate(b_rows, axis=0).astype(BF16))
-    lhs_a = jnp.concatenate(first, axis=1)
-    lhs_b = jnp.concatenate(second, axis=1)
-    d_a = jnp.dot(lhs_a, rhs, preferred_element_type=F32)
-    d_b = jnp.dot(lhs_b, rhs, preferred_element_type=F32)
-    out_a = jnp.zeros((8, TILE), F32)
-    for r in range(half):
-        out_a = jnp.where(lane == r, d_a[8 * r : 8 * r + 8, :], out_a)
-    out_b = jnp.zeros((8, TILE), F32)
-    near = lane - (lax.broadcasted_iota(jnp.int32, (8, TILE), 0) >> 1)
-    for q in range(half // 4):
-        out_b = jnp.where(near == 4 * q, d_b[8 * q : 8 * q + 8, :], out_b)
-    return jnp.concatenate([out_a, out_b], axis=0)
-
-
-def own_kernel(state_ref, table_hbm, w_ref, turned_ref, eq_ref, cell_ref, cell_sem):
-    members, levels, cells = state_ref.shape
+            sides.append(jnp.concatenate(a_rows + b_rows, axis=0).astype(BF16))
+        parts.append(jnp.concatenate(sides, axis=1))
+    d = jnp.dot(jnp.concatenate(parts, axis=0), rhs, preferred_element_type=F32)
+    out_a = [jnp.zeros((8, 128), F32)] * 2
+    out_b = [jnp.zeros((8, 128), F32)] * 2
+    for o in range(half // 8):
+        for j in range(8):
+            low = 80 * o + 8 * j
+            hit = lane == 8 * o + j
+            for h in range(2):
+                out_a[h] = jnp.where(hit, d[low : low + 8, h * half : (h + 1) * half], out_a[h])
+        for i in range(2):
+            low = 80 * o + 64 + 8 * i
+            hit = near == 8 * o + 4 * i
+            for h in range(2):
+                out_b[h] = jnp.where(hit, d[low : low + 8, h * half : (h + 1) * half], out_b[h])
+    return jnp.concatenate([jnp.concatenate(out_a, axis=1), jnp.concatenate(out_b, axis=1)], axis=0)
+
+
+def own_kernel(state_hbm, table_hbm, w_ref, turned_ref, eq_ref, state_ref, cell_ref, cell_sem, sems):
+    members, levels, cells = state_hbm.shape
+    for m in range(members):
+        state_ref[m, levels:, :] = jnp.zeros((state_ref.shape[1] - levels, cells), BF16)
+    copies = [
+        pltpu.make_async_copy(
+            state_hbm.at[pl.ds(m, 2)], state_ref.at[pl.ds(m, 2), pl.ds(0, levels), :], sems.at[m // 2]
+        )
+        for m in range(0, members, 2)
+    ]
+    for each in copies:
+        each.start()
     copy = pltpu.make_async_copy(table_hbm.at[:, pl.ds(0, eq_ref.shape[1])], cell_ref, cell_sem)
     copy.start()
     r = lax.broadcasted_iota(jnp.int32, (TILE, TILE), 0)
     eye = jnp.where(r == lax.broadcasted_iota(jnp.int32, (TILE, TILE), 1), 1.0, 0.0).astype(BF16)
     for m in range(0, members, 2):
+        copies[m // 2].wait()
         for part in range(cells // TILE):
             at = slice(part * TILE, (part + 1) * TILE)
             block = jnp.concatenate([state_ref[m, :, at], state_ref[m + 1, :, at]], axis=0)
@@ -277,7 +287,7 @@
     width = d.shape[1]
     i = lax.broadcasted_iota(jnp.int32, (width, members), 0)
     j = lax.broadcasted_iota(jnp.int32, (width, members), 1)
-    block = (lax.axis_index("mem") + 4 - (i >> 4)) & 3
+    block = lax.axis_index("mem") ^ (i >> 4)
     place = jnp.where(((i & 15) < mem_dev) & (block * mem_dev + (i & 15) == j), 1.0, 0.0)
     cov = jnp.dot(d, place, precision=lax.Precision.HIGHEST, preferred_element_type=F32)
     lane = lax.broadcasted_iota(jnp.int32, (regions, mem_dev), 1)
@@ -299,23 +309,22 @@
     params = pltpu.CompilerParams(vmem_limit_bytes=16 * 1024 * 1024)
 
     w_shape = jax.ShapeDtypeStruct((128, halo), BF16)
-    inv, vw_near, table, state_near, ask_m2, ask_m1 = pl.pallas_call(
+    inv, vw_near, table, ask_m2, ask_m1 = pl.pallas_call(
         ask_low_kernel,
         out_shape=[
             pltpu.VMEM((neigh * obs // 128, 128), jnp.int32),
             pltpu.VMEM((levels, obs), BF16),
             pltpu.VMEM((1, neigh * obs), jnp.int32),
-            pltpu.VMEM((mem_dev, 128, cells), BF16),
             w_shape,
             w_shape,
         ],
-        in_specs=[ANY] * 4,
-        out_specs=[VMEM] * 6,
-        scratch_shapes=[pltpu.VMEM((neigh, obs), jnp.int32), pltpu.SemaphoreType.DMA((4,))],
+        in_specs=[ANY] * 3,
+        out_specs=[VMEM] * 5,
+        scratch_shapes=[pltpu.VMEM((neigh, obs), jnp.int32), pltpu.SemaphoreType.DMA((3,))],
         compiler_params=params,
         cost_estimate=pl.CostEstimate(flops=2_000_000_000, bytes_accessed=6_000_000, transcendentals=0),
         name="ask_low",
-    )(far(slot_t), far(request_cell), far(vw_t), far(state_t))
+    )(far(slot_t), far(request_cell), far(vw_t))
     w_m2, w_m1 = passed_along(ask_m2, "cell", -2), passed_along(ask_m1, "cell", -1)
     w_own, ask_p1, ask_p2 = pl.pallas_call(
         ask_high_kernel,
@@ -333,13 +342,18 @@
             pltpu.VMEM((mem_dev * row_stride(cells), 128), F32),
             pltpu.VMEM((16, obs), F32),
         ],
-        in_specs=[VMEM, ANY, VMEM],
+        in_specs=[ANY, ANY, VMEM],
         out_specs=[VMEM] * 2,
-        scratch_shapes=[pltpu.SMEM((1, obs), jnp.int32), pltpu.SemaphoreType.DMA],
+        scratch_shapes=[
+            pltpu.VMEM((mem_dev, 128, cells), BF16),
+            pltpu.SMEM((1, obs), jnp.int32),
+            pltpu.SemaphoreType.DMA,
+            pltpu.SemaphoreType.DMA((mem_dev // 2,)),
+        ],
         compiler_params=params,
         cost_estimate=pl.CostEstimate(flops=8_000_000_000, bytes_accessed=10_000_000, transcendentals=0),
         name="own",
-    )(state_near, far(request_cell), w_own)
+    )(far(state_t), far(request_cell), w_own)
     turned = pltpu.with_memory_space_constraint(turned, pltpu.VMEM)
     answer = pl.pallas_call(
         lambda *refs: answer_kernel(levels, cells, *refs),
@@ -372,7 +386,7 @@
 
     own = combine([(-1, eq_own), (0, eq_m2), (1, eq_m1)])
     own = combine([(2, eq_p1), (3, eq_p2)], own)
-    others = [passed_along(own, "mem", by) for by in (1, 2, 3)]
+    others = [swapped(own, "mem", mask) for mask in (1, 2, 3)]
     wide = 4 * 16
     mid, to_prev, to_next = pl.pallas_call(
         lambda *refs: cov_kernel(members, *refs),

time: 49.2 us -> 48.9 us (level)
  waiting for transfers between devices: 11.8 us -> 8.98 us
  starting transfers between devices: 22 us -> 23.5 us
  Pallas kernels: 14.4 us -> 15.5 us
    ppermute x13 -> x10, waiting for transfers between devices: 11.8 us -> 5.81 us  [passed_along(): lax.ppermute(x, axis, [(i, (i + by) % devices) for i in range(devices)])]
    ppermute x0 -> x3, starting transfers between devices: none -> 4.18 us  [swapped(): lax.ppermute(x, axis, [(i, i ^ mask) for i in range(lax.axis_size(axis))])]
    ppermute x0 -> x3, waiting for transfers between devices: none -> 3.17 us  [swapped(): lax.ppermute(x, axis, [(i, i ^ mask) for i in range(lax.axis_size(axis))])]
    ppermute x13 -> x10, starting transfers between devices: 22 us -> 19.3 us  [passed_along(): lax.ppermute(x, axis, [(i, (i + by) % devices) for i in range(devices)])]
    pallas_call x1, Pallas kernels: 2.85 us -> 4.76 us  [on_device(): pl.pallas_call(own_kernel, out_shape=[pltpu.VMEM((mem_dev * row_stride(ce...]
  transfers between devices with their start and end apart: 13 -> 13, of which waited for: 8 -> 6; matrix products, arithmetic and copies ran while one was open for 0% -> 0% of each run, Pallas kernels for 20% -> 23%
where the time goes in v4:
time: 48.9 us; the launch traced here: 48.8 us
  starting transfers between devices  23.5 us (48%)
  Pallas kernels  15.5 us (32%)
  waiting for transfers between devices  8.98 us (18%)
  between operations  0.79 us (2%)
    ppermute x10, starting transfers between devices, passed_along(): lax.ppermute(x, axis, [(i, (i + by) % devices) for i in range(devices)])  19.3 us
    ppermute x10, waiting for transfers between devices, passed_along(): lax.ppermute(x, axis, [(i, (i + by) % devices) for i in range(devices)])  5.81 us
    pallas_call x1, Pallas kernels, on_device(): pl.pallas_call(own_kernel, out_shape=[pltpu.VMEM((mem_dev * row_stride(ce...  4.76 us
    ppermute x3, starting transfers between devices, swapped(): lax.ppermute(x, axis, [(i, i ^ mask) for i in range(lax.axis_size(axis))])  4.18 us
    ppermute x3, waiting for transfers between devices, swapped(): lax.ppermute(x, axis, [(i, i ^ mask) for i in range(lax.axis_size(axis))])  3.17 us
    pallas_call x1, Pallas kernels, on_device(): pl.pallas_call(ask_low_kernel, out_shape=[pltpu.VMEM((neigh * obs // 128,...  2.31 us
    pallas_call x1, Pallas kernels, on_device(): eq_m2, eq_m1 = answer(turned, w_m2, w_m1)  2.26 us
    pallas_call x1, Pallas kernels, on_device(): eq_p1, eq_p2 = answer(turned, w_p1, w_p2)  2.25 us
  transfers between devices with their start and end apart: 13, of which 6 were waited for; matrix products, arithmetic and copies ran while one was open for 0% of the time, Pallas kernels for 23%

profile of v4, /device:TPU:4, one launch (start us, length us, event | category | flops | bytes accessed | tf_op | source)
XLA Modules:
  0.0 48.8 jit_solution(2465292474487610400)
XLA Ops:
  0.6 2.3 %ask_low.1 = (s32[32,128]{1,0:T(8,128)S(1)}, bf16[120,1024]{1,0:T(8,128)(2,1)S(1)}, s32[1,4096]{1,0:T(1,128)S(1)}, bf16[128,768]{1,0:T(8,128)(2,1)S(1)}, bf16[128,768]{1,0:T(8,128)(2,1)S(1)}) custom-call(s32[4,1024]{1,0:T(4,128)} %bitcast.11, s32[1,4096]{1,0:T(1,128)} %table_hbm.3, bf16[120,1024]{1,0:T(8,128)(2,1)} %bitcast.17), custom_call_target="tpu_custom_call" | custom-call | flops 2000000000 | bytes 6000000 | tf_op jit(solution)/shard_map/ask_low/pallas_call | solution.py:312
  2.9 8.4 %collective-permute-start = (bf16[128,768]{1,0:T(8,128)(2,1)S(1)}, bf16[128,768]{1,0:T(8,128)(2,1)S(1)}, u32[]{:S(2)}, u32[]{:S(2)}) collective-permute-start(bf16[128,768]{1,0:T(8,128)(2,1)S(1)} %get-tuple-element.27), channel_id=1, source_target_pairs={{0,62},{1,63},{2,0},{3,1},{4,2},{5,3},{6,4},{7,5},{8,6},{9,7},{10,... | collective-permute-start | bytes 589832 | tf_op jit(solution)/shard_map/ppermute | solution.py:20
  11.3 0.2 collective-permute-start.1
  11.5 0.9 %ask_high.1 = (bf16[128,1024]{1,0:T(8,128)(2,1)S(1)}, bf16[128,768]{1,0:T(8,128)(2,1)S(1)}, bf16[128,768]{1,0:T(8,128)(2,1)S(1)}) custom-call(s32[32,128]{1,0:T(8,128)S(1)} %get-tuple-element.21.inv_ref, bf16[120,1024]{1,0:T(8,128)(2,1)S(1)} %get-tuple-element.22.vw_ref, s32[1,4096]{1,0:T(1,128)S(1)} %get-tuple-element.23.table_ref), custom_call_target="tpu_custom_call" | custom-call | flops 2000000000 | bytes 1000000 | tf_op jit(solution)/shard_map/ask_high/pallas_call | solution.py:329
  12.4 0.4 collective-permute-start.4
  12.8 0.8 %collective-permute-start.5 = (bf16[128,768]{1,0:T(8,128)(2,1)S(1)}, bf16[128,768]{1,0:T(8,128)(2,1)S(1)}, u32[]{:S(2)}, u32[]{:S(2)}) collective-permute-start(bf16[128,768]{1,0:T(8,128)(2,1)S(1)} %get-tuple-element.32), channel_id=1, source_target_pairs={{0,2},{1,3},{2,4},{3,5},{4,6},{5,7},{6,8},{7,9},{8,10},{9,11},{10,... | collective-permute-start | bytes 589832 | tf_op jit(solution)/shard_map/ppermute | solution.py:20
  13.6 4.8 %own.1 = (f32[20520,128]{1,0:T(8,128)S(1)}, f32[16,1024]{1,0:T(8,128)S(1)}) custom-call(bf16[10,120,2048]{2,1,0:T(8,128)(2,1)} %bitcast.16, s32[1,4096]{1,0:T(1,128)} %table_hbm.3, bf16[128,1024]{1,0:T(8,128)(2,1)S(1)} %get-tuple-element.24.w_ref), custom_call_target="tpu_custom_call" | custom-call | flops 8000000000 | bytes 10000000 | tf_op jit(solution)/shard_map/own/pallas_call | solution.py:339
  18.3 0.0 collective-permute-done.refs_1_
  18.4 0.0 collective-permute-done.1.refs_2_
  18.4 2.3 %answer.2 = (f32[16,768]{1,0:T(8,128)S(1)}, f32[16,768]{1,0:T(8,128)S(1)}) custom-call(f32[20520,128]{1,0:T(8,128)S(1)} %get-tuple-element.26.refs_0_, bf16[128,768]{1,0:T(8,128)(2,1)S(1)} %collective-permute-done.refs_1_, bf16[128,768]{1,0:T(8,128)(2,1)S(1)} %collective-permute-done.1.refs_2_), custom_call_target="tpu_custom_call" | custom-call | flops 4000000000 | bytes 1000000 | tf_op jit(solution)/shard_map/answer/pallas_call | solution.py:370
  20.6 0.0 copy-start.3
  20.6 0.0 copy-start.4
  20.7 0.1 collective-permute-start.2
  20.7 0.0 copy-start
  20.8 0.0 copy-start.1
  20.8 0.0 copy-start.2
  20.8 0.3 collective-permute-start.3
  21.1 1.0 %collective-permute-done.4.refs_1_ = bf16[128,768]{1,0:T(8,128)(2,1)S(1)} collective-permute-done((bf16[128,768]{1,0:T(8,128)(2,1)S(1)}, bf16[128,768]{1,0:T(8,128)(2,1)S(1)}, u32[]{:S(2)}, u32[]{:S(2)}) %collective-permute-start.4) | collective-permute-done | bytes 196640 | tf_op jit(solution)/shard_map/ppermute | solution.py:20
  22.1 1.8 %collective-permute-done.5.refs_2_ = bf16[128,768]{1,0:T(8,128)(2,1)S(1)} collective-permute-done((bf16[128,768]{1,0:T(8,128)(2,1)S(1)}, bf16[128,768]{1,0:T(8,128)(2,1)S(1)}, u32[]{:S(2)}, u32[]{:S(2)}) %collective-permute-start.5) | collective-permute-done | bytes 196640 | tf_op jit(solution)/shard_map/ppermute | solution.py:20
  23.9 2.2 %answer.3 = (f32[16,768]{1,0:T(8,128)S(1)}, f32[16,768]{1,0:T(8,128)S(1)}) custom-call(f32[20520,128]{1,0:T(8,128)S(1)} %get-tuple-element.26.refs_0_, bf16[128,768]{1,0:T(8,128)(2,1)S(1)} %collective-permute-done.4.refs_1_, bf16[128,768]{1,0:T(8,128)(2,1)S(1)} %collective-permute-done.5.refs_2_), custom_call_target="tpu_custom_call" | custom-call | flops 4000000000 | bytes 1000000 | tf_op jit(solution)/shard_map/answer/pallas_call | solution.py:372
  26.2 2.3 %collective-permute-start.6 = (f32[16,768]{1,0:T(8,128)S(1)}, f32[16,768]{1,0:T(8,128)S(1)}, u32[]{:S(2)}, u32[]{:S(2)}) collective-permute-start(f32[16,768]{1,0:T(8,128)S(1)} %get-tuple-element.33), channel_id=1, source_target_pairs={{0,63},{1,0},{2,1},{3,2},{4,3},{5,4},{6,5},{7,6},{8,7},{9,8},{10,9... | collective-permute-start | bytes 147464 | tf_op jit(solution)/shard_map/ppermute | solution.py:20
  28.4 1.7 %collective-permute-start.7 = (f32[16,768]{1,0:T(8,128)S(1)}, f32[16,768]{1,0:T(8,128)S(1)}, u32[]{:S(2)}, u32[]{:S(2)}) collective-permute-start(f32[16,768]{1,0:T(8,128)S(1)} %get-tuple-element.34), channel_id=1, source_target_pairs={{0,62},{1,63},{2,0},{3,1},{4,2},{5,3},{6,4},{7,5},{8,6},{9,7},{10,... | collective-permute-start | bytes 147464 | tf_op jit(solution)/shard_map/ppermute | solution.py:20
  30.2 0.0 collective-permute-done.2.refs_3_
  30.2 0.0 collective-permute-done.3.refs_4_
  30.2 0.0 copy-done.3
  30.2 0.0 copy-done.4
  30.2 1.0 %combine.2.refs_2_ = f32[8,1280]{1,0:T(8,128)S(1)} custom-call(s32[4,1024]{1,0:T(4,128)S(1)} %bitcast.12, f32[4,1024]{1,0:T(4,128)S(1)} %bitcast.14, f32[16,1024]{1,0:T(8,128)S(1)} %get-tuple-element.25.refs_2_, f32[16,768]{1,0:T(8,128)S(1)} %collective-permute-done.2.refs_3_, f32[16,768]{1,0:T(8,128)S(1)} %collective-permute-done.3.refs_4_), custom_call_target="tpu_custom_call" | custom-call | flops 1000000000 | bytes 1000000 | tf_op jit(solution)/shard_map/combine/pallas_call | solution.py:377
  31.2 0.0 collective-permute-done.6.refs_3_
  31.2 1.3 %collective-permute-done.7.refs_4_ = f32[16,768]{1,0:T(8,128)S(1)} collective-permute-done((f32[16,768]{1,0:T(8,128)S(1)}, f32[16,768]{1,0:T(8,128)S(1)}, u32[]{:S(2)}, u32[]{:S(2)}) %collective-permute-start.7) | collective-permute-done | bytes 49184 | tf_op jit(solution)/shard_map/ppermute | solution.py:20
  32.5 0.7 %combine.3.refs_0_ = f32[8,1280]{1,0:T(8,128)S(1)} custom-call(s32[4,1024]{1,0:T(4,128)S(1)} %bitcast.13, f32[4,1024]{1,0:T(4,128)S(1)} %bitcast.15, f32[8,1280]{1,0:T(8,128)S(1)} %combine.2.refs_2_, f32[16,768]{1,0:T(8,128)S(1)} %collective-permute-done.6.refs_3_, f32[16,768]{1,0:T(8,128)S(1)} %collective-permute-done.7.refs_4_), custom_call_target="tpu_custom_call" | custom-call | flops 1000000000 | bytes 1000000 | tf_op jit(solution)/shard_map/combine/pallas_call | solution.py:377
  33.2 0.6 %collective-permute-start.10 = (f32[8,1280]{1,0:T(8,128)S(1)}, f32[8,1280]{1,0:T(8,128)S(1)}, u32[]{:S(2)}, u32[]{:S(2)}) collective-permute-start(f32[8,1280]{1,0:T(8,128)S(1)} %combine.3.refs_0_), channel_id=1, source_target_pairs={{0,192},{64,128},{128,64},{192,0},{1,193},{65,129},{129,65},{193,1... | collective-permute-start | bytes 122888 | tf_op jit(solution)/shard_map/ppermute | solution.py:24
  33.8 2.7 %collective-permute-start.9 = (f32[8,1280]{1,0:T(8,128)S(1)}, f32[8,1280]{1,0:T(8,128)S(1)}, u32[]{:S(2)}, u32[]{:S(2)}) collective-permute-start(f32[8,1280]{1,0:T(8,128)S(1)} %combine.3.refs_0_), channel_id=1, source_target_pairs={{0,128},{64,192},{128,0},{192,64},{1,129},{65,193},{129,1},{193,65... | collective-permute-start | bytes 122888 | tf_op jit(solution)/shard_map/ppermute | solution.py:24
  36.6 0.8 %collective-permute-start.8 = (f32[8,1280]{1,0:T(8,128)S(1)}, f32[8,1280]{1,0:T(8,128)S(1)}, u32[]{:S(2)}, u32[]{:S(2)}) collective-permute-start(f32[8,1280]{1,0:T(8,128)S(1)} %combine.3.refs_0_), channel_id=1, source_target_pairs={{0,64},{64,0},{128,192},{192,128},{1,65},{65,1},{129,193},{193,129... | collective-permute-start | bytes 122888 | tf_op jit(solution)/shard_map/ppermute | solution.py:24
  37.4 0.0 collective-permute-done.10.refs_3_
  37.4 1.9 %collective-permute-done.9.refs_2_ = f32[8,1280]{1,0:T(8,128)S(1)} collective-permute-done((f32[8,1280]{1,0:T(8,128)S(1)}, f32[8,1280]{1,0:T(8,128)S(1)}, u32[]{:S(2)}, u32[]{:S(2)}) %collective-permute-start.9) | collective-permute-done | bytes 40992 | tf_op jit(solution)/shard_map/ppermute | solution.py:24
  39.4 1.2 %collective-permute-done.8.refs_1_ = f32[8,1280]{1,0:T(8,128)S(1)} collective-permute-done((f32[8,1280]{1,0:T(8,128)S(1)}, f32[8,1280]{1,0:T(8,128)S(1)}, u32[]{:S(2)}, u32[]{:S(2)}) %collective-permute-start.8) | collective-permute-done | bytes 40992 | tf_op jit(solution)/shard_map/ppermute | solution.py:24
  40.6 0.0 copy-done
  40.6 0.0 copy-done.1
  40.6 0.0 copy-done.2
  40.6 0.6 %cov.1 = (f32[80,64]{1,0:T(8,128)S(1)}, f32[80,64]{1,0:T(8,128)S(1)}, f32[80,64]{1,0:T(8,128)S(1)}) custom-call(f32[8,1280]{1,0:T(8,128)S(1)} %combine.3.refs_0_, f32[8,1280]{1,0:T(8,128)S(1)} %collective-permute-done.8.refs_1_, f32[8,1280]{1,0:T(8,128)S(1)} %collective-permute-done.9.refs_2_, f32[8,1280]{1,0:T(8,128)S(1)} %collective-permute-done.10.refs_3_, ...), custom_call_target="tpu_custom_call" | custom-call | tf_op jit(solution)/shard_map/cov/pallas_call | solution.py:391
  41.2 0.1 collective-permute-start.11
  41.3 5.1 %collective-permute-start.12 = (f32[80,64]{1,0:T(8,128)S(1)}, f32[80,64]{1,0:T(8,128)S(1)}, u32[]{:S(2)}, u32[]{:S(2)}) collective-permute-start(f32[80,64]{1,0:T(8,128)S(1)} %get-tuple-element.37), channel_id=1, source_target_pairs={{0,63},{1,0},{2,1},{3,2},{4,3},{5,4},{6,5},{7,6},{8,7},{9,8},{10,9... | collective-permute-start | bytes 61448 | tf_op jit(solution)/shard_map/ppermute | solution.py:20
  46.3 1.7 %collective-permute-done.11.a_ref = f32[80,64]{1,0:T(8,128)S(1)} collective-permute-done((f32[80,64]{1,0:T(8,128)S(1)}, f32[80,64]{1,0:T(8,128)S(1)}, u32[]{:S(2)}, u32[]{:S(2)}) %collective-permute-start.11) | collective-permute-done | bytes 20512 | tf_op jit(solution)/shard_map/ppermute | solution.py:20
  48.0 0.0 collective-permute-done.12.b_ref
  48.0 0.8 %final.1 = (f32[10,8,40]{2,1,0:T(8,128)}, f32[8,10]{1,0:T(8,128)}) custom-call(f32[80,64]{1,0:T(8,128)S(1)} %get-tuple-element.35.mid_ref, f32[80,64]{1,0:T(8,128)S(1)} %collective-permute-done.11.a_ref, f32[80,64]{1,0:T(8,128)S(1)} %collective-permute-done.12.b_ref), custom_call_target="tpu_custom_call" | custom-call | tf_op jit(solution)/shard_map/final/pallas_call | solution.py:401
Async XLA Ops:
  2.9 15.4 %collective-permute-start = (bf16[128,768]{1,0:T(8,128)(2,1)S(1)}, bf16[128,768]{1,0:T(8,128)(2,1)S(1)}, u32[]{:S(2)}, u32[]{:S(2)}) collective-permute-start(bf16[128,768]{1,0:T(8,128)(2,1)S(1)} %get-tuple-element.27), channel_id=1, source_target_pairs={{0,62},{1,63},{2,0},{3,1},{4,2},{5,3},{6,4},{7,5},{8,6},{9,7},{10,... | collective-permute-start | bytes 589832 | tf_op jit(solution)/shard_map/ppermute | solution.py:20
  11.3 7.0 %collective-permute-start.1 = (bf16[128,768]{1,0:T(8,128)(2,1)S(1)}, bf16[128,768]{1,0:T(8,128)(2,1)S(1)}, u32[]{:S(2)}, u32[]{:S(2)}) collective-permute-start(bf16[128,768]{1,0:T(8,128)(2,1)S(1)} %get-tuple-element.28), channel_id=1, source_target_pairs={{0,63},{1,0},{2,1},{3,2},{4,3},{5,4},{6,5},{7,6},{8,7},{9,8},{10,9... | collective-permute-start | bytes 589832 | tf_op jit(solution)/shard_map/ppermute | solution.py:20
  12.4 9.7 %collective-permute-start.4 = (bf16[128,768]{1,0:T(8,128)(2,1)S(1)}, bf16[128,768]{1,0:T(8,128)(2,1)S(1)}, u32[]{:S(2)}, u32[]{:S(2)}) collective-permute-start(bf16[128,768]{1,0:T(8,128)(2,1)S(1)} %get-tuple-element.31), channel_id=1, source_target_pairs={{0,1},{1,2},{2,3},{3,4},{4,5},{5,6},{6,7},{7,8},{8,9},{9,10},{10,1... | collective-permute-start | bytes 589832 | tf_op jit(solution)/shard_map/ppermute | solution.py:20
  12.8 11.1 %collective-permute-start.5 = (bf16[128,768]{1,0:T(8,128)(2,1)S(1)}, bf16[128,768]{1,0:T(8,128)(2,1)S(1)}, u32[]{:S(2)}, u32[]{:S(2)}) collective-permute-start(bf16[128,768]{1,0:T(8,128)(2,1)S(1)} %get-tuple-element.32), channel_id=1, source_target_pairs={{0,2},{1,3},{2,4},{3,5},{4,6},{5,7},{6,8},{7,9},{8,10},{9,11},{10,... | collective-permute-start | bytes 589832 | tf_op jit(solution)/shard_map/ppermute | solution.py:20
  20.6 9.5 %copy-start.3 = (s32[1024,4]{0,1:T(4,128)S(1)}, s32[1024,4]{0,1:T(4,128)}, u32[]{:S(2)}) copy-start(s32[1024,4]{0,1:T(4,128)} %param.11) | copy-start | bytes 49156
  20.6 9.5 %copy-start.4 = (f32[1024,4]{0,1:T(4,128)S(1)}, f32[1024,4]{0,1:T(4,128)}, u32[]{:S(2)}) copy-start(f32[1024,4]{0,1:T(4,128)} %param.10) | copy-start | bytes 49156
  20.7 9.5 %collective-permute-start.2 = (f32[16,768]{1,0:T(8,128)S(1)}, f32[16,768]{1,0:T(8,128)S(1)}, u32[]{:S(2)}, u32[]{:S(2)}) collective-permute-start(f32[16,768]{1,0:T(8,128)S(1)} %get-tuple-element.29), channel_id=1, source_target_pairs={{0,2},{1,3},{2,4},{3,5},{4,6},{5,7},{6,8},{7,9},{8,10},{9,11},{10,... | collective-permute-start | bytes 147464 | tf_op jit(solution)/shard_map/ppermute | solution.py:20
  20.7 19.8 %copy-start = (f32[1024]{0:T(1024)S(1)}, f32[1024]{0:T(1024)}, u32[]{:S(2)}) copy-start(f32[1024]{0:T(1024)} %param.13) | copy-start | bytes 12292
  20.8 19.8 %copy-start.1 = (f32[1024]{0:T(1024)S(1)}, f32[1024]{0:T(1024)}, u32[]{:S(2)}) copy-start(f32[1024]{0:T(1024)} %param.14) | copy-start | bytes 12292
  20.8 19.8 %copy-start.2 = (s32[1024]{0:T(1024)S(1)}, s32[1024]{0:T(1024)}, u32[]{:S(2)}) copy-start(s32[1024]{0:T(1024)} %param.15) | copy-start | bytes 12292
  20.8 9.4 %collective-permute-start.3 = (f32[16,768]{1,0:T(8,128)S(1)}, f32[16,768]{1,0:T(8,128)S(1)}, u32[]{:S(2)}, u32[]{:S(2)}) collective-permute-start(f32[16,768]{1,0:T(8,128)S(1)} %get-tuple-element.30), channel_id=1, source_target_pairs={{0,1},{1,2},{2,3},{3,4},{4,5},{5,6},{6,7},{7,8},{8,9},{9,10},{10,1... | collective-permute-start | bytes 147464 | tf_op jit(solution)/shard_map/ppermute | solution.py:20
  26.2 5.0 %collective-permute-start.6 = (f32[16,768]{1,0:T(8,128)S(1)}, f32[16,768]{1,0:T(8,128)S(1)}, u32[]{:S(2)}, u32[]{:S(2)}) collective-permute-start(f32[16,768]{1,0:T(8,128)S(1)} %get-tuple-element.33), channel_id=1, source_target_pairs={{0,63},{1,0},{2,1},{3,2},{4,3},{5,4},{6,5},{7,6},{8,7},{9,8},{10,9... | collective-permute-start | bytes 147464 | tf_op jit(solution)/shard_map/ppermute | solution.py:20
  28.4 4.1 %collective-permute-start.7 = (f32[16,768]{1,0:T(8,128)S(1)}, f32[16,768]{1,0:T(8,128)S(1)}, u32[]{:S(2)}, u32[]{:S(2)}) collective-permute-start(f32[16,768]{1,0:T(8,128)S(1)} %get-tuple-element.34), channel_id=1, source_target_pairs={{0,62},{1,63},{2,0},{3,1},{4,2},{5,3},{6,4},{7,5},{8,6},{9,7},{10,... | collective-permute-start | bytes 147464 | tf_op jit(solution)/shard_map/ppermute | solution.py:20
  33.2 4.2 %collective-permute-start.10 = (f32[8,1280]{1,0:T(8,128)S(1)}, f32[8,1280]{1,0:T(8,128)S(1)}, u32[]{:S(2)}, u32[]{:S(2)}) collective-permute-start(f32[8,1280]{1,0:T(8,128)S(1)} %combine.3.refs_0_), channel_id=1, source_target_pairs={{0,192},{64,128},{128,64},{192,0},{1,193},{65,129},{129,65},{193,1... | collective-permute-start | bytes 122888 | tf_op jit(solution)/shard_map/ppermute | solution.py:24
  33.8 5.5 %collective-permute-start.9 = (f32[8,1280]{1,0:T(8,128)S(1)}, f32[8,1280]{1,0:T(8,128)S(1)}, u32[]{:S(2)}, u32[]{:S(2)}) collective-permute-start(f32[8,1280]{1,0:T(8,128)S(1)} %combine.3.refs_0_), channel_id=1, source_target_pairs={{0,128},{64,192},{128,0},{192,64},{1,129},{65,193},{129,1},{193,65... | collective-permute-start | bytes 122888 | tf_op jit(solution)/shard_map/ppermute | solution.py:24
  36.6 4.0 %collective-permute-start.8 = (f32[8,1280]{1,0:T(8,128)S(1)}, f32[8,1280]{1,0:T(8,128)S(1)}, u32[]{:S(2)}, u32[]{:S(2)}) collective-permute-start(f32[8,1280]{1,0:T(8,128)S(1)} %combine.3.refs_0_), channel_id=1, source_target_pairs={{0,64},{64,0},{128,192},{192,128},{1,65},{65,1},{129,193},{193,129... | collective-permute-start | bytes 122888 | tf_op jit(solution)/shard_map/ppermute | solution.py:24
  41.2 6.8 %collective-permute-start.11 = (f32[80,64]{1,0:T(8,128)S(1)}, f32[80,64]{1,0:T(8,128)S(1)}, u32[]{:S(2)}, u32[]{:S(2)}) collective-permute-start(f32[80,64]{1,0:T(8,128)S(1)} %get-tuple-element.36), channel_id=1, source_target_pairs={{0,1},{1,2},{2,3},{3,4},{4,5},{5,6},{6,7},{7,8},{8,9},{9,10},{10,1... | collective-permute-start | bytes 61448 | tf_op jit(solution)/shard_map/ppermute | solution.py:20
  41.3 6.7 %collective-permute-start.12 = (f32[80,64]{1,0:T(8,128)S(1)}, f32[80,64]{1,0:T(8,128)S(1)}, u32[]{:S(2)}, u32[]{:S(2)}) collective-permute-start(f32[80,64]{1,0:T(8,128)S(1)} %get-tuple-element.37), channel_id=1, source_target_pairs={{0,63},{1,0},{2,1},{3,2},{4,3},{5,4},{6,5},{7,6},{8,7},{9,8},{10,9... | collective-permute-start | bytes 61448 | tf_op jit(solution)/shard_map/ppermute | solution.py:20

commit v5 on v4

--- a/solution.py
+++ b/solution.py
@@ -65,9 +65,14 @@
     return jnp.concatenate([w, extra], axis=0).astype(BF16)
 
 
-def ask_low_kernel(slot_hbm, table_hbm, vw_hbm, inv_ref, vw_ref, table_ref, *refs):
+def ask_low_kernel(slot_hbm, table_hbm, vw_hbm, state_hbm, inv_ref, vw_ref, table_ref, state_ref, *refs):
     *out_refs, slot_ref, sems = refs
-    pairs = ((slot_hbm, slot_ref), (vw_hbm, vw_ref), (table_hbm, table_ref))
+    members, levels, cells = state_hbm.shape
+    pairs = [(slot_hbm, slot_ref), (vw_hbm, vw_ref), (table_hbm, table_ref)]
+    for m in range(0, members, 2):
+        pairs.append((state_hbm.at[pl.ds(m, 2)], state_ref.at[pl.ds(m, 2), pl.ds(0, levels), :]))
+    for m in range(members):
+        state_ref[m, levels:, :] = jnp.zeros((state_ref.shape[1] - levels, cells), BF16)
     copies = [pltpu.make_async_copy(src, dst, sems.at[i]) for i, (src, dst) in enumerate(pairs)]
     for copy in copies:
         copy.start()
@@ -76,6 +81,8 @@
     copies[1].wait()
     copies[2].wait()
     halo_weights(inv_ref, vw_ref, table_ref, out_refs, (0, 1))
+    for copy in copies[3:]:
+        copy.wait()
 
 
 def ask_high_kernel(inv_ref, vw_ref, table_ref, own_ref, *out_refs):
@@ -129,24 +136,13 @@
     return jnp.concatenate([jnp.concatenate(out_a, axis=1), jnp.concatenate(out_b, axis=1)], axis=0)
 
 
-def own_kernel(state_hbm, table_hbm, w_ref, turned_ref, eq_ref, state_ref, cell_ref, cell_sem, sems):
-    members, levels, cells = state_hbm.shape
-    for m in range(members):
-        state_ref[m, levels:, :] = jnp.zeros((state_ref.shape[1] - levels, cells), BF16)
-    copies = [
-        pltpu.make_async_copy(
-            state_hbm.at[pl.ds(m, 2)], state_ref.at[pl.ds(m, 2), pl.ds(0, levels), :], sems.at[m // 2]
-        )
-        for m in range(0, members, 2)
-    ]
-    for each in copies:
-        each.start()
+def own_kernel(state_ref, table_hbm, w_ref, turned_ref, eq_ref, cell_ref, cell_sem):
+    members, levels, cells = state_ref.shape
     copy = pltpu.make_async_copy(table_hbm.at[:, pl.ds(0, eq_ref.shape[1])], cell_ref, cell_sem)
     copy.start()
     r = lax.broadcasted_iota(jnp.int32, (TILE, TILE), 0)
     eye = jnp.where(r == lax.broadcasted_iota(jnp.int32, (TILE, TILE), 1), 1.0, 0.0).astype(BF16)
     for m in range(0, members, 2):
-        copies[m // 2].wait()
         for part in range(cells // TILE):
             at = slice(part * TILE, (part + 1) * TILE)
             block = jnp.concatenate([state_ref[m, :, at], state_ref[m + 1, :, at]], axis=0)
@@ -160,26 +156,19 @@
         eq_ref[:, at] = answer_tile(lambda i: cell_ref[0, tile * TILE + i], w_ref[:, at], turned_ref, cells)
 
 
-def answer_kernel(levels, cells, turned_ref, *refs):
-    count = len(refs) // 4
-    w_refs, eq_refs = refs[:count], refs[count : 2 * count]
-    words, scalars, sems = refs[2 * count : 3 * count], refs[3 * count : 4 * count], refs[-1]
-    copies = []
-    for i in range(count):
-        tail = w_refs[i][112:128, :].astype(F32)
-        row = levels - 112
-        words[i][...] = (8.0 * tail[row : row + 1, :] + tail[row + 1 : row + 2, :]).astype(jnp.int32)
-        copies.append(pltpu.make_async_copy(words[i], scalars[i], sems.at[i]))
-        copies[-1].start()
+def answer_kernel(levels, cells, turned_ref, w_ref, before_ref, eq_ref, words, scalars, sem):
+    tail = w_ref[112:128, :].astype(F32)
+    row = levels - 112
+    words[...] = (8.0 * tail[row : row + 1, :] + tail[row + 1 : row + 2, :]).astype(jnp.int32)
+    copy = pltpu.make_async_copy(words, scalars, sem)
+    copy.start()
     keep = lax.broadcasted_iota(jnp.int32, (128, TILE), 0) < levels
-    for copy in copies:
-        copy.wait()
-    for i in range(count):
-        for tile in range(eq_refs[i].shape[1] // TILE):
-            at = slice(tile * TILE, (tile + 1) * TILE)
-            w = w_refs[i][:, at]
-            w = jnp.where(keep, w, jnp.zeros_like(w))
-            eq_refs[i][:, at] = answer_tile(lambda j: scalars[i][0, tile * TILE + j], w, turned_ref, cells)
+    copy.wait()
+    for tile in range(eq_ref.shape[1] // TILE):
+        at = slice(tile * TILE, (tile + 1) * TILE)
+        w = w_ref[:, at]
+        w = jnp.where(keep, w, jnp.zeros_like(w))
+        eq_ref[:, at] = answer_tile(lambda j: scalars[0, tile * TILE + j], w, turned_ref, cells)
 
 
 def combine_kernel(firsts, slot_ref, hw_ref, *refs):
@@ -309,22 +298,23 @@
     params = pltpu.CompilerParams(vmem_limit_bytes=16 * 1024 * 1024)
 
     w_shape = jax.ShapeDtypeStruct((128, halo), BF16)
-    inv, vw_near, table, ask_m2, ask_m1 = pl.pallas_call(
+    inv, vw_near, table, state_near, ask_m2, ask_m1 = pl.pallas_call(
         ask_low_kernel,
         out_shape=[
             pltpu.VMEM((neigh * obs // 128, 128), jnp.int32),
             pltpu.VMEM((levels, obs), BF16),
             pltpu.VMEM((1, neigh * obs), jnp.int32),
+            pltpu.VMEM((mem_dev, 128, cells), BF16),
             w_shape,
             w_shape,
         ],
-        in_specs=[ANY] * 3,
-        out_specs=[VMEM] * 5,
-        scratch_shapes=[pltpu.VMEM((neigh, obs), jnp.int32), pltpu.SemaphoreType.DMA((3,))],
+        in_specs=[ANY] * 4,
+        out_specs=[VMEM] * 6,
+        scratch_shapes=[pltpu.VMEM((neigh, obs), jnp.int32), pltpu.SemaphoreType.DMA((3 + mem_dev // 2,))],
         compiler_params=params,
         cost_estimate=pl.CostEstimate(flops=2_000_000_000, bytes_accessed=6_000_000, transcendentals=0),
         name="ask_low",
-    )(far(slot_t), far(request_cell), far(vw_t))
+    )(far(slot_t), far(request_cell), far(vw_t), far(state_t))
     w_m2, w_m1 = passed_along(ask_m2, "cell", -2), passed_along(ask_m1, "cell", -1)
     w_own, ask_p1, ask_p2 = pl.pallas_call(
         ask_high_kernel,
@@ -342,35 +332,36 @@
             pltpu.VMEM((mem_dev * row_stride(cells), 128), F32),
             pltpu.VMEM((16, obs), F32),
         ],
-        in_specs=[ANY, ANY, VMEM],
+        in_specs=[VMEM, ANY, VMEM],
         out_specs=[VMEM] * 2,
-        scratch_shapes=[
-            pltpu.VMEM((mem_dev, 128, cells), BF16),
-            pltpu.SMEM((1, obs), jnp.int32),
-            pltpu.SemaphoreType.DMA,
-            pltpu.SemaphoreType.DMA((mem_dev // 2,)),
-        ],
+        scratch_shapes=[pltpu.SMEM((1, obs), jnp.int32), pltpu.SemaphoreType.DMA],
         compiler_params=params,
         cost_estimate=pl.CostEstimate(flops=8_000_000_000, bytes_accessed=10_000_000, transcendentals=0),
         name="own",
-    )(far(state_t), far(request_cell), w_own)
+    )(state_near, far(request_cell), w_own)
     turned = pltpu.with_memory_space_constraint(turned, pltpu.VMEM)
     answer = pl.pallas_call(
         lambda *refs: answer_kernel(levels, cells, *refs),
-        out_shape=[jax.ShapeDtypeStruct((16, halo), F32)] * 2,
+        out_shape=pltpu.VMEM((16, halo), F32),
         in_specs=[VMEM] * 3,
-        out_specs=[VMEM] * 2,
-        scratch_shapes=[pltpu.VMEM((1, halo), jnp.int32)] * 2
-        + [pltpu.SMEM((1, halo), jnp.int32)] * 2
-        + [pltpu.SemaphoreType.DMA((2,))],
-        compiler_params=params,
-        cost_estimate=pl.CostEstimate(flops=4_000_000_000, bytes_accessed=1_000_000, transcendentals=0),
+        out_specs=VMEM,
+        scratch_shapes=[
+            pltpu.VMEM((1, halo), jnp.int32),
+            pltpu.SMEM((1, halo), jnp.int32),
+            pltpu.SemaphoreType.DMA,
+        ],
+        compiler_params=params,
+        cost_estimate=pl.CostEstimate(flops=2_000_000_000, bytes_accessed=1_000_000, transcendentals=0),
         name="answer",
     )
-    eq_m2, eq_m1 = answer(turned, w_m2, w_m1)
-    eq_m2, eq_m1 = passed_along(eq_m2, "cell", 2), passed_along(eq_m1, "cell", 1)
-    eq_p1, eq_p2 = answer(turned, w_p1, w_p2)
-    eq_p1, eq_p2 = passed_along(eq_p1, "cell", -1), passed_along(eq_p2, "cell", -2)
+    sent_m2 = answer(turned, w_m2, eq_own)
+    eq_m2 = passed_along(sent_m2, "cell", 2)
+    sent_m1 = answer(turned, w_m1, sent_m2)
+    eq_m1 = passed_along(sent_m1, "cell", 1)
+    sent_p1 = answer(turned, w_p1, sent_m1)
+    eq_p1 = passed_along(sent_p1, "cell", -1)
+    sent_p2 = answer(turned, w_p2, sent_p1)
+    eq_p2 = passed_along(sent_p2, "cell", -2)
 
     def combine(tables, *before):
         firsts = [obs // 128 + n * halo // 128 if n >= 0 else 0 for n, _ in tables]

time: 48.9 us -> 48.8 us (level)
  starting transfers between devices: 23.5 us -> 24.1 us
  waiting for transfers between devices: 8.98 us -> 8.41 us
    pallas_call x1, Pallas kernels: 4.76 us -> 2.69 us  [on_device(): pl.pallas_call(own_kernel, out_shape=[pltpu.VMEM((mem_dev * row_stride(ce...]
    pallas_call x2 -> x4, Pallas kernels: 4.51 us -> 6.04 us  [the longest x1 1.52 us: on_device(): sent_m1 = answer(turned, w_m1, sent_m2)]
    ppermute x10, starting transfers between devices: 19.3 us -> 19.9 us  [passed_along(): lax.ppermute(x, axis, [(i, (i + by) % devices) for i in range(devices)])]
    ppermute x10, waiting for transfers between devices: 5.81 us -> 5.3 us  [passed_along(): lax.ppermute(x, axis, [(i, (i + by) % devices) for i in range(devices)])]
  transfers between devices with their start and end apart: 13 -> 13, of which waited for: 6 -> 5; matrix products, arithmetic and copies ran while one was open for 0% -> 0% of each run, Pallas kernels for 23% -> 22%
where the time goes in v5:
time: 48.8 us; the launch traced here: 48.7 us
  starting transfers between devices  24.1 us (49%)
  Pallas kernels  15.3 us (31%)
  waiting for transfers between devices  8.41 us (17%)
  between operations  0.79 us (2%)
    ppermute x10, starting transfers between devices, passed_along(): lax.ppermute(x, axis, [(i, (i + by) % devices) for i in range(devices)])  19.9 us
    ppermute x10, waiting for transfers between devices, passed_along(): lax.ppermute(x, axis, [(i, (i + by) % devices) for i in range(devices)])  5.3 us
    ppermute x3, starting transfers between devices, swapped(): lax.ppermute(x, axis, [(i, i ^ mask) for i in range(lax.axis_size(axis))])  4.18 us
    ppermute x3, waiting for transfers between devices, swapped(): lax.ppermute(x, axis, [(i, i ^ mask) for i in range(lax.axis_size(axis))])  3.11 us
    pallas_call x1, Pallas kernels, on_device(): pl.pallas_call(own_kernel, out_shape=[pltpu.VMEM((mem_dev * row_stride(ce...  2.69 us
    pallas_call x1, Pallas kernels, on_device(): pl.pallas_call(ask_low_kernel, out_shape=[pltpu.VMEM((neigh * obs // 128,...  2.63 us
    pallas_call x2, Pallas kernels, combine(): pl.pallas_call(lambda *refs: combine_kernel(firsts, *refs), out_shape=jax...  1.69 us
    pallas_call x1, Pallas kernels, on_device(): sent_m1 = answer(turned, w_m1, sent_m2)  1.52 us
  transfers between devices with their start and end apart: 13, of which 5 were waited for; matrix products, arithmetic and copies ran while one was open for 0% of the time, Pallas kernels for 22%

profile of v5, /device:TPU:4, one launch (start us, length us, event | category | flops | bytes accessed | tf_op | source)
XLA Modules:
  0.0 48.7 jit_solution(3636614936829732838)
XLA Ops:
  0.6 2.6 %ask_low.1 = (s32[32,128]{1,0:T(8,128)S(1)}, bf16[120,1024]{1,0:T(8,128)(2,1)S(1)}, s32[1,4096]{1,0:T(1,128)S(1)}, bf16[10,128,2048]{2,1,0:T(8,128)(2,1)S(1)}, b...) custom-call(s32[4,1024]{1,0:T(4,128)} %bitcast.11, s32[1,4096]{1,0:T(1,128)} %table_hbm.3, ...), custom_call_target="tpu_custom_call" | custom-call | flops 2000000000 | bytes 6000000 | tf_op jit(solution)/shard_map/ask_low/pallas_call | solution.py:301
  3.3 8.4 %collective-permute-start = (bf16[128,768]{1,0:T(8,128)(2,1)S(1)}, bf16[128,768]{1,0:T(8,128)(2,1)S(1)}, u32[]{:S(2)}, u32[]{:S(2)}) collective-permute-start(bf16[128,768]{1,0:T(8,128)(2,1)S(1)} %get-tuple-element.25), channel_id=1, source_target_pairs={{0,62},{1,63},{2,0},{3,1},{4,2},{5,3},{6,4},{7,5},{8,6},{9,7},{10,... | collective-permute-start | bytes 589832 | tf_op jit(solution)/shard_map/ppermute | solution.py:20
  11.7 0.2 collective-permute-start.2
  11.8 0.9 %ask_high.1 = (bf16[128,1024]{1,0:T(8,128)(2,1)S(1)}, bf16[128,768]{1,0:T(8,128)(2,1)S(1)}, bf16[128,768]{1,0:T(8,128)(2,1)S(1)}) custom-call(s32[32,128]{1,0:T(8,128)S(1)} %get-tuple-element.19.inv_ref, bf16[120,1024]{1,0:T(8,128)(2,1)S(1)} %get-tuple-element.20.vw_ref, s32[1,4096]{1,0:T(1,128)S(1)} %get-tuple-element.21.table_ref), custom_call_target="tpu_custom_call" | custom-call | flops 2000000000 | bytes 1000000 | tf_op jit(solution)/shard_map/ask_high/pallas_call | solution.py:319
  12.7 0.4 collective-permute-start.4
  13.1 0.8 %collective-permute-start.6 = (bf16[128,768]{1,0:T(8,128)(2,1)S(1)}, bf16[128,768]{1,0:T(8,128)(2,1)S(1)}, u32[]{:S(2)}, u32[]{:S(2)}) collective-permute-start(bf16[128,768]{1,0:T(8,128)(2,1)S(1)} %get-tuple-element.28), channel_id=1, source_target_pairs={{0,2},{1,3},{2,4},{3,5},{4,6},{5,7},{6,8},{7,9},{8,10},{9,11},{10,... | collective-permute-start | bytes 589832 | tf_op jit(solution)/shard_map/ppermute | solution.py:20
  13.9 2.7 %own.1 = (f32[20520,128]{1,0:T(8,128)S(1)}, f32[16,1024]{1,0:T(8,128)S(1)}) custom-call(bf16[10,128,2048]{2,1,0:T(8,128)(2,1)S(1)} %get-tuple-element.18.state_ref, s32[1,4096]{1,0:T(1,128)} %table_hbm.3, bf16[128,1024]{1,0:T(8,128)(2,1)S(1)} %get-tuple-element.22.w_ref), custom_call_target="tpu_custom_call" | custom-call | flops 8000000000 | bytes 10000000 | tf_op jit(solution)/shard_map/own/pallas_call | solution.py:329
  16.6 0.0 collective-permute-done.refs_1_
  16.6 1.5 %answer.4.refs_2_ = f32[16,768]{1,0:T(8,128)S(1)} custom-call(f32[20520,128]{1,0:T(8,128)S(1)} %get-tuple-element.24.refs_0_, bf16[128,768]{1,0:T(8,128)(2,1)S(1)} %collective-permute-done.refs_1_, f32[16,1024]{1,0:T(8,128)S(1)} %get-tuple-element.23.refs_2_), custom_call_target="tpu_custom_call" | custom-call | flops 2000000000 | bytes 1000000 | tf_op jit(solution)/shard_map/answer/pallas_call | solution.py:357
  18.1 0.2 collective-permute-start.1
  18.3 0.0 collective-permute-done.2.refs_1_
  18.3 1.5 %answer.5.refs_2_ = f32[16,768]{1,0:T(8,128)S(1)} custom-call(f32[20520,128]{1,0:T(8,128)S(1)} %get-tuple-element.24.refs_0_, bf16[128,768]{1,0:T(8,128)(2,1)S(1)} %collective-permute-done.2.refs_1_, f32[16,768]{1,0:T(8,128)S(1)} %answer.4.refs_2_), custom_call_target="tpu_custom_call" | custom-call | flops 2000000000 | bytes 1000000 | tf_op jit(solution)/shard_map/answer/pallas_call | solution.py:359
  19.8 0.1 collective-permute-start.3
  19.9 2.5 %collective-permute-done.4.refs_1_ = bf16[128,768]{1,0:T(8,128)(2,1)S(1)} collective-permute-done((bf16[128,768]{1,0:T(8,128)(2,1)S(1)}, bf16[128,768]{1,0:T(8,128)(2,1)S(1)}, u32[]{:S(2)}, u32[]{:S(2)}) %collective-permute-start.4) | collective-permute-done | bytes 196640 | tf_op jit(solution)/shard_map/ppermute | solution.py:20
  22.4 1.5 %answer.6.refs_2_ = f32[16,768]{1,0:T(8,128)S(1)} custom-call(f32[20520,128]{1,0:T(8,128)S(1)} %get-tuple-element.24.refs_0_, bf16[128,768]{1,0:T(8,128)(2,1)S(1)} %collective-permute-done.4.refs_1_, f32[16,768]{1,0:T(8,128)S(1)} %answer.5.refs_2_), custom_call_target="tpu_custom_call" | custom-call | flops 2000000000 | bytes 1000000 | tf_op jit(solution)/shard_map/answer/pallas_call | solution.py:361
  23.9 0.0 copy-start.3
  23.9 0.0 copy-start.4
  23.9 2.8 %collective-permute-start.5 = (f32[16,768]{1,0:T(8,128)S(1)}, f32[16,768]{1,0:T(8,128)S(1)}, u32[]{:S(2)}, u32[]{:S(2)}) collective-permute-start(f32[16,768]{1,0:T(8,128)S(1)} %answer.6.refs_2_), channel_id=1, source_target_pairs={{0,63},{1,0},{2,1},{3,2},{4,3},{5,4},{6,5},{7,6},{8,7},{9,8},{10,9... | collective-permute-start | bytes 147464 | tf_op jit(solution)/shard_map/ppermute | solution.py:20
  26.7 0.0 collective-permute-done.6.refs_1_
  26.7 1.5 %answer.7 = f32[16,768]{1,0:T(8,128)S(1)} custom-call(f32[20520,128]{1,0:T(8,128)S(1)} %get-tuple-element.24.refs_0_, bf16[128,768]{1,0:T(8,128)(2,1)S(1)} %collective-permute-done.6.refs_1_, f32[16,768]{1,0:T(8,128)S(1)} %answer.6.refs_2_), custom_call_target="tpu_custom_call" | custom-call | flops 2000000000 | bytes 1000000 | tf_op jit(solution)/shard_map/answer/pallas_call | solution.py:363
  28.3 0.0 copy-start
  28.3 0.0 copy-start.1
  28.3 0.0 copy-start.2
  28.3 2.0 %collective-permute-start.7 = (f32[16,768]{1,0:T(8,128)S(1)}, f32[16,768]{1,0:T(8,128)S(1)}, u32[]{:S(2)}, u32[]{:S(2)}) collective-permute-start(f32[16,768]{1,0:T(8,128)S(1)} %answer.7), channel_id=1, source_target_pairs={{0,62},{1,63},{2,0},{3,1},{4,2},{5,3},{6,4},{7,5},{8,6},{9,7},{10,... | collective-permute-start | bytes 147464 | tf_op jit(solution)/shard_map/ppermute | solution.py:20
  30.3 0.0 collective-permute-done.3.refs_4_
  30.3 0.0 collective-permute-done.1.refs_3_
  30.3 0.0 copy-done.3
  30.3 0.0 copy-done.4
  30.3 1.0 %combine.2.refs_2_ = f32[8,1280]{1,0:T(8,128)S(1)} custom-call(s32[4,1024]{1,0:T(4,128)S(1)} %bitcast.12, f32[4,1024]{1,0:T(4,128)S(1)} %bitcast.14, f32[16,1024]{1,0:T(8,128)S(1)} %get-tuple-element.23.refs_2_, f32[16,768]{1,0:T(8,128)S(1)} %collective-permute-done.1.refs_3_, f32[16,768]{1,0:T(8,128)S(1)} %collective-permute-done.3.refs_4_), custom_call_target="tpu_custom_call" | custom-call | flops 1000000000 | bytes 1000000 | tf_op jit(solution)/shard_map/combine/pallas_call | solution.py:368
  31.4 1.1 %collective-permute-done.7.refs_4_ = f32[16,768]{1,0:T(8,128)S(1)} collective-permute-done((f32[16,768]{1,0:T(8,128)S(1)}, f32[16,768]{1,0:T(8,128)S(1)}, u32[]{:S(2)}, u32[]{:S(2)}) %collective-permute-start.7) | collective-permute-done | bytes 49184 | tf_op jit(solution)/shard_map/ppermute | solution.py:20
  32.5 0.0 collective-permute-done.5.refs_3_
  32.5 0.7 %combine.3.refs_0_ = f32[8,1280]{1,0:T(8,128)S(1)} custom-call(s32[4,1024]{1,0:T(4,128)S(1)} %bitcast.13, f32[4,1024]{1,0:T(4,128)S(1)} %bitcast.15, f32[8,1280]{1,0:T(8,128)S(1)} %combine.2.refs_2_, f32[16,768]{1,0:T(8,128)S(1)} %collective-permute-done.5.refs_3_, f32[16,768]{1,0:T(8,128)S(1)} %collective-permute-done.7.refs_4_), custom_call_target="tpu_custom_call" | custom-call | flops 1000000000 | bytes 1000000 | tf_op jit(solution)/shard_map/combine/pallas_call | solution.py:368
  33.2 0.6 %collective-permute-start.10 = (f32[8,1280]{1,0:T(8,128)S(1)}, f32[8,1280]{1,0:T(8,128)S(1)}, u32[]{:S(2)}, u32[]{:S(2)}) collective-permute-start(f32[8,1280]{1,0:T(8,128)S(1)} %combine.3.refs_0_), channel_id=1, source_target_pairs={{0,192},{64,128},{128,64},{192,0},{1,193},{65,129},{129,65},{193,1... | collective-permute-start | bytes 122888 | tf_op jit(solution)/shard_map/ppermute | solution.py:24
  33.7 2.7 %collective-permute-start.9 = (f32[8,1280]{1,0:T(8,128)S(1)}, f32[8,1280]{1,0:T(8,128)S(1)}, u32[]{:S(2)}, u32[]{:S(2)}) collective-permute-start(f32[8,1280]{1,0:T(8,128)S(1)} %combine.3.refs_0_), channel_id=1, source_target_pairs={{0,128},{64,192},{128,0},{192,64},{1,129},{65,193},{129,1},{193,65... | collective-permute-start | bytes 122888 | tf_op jit(solution)/shard_map/ppermute | solution.py:24
  36.4 0.9 %collective-permute-start.8 = (f32[8,1280]{1,0:T(8,128)S(1)}, f32[8,1280]{1,0:T(8,128)S(1)}, u32[]{:S(2)}, u32[]{:S(2)}) collective-permute-start(f32[8,1280]{1,0:T(8,128)S(1)} %combine.3.refs_0_), channel_id=1, source_target_pairs={{0,64},{64,0},{128,192},{192,128},{1,65},{65,1},{129,193},{193,129... | collective-permute-start | bytes 122888 | tf_op jit(solution)/shard_map/ppermute | solution.py:24
  37.3 0.0 collective-permute-done.10.refs_3_
  37.3 1.9 %collective-permute-done.9.refs_2_ = f32[8,1280]{1,0:T(8,128)S(1)} collective-permute-done((f32[8,1280]{1,0:T(8,128)S(1)}, f32[8,1280]{1,0:T(8,128)S(1)}, u32[]{:S(2)}, u32[]{:S(2)}) %collective-permute-start.9) | collective-permute-done | bytes 40992 | tf_op jit(solution)/shard_map/ppermute | solution.py:24
  39.2 1.2 %collective-permute-done.8.refs_1_ = f32[8,1280]{1,0:T(8,128)S(1)} collective-permute-done((f32[8,1280]{1,0:T(8,128)S(1)}, f32[8,1280]{1,0:T(8,128)S(1)}, u32[]{:S(2)}, u32[]{:S(2)}) %collective-permute-start.8) | collective-permute-done | bytes 40992 | tf_op jit(solution)/shard_map/ppermute | solution.py:24
  40.4 0.0 copy-done
  40.4 0.0 copy-done.1
  40.5 0.0 copy-done.2
  40.5 0.6 %cov.1 = (f32[80,64]{1,0:T(8,128)S(1)}, f32[80,64]{1,0:T(8,128)S(1)}, f32[80,64]{1,0:T(8,128)S(1)}) custom-call(f32[8,1280]{1,0:T(8,128)S(1)} %combine.3.refs_0_, f32[8,1280]{1,0:T(8,128)S(1)} %collective-permute-done.8.refs_1_, f32[8,1280]{1,0:T(8,128)S(1)} %collective-permute-done.9.refs_2_, f32[8,1280]{1,0:T(8,128)S(1)} %collective-permute-done.10.refs_3_, ...), custom_call_target="tpu_custom_call" | custom-call | tf_op jit(solution)/shard_map/cov/pallas_call | solution.py:382
  41.0 0.1 collective-permute-start.11
  41.1 5.1 %collective-permute-start.12 = (f32[80,64]{1,0:T(8,128)S(1)}, f32[80,64]{1,0:T(8,128)S(1)}, u32[]{:S(2)}, u32[]{:S(2)}) collective-permute-start(f32[80,64]{1,0:T(8,128)S(1)} %get-tuple-element.31), channel_id=1, source_target_pairs={{0,63},{1,0},{2,1},{3,2},{4,3},{5,4},{6,5},{7,6},{8,7},{9,8},{10,9... | collective-permute-start | bytes 61448 | tf_op jit(solution)/shard_map/ppermute | solution.py:20
  46.2 1.7 %collective-permute-done.11.a_ref = f32[80,64]{1,0:T(8,128)S(1)} collective-permute-done((f32[80,64]{1,0:T(8,128)S(1)}, f32[80,64]{1,0:T(8,128)S(1)}, u32[]{:S(2)}, u32[]{:S(2)}) %collective-permute-start.11) | collective-permute-done | bytes 20512 | tf_op jit(solution)/shard_map/ppermute | solution.py:20
  47.9 0.0 collective-permute-done.12.b_ref
  47.9 0.8 %final.1 = (f32[10,8,40]{2,1,0:T(8,128)}, f32[8,10]{1,0:T(8,128)}) custom-call(f32[80,64]{1,0:T(8,128)S(1)} %get-tuple-element.29.mid_ref, f32[80,64]{1,0:T(8,128)S(1)} %collective-permute-done.11.a_ref, f32[80,64]{1,0:T(8,128)S(1)} %collective-permute-done.12.b_ref), custom_call_target="tpu_custom_call" | custom-call | tf_op jit(solution)/shard_map/final/pallas_call | solution.py:392
Async XLA Ops:
  3.3 13.3 %collective-permute-start = (bf16[128,768]{1,0:T(8,128)(2,1)S(1)}, bf16[128,768]{1,0:T(8,128)(2,1)S(1)}, u32[]{:S(2)}, u32[]{:S(2)}) collective-permute-start(bf16[128,768]{1,0:T(8,128)(2,1)S(1)} %get-tuple-element.25), channel_id=1, source_target_pairs={{0,62},{1,63},{2,0},{3,1},{4,2},{5,3},{6,4},{7,5},{8,6},{9,7},{10,... | collective-permute-start | bytes 589832 | tf_op jit(solution)/shard_map/ppermute | solution.py:20
  11.7 6.6 %collective-permute-start.2 = (bf16[128,768]{1,0:T(8,128)(2,1)S(1)}, bf16[128,768]{1,0:T(8,128)(2,1)S(1)}, u32[]{:S(2)}, u32[]{:S(2)}) collective-permute-start(bf16[128,768]{1,0:T(8,128)(2,1)S(1)} %get-tuple-element.26), channel_id=1, source_target_pairs={{0,63},{1,0},{2,1},{3,2},{4,3},{5,4},{6,5},{7,6},{8,7},{9,8},{10,9... | collective-permute-start | bytes 589832 | tf_op jit(solution)/shard_map/ppermute | solution.py:20
  12.7 9.7 %collective-permute-start.4 = (bf16[128,768]{1,0:T(8,128)(2,1)S(1)}, bf16[128,768]{1,0:T(8,128)(2,1)S(1)}, u32[]{:S(2)}, u32[]{:S(2)}) collective-permute-start(bf16[128,768]{1,0:T(8,128)(2,1)S(1)} %get-tuple-element.27), channel_id=1, source_target_pairs={{0,1},{1,2},{2,3},{3,4},{4,5},{5,6},{6,7},{7,8},{8,9},{9,10},{10,1... | collective-permute-start | bytes 589832 | tf_op jit(solution)/shard_map/ppermute | solution.py:20
  13.1 13.6 %collective-permute-start.6 = (bf16[128,768]{1,0:T(8,128)(2,1)S(1)}, bf16[128,768]{1,0:T(8,128)(2,1)S(1)}, u32[]{:S(2)}, u32[]{:S(2)}) collective-permute-start(bf16[128,768]{1,0:T(8,128)(2,1)S(1)} %get-tuple-element.28), channel_id=1, source_target_pairs={{0,2},{1,3},{2,4},{3,5},{4,6},{5,7},{6,8},{7,9},{8,10},{9,11},{10,... | collective-permute-start | bytes 589832 | tf_op jit(solution)/shard_map/ppermute | solution.py:20
  18.1 12.2 %collective-permute-start.1 = (f32[16,768]{1,0:T(8,128)S(1)}, f32[16,768]{1,0:T(8,128)S(1)}, u32[]{:S(2)}, u32[]{:S(2)}) collective-permute-start(f32[16,768]{1,0:T(8,128)S(1)} %answer.4.refs_2_), channel_id=1, source_target_pairs={{0,2},{1,3},{2,4},{3,5},{4,6},{5,7},{6,8},{7,9},{8,10},{9,11},{10,... | collective-permute-start | bytes 147464 | tf_op jit(solution)/shard_map/ppermute | solution.py:20
  19.8 10.5 %collective-permute-start.3 = (f32[16,768]{1,0:T(8,128)S(1)}, f32[16,768]{1,0:T(8,128)S(1)}, u32[]{:S(2)}, u32[]{:S(2)}) collective-permute-start(f32[16,768]{1,0:T(8,128)S(1)} %answer.5.refs_2_), channel_id=1, source_target_pairs={{0,1},{1,2},{2,3},{3,4},{4,5},{5,6},{6,7},{7,8},{8,9},{9,10},{10,1... | collective-permute-start | bytes 147464 | tf_op jit(solution)/shard_map/ppermute | solution.py:20
  23.9 6.4 %copy-start.3 = (s32[1024,4]{0,1:T(4,128)S(1)}, s32[1024,4]{0,1:T(4,128)}, u32[]{:S(2)}) copy-start(s32[1024,4]{0,1:T(4,128)} %param.11) | copy-start | bytes 49156
  23.9 6.4 %copy-start.4 = (f32[1024,4]{0,1:T(4,128)S(1)}, f32[1024,4]{0,1:T(4,128)}, u32[]{:S(2)}) copy-start(f32[1024,4]{0,1:T(4,128)} %param.10) | copy-start | bytes 49156
  23.9 8.5 %collective-permute-start.5 = (f32[16,768]{1,0:T(8,128)S(1)}, f32[16,768]{1,0:T(8,128)S(1)}, u32[]{:S(2)}, u32[]{:S(2)}) collective-permute-start(f32[16,768]{1,0:T(8,128)S(1)} %answer.6.refs_2_), channel_id=1, source_target_pairs={{0,63},{1,0},{2,1},{3,2},{4,3},{5,4},{6,5},{7,6},{8,7},{9,8},{10,9... | collective-permute-start | bytes 147464 | tf_op jit(solution)/shard_map/ppermute | solution.py:20
  28.3 12.2 %copy-start = (f32[1024]{0:T(1024)S(1)}, f32[1024]{0:T(1024)}, u32[]{:S(2)}) copy-start(f32[1024]{0:T(1024)} %param.13) | copy-start | bytes 12292
  28.3 12.2 %copy-start.1 = (f32[1024]{0:T(1024)S(1)}, f32[1024]{0:T(1024)}, u32[]{:S(2)}) copy-start(f32[1024]{0:T(1024)} %param.14) | copy-start | bytes 12292
  28.3 12.2 %copy-start.2 = (s32[1024]{0:T(1024)S(1)}, s32[1024]{0:T(1024)}, u32[]{:S(2)}) copy-start(s32[1024]{0:T(1024)} %param.15) | copy-start | bytes 12292
  28.3 4.2 %collective-permute-start.7 = (f32[16,768]{1,0:T(8,128)S(1)}, f32[16,768]{1,0:T(8,128)S(1)}, u32[]{:S(2)}, u32[]{:S(2)}) collective-permute-start(f32[16,768]{1,0:T(8,128)S(1)} %answer.7), channel_id=1, source_target_pairs={{0,62},{1,63},{2,0},{3,1},{4,2},{5,3},{6,4},{7,5},{8,6},{9,7},{10,... | collective-permute-start | bytes 147464 | tf_op jit(solution)/shard_map/ppermute | solution.py:20
  33.2 4.2 %collective-permute-start.10 = (f32[8,1280]{1,0:T(8,128)S(1)}, f32[8,1280]{1,0:T(8,128)S(1)}, u32[]{:S(2)}, u32[]{:S(2)}) collective-permute-start(f32[8,1280]{1,0:T(8,128)S(1)} %combine.3.refs_0_), channel_id=1, source_target_pairs={{0,192},{64,128},{128,64},{192,0},{1,193},{65,129},{129,65},{193,1... | collective-permute-start | bytes 122888 | tf_op jit(solution)/shard_map/ppermute | solution.py:24
  33.7 5.5 %collective-permute-start.9 = (f32[8,1280]{1,0:T(8,128)S(1)}, f32[8,1280]{1,0:T(8,128)S(1)}, u32[]{:S(2)}, u32[]{:S(2)}) collective-permute-start(f32[8,1280]{1,0:T(8,128)S(1)} %combine.3.refs_0_), channel_id=1, source_target_pairs={{0,128},{64,192},{128,0},{192,64},{1,129},{65,193},{129,1},{193,65... | collective-permute-start | bytes 122888 | tf_op jit(solution)/shard_map/ppermute | solution.py:24
  36.4 4.0 %collective-permute-start.8 = (f32[8,1280]{1,0:T(8,128)S(1)}, f32[8,1280]{1,0:T(8,128)S(1)}, u32[]{:S(2)}, u32[]{:S(2)}) collective-permute-start(f32[8,1280]{1,0:T(8,128)S(1)} %combine.3.refs_0_), channel_id=1, source_target_pairs={{0,64},{64,0},{128,192},{192,128},{1,65},{65,1},{129,193},{193,129... | collective-permute-start | bytes 122888 | tf_op jit(solution)/shard_map/ppermute | solution.py:24
  41.0 6.8 %collective-permute-start.11 = (f32[80,64]{1,0:T(8,128)S(1)}, f32[80,64]{1,0:T(8,128)S(1)}, u32[]{:S(2)}, u32[]{:S(2)}) collective-permute-start(f32[80,64]{1,0:T(8,128)S(1)} %get-tuple-element.30), channel_id=1, source_target_pairs={{0,1},{1,2},{2,3},{3,4},{4,5},{5,6},{6,7},{7,8},{8,9},{9,10},{10,1... | collective-permute-start | bytes 61448 | tf_op jit(solution)/shard_map/ppermute | solution.py:20
  41.1 6.7 %collective-permute-start.12 = (f32[80,64]{1,0:T(8,128)S(1)}, f32[80,64]{1,0:T(8,128)S(1)}, u32[]{:S(2)}, u32[]{:S(2)}) collective-permute-start(f32[80,64]{1,0:T(8,128)S(1)} %get-tuple-element.31), channel_id=1, source_target_pairs={{0,63},{1,0},{2,1},{3,2},{4,3},{5,4},{6,5},{7,6},{8,7},{9,8},{10,9... | collective-permute-start | bytes 61448 | tf_op jit(solution)/shard_map/ppermute | solution.py:20

commit v6 on v5

--- a/solution.py
+++ b/solution.py
@@ -156,19 +156,16 @@
         eq_ref[:, at] = answer_tile(lambda i: cell_ref[0, tile * TILE + i], w_ref[:, at], turned_ref, cells)
 
 
-def answer_kernel(levels, cells, turned_ref, w_ref, before_ref, eq_ref, words, scalars, sem):
+def answer_kernel(levels, cells, turned_ref, w_ref, before_ref, eq_ref):
     tail = w_ref[112:128, :].astype(F32)
     row = levels - 112
-    words[...] = (8.0 * tail[row : row + 1, :] + tail[row + 1 : row + 2, :]).astype(jnp.int32)
-    copy = pltpu.make_async_copy(words, scalars, sem)
-    copy.start()
+    words = (8.0 * tail[row : row + 1, :] + tail[row + 1 : row + 2, :]).astype(jnp.int32)
     keep = lax.broadcasted_iota(jnp.int32, (128, TILE), 0) < levels
-    copy.wait()
     for tile in range(eq_ref.shape[1] // TILE):
         at = slice(tile * TILE, (tile + 1) * TILE)
         w = w_ref[:, at]
         w = jnp.where(keep, w, jnp.zeros_like(w))
-        eq_ref[:, at] = answer_tile(lambda j: scalars[0, tile * TILE + j], w, turned_ref, cells)
+        eq_ref[:, at] = answer_tile(lambda j: words[0, tile * TILE + j], w, turned_ref, cells)
 
 
 def combine_kernel(firsts, slot_ref, hw_ref, *refs):
@@ -345,11 +342,6 @@
         out_shape=pltpu.VMEM((16, halo), F32),
         in_specs=[VMEM] * 3,
         out_specs=VMEM,
-        scratch_shapes=[
-            pltpu.VMEM((1, halo), jnp.int32),
-            pltpu.SMEM((1, halo), jnp.int32),
-            pltpu.SemaphoreType.DMA,
-        ],
         compiler_params=params,
         cost_estimate=pl.CostEstimate(flops=2_000_000_000, bytes_accessed=1_000_000, transcendentals=0),
         name="answer",

time: 48.8 us -> 47.8 us (0.980)
  Pallas kernels: 15.3 us -> 14 us
  waiting for transfers between devices: 8.41 us -> 9.08 us
    ppermute x10, waiting for transfers between devices: 5.3 us -> 5.91 us  [passed_along(): lax.ppermute(x, axis, [(i, (i + by) % devices) for i in range(devices)])]
  transfers between devices with their start and end apart: 13 -> 13, of which waited for: 5 -> 5; matrix products, arithmetic and copies ran while one was open for 0% -> 0% of each run, Pallas kernels for 22% -> 20%
where the time goes in v6:
time: 47.8 us; the launch traced here: 47.6 us
  starting transfers between devices  23.7 us (50%)
  Pallas kernels  14 us (29%)
  waiting for transfers between devices  9.08 us (19%)
  between operations  0.77 us (2%)
    ppermute x10, starting transfers between devices, passed_along(): lax.ppermute(x, axis, [(i, (i + by) % devices) for i in range(devices)])  19.5 us
    ppermute x10, waiting for transfers between devices, passed_along(): lax.ppermute(x, axis, [(i, (i + by) % devices) for i in range(devices)])  5.91 us
    ppermute x3, starting transfers between devices, swapped(): lax.ppermute(x, axis, [(i, i ^ mask) for i in range(lax.axis_size(axis))])  4.18 us
    ppermute x3, waiting for transfers between devices, swapped(): lax.ppermute(x, axis, [(i, i ^ mask) for i in range(lax.axis_size(axis))])  3.17 us
    pallas_call x1, Pallas kernels, on_device(): pl.pallas_call(own_kernel, out_shape=[pltpu.VMEM((mem_dev * row_stride(ce...  2.67 us
    pallas_call x1, Pallas kernels, on_device(): pl.pallas_call(ask_low_kernel, out_shape=[pltpu.VMEM((neigh * obs // 128,...  2.63 us
    pallas_call x2, Pallas kernels, combine(): pl.pallas_call(lambda *refs: combine_kernel(firsts, *refs), out_shape=jax...  1.69 us
    pallas_call x1, Pallas kernels, on_device(): sent_m2 = answer(turned, w_m2, eq_own)  1.2 us
  transfers between devices with their start and end apart: 13, of which 5 were waited for; matrix products, arithmetic and copies ran while one was open for 0% of the time, Pallas kernels for 20%

profile of v6, /device:TPU:4, one launch (start us, length us, event | category | flops | bytes accessed | tf_op | source)
XLA Modules:
  0.0 47.6 jit_solution(9841817414899672720)
XLA Ops:
  0.6 2.6 %ask_low.1 = (s32[32,128]{1,0:T(8,128)S(1)}, bf16[120,1024]{1,0:T(8,128)(2,1)S(1)}, s32[1,4096]{1,0:T(1,128)S(1)}, bf16[10,128,2048]{2,1,0:T(8,128)(2,1)S(1)}, b...) custom-call(s32[4,1024]{1,0:T(4,128)} %bitcast.11, s32[1,4096]{1,0:T(1,128)} %table_hbm.3, ...), custom_call_target="tpu_custom_call" | custom-call | flops 2000000000 | bytes 6000000 | tf_op jit(solution)/shard_map/ask_low/pallas_call | solution.py:298
  3.3 8.4 %collective-permute-start = (bf16[128,768]{1,0:T(8,128)(2,1)S(1)}, bf16[128,768]{1,0:T(8,128)(2,1)S(1)}, u32[]{:S(2)}, u32[]{:S(2)}) collective-permute-start(bf16[128,768]{1,0:T(8,128)(2,1)S(1)} %get-tuple-element.25), channel_id=1, source_target_pairs={{0,62},{1,63},{2,0},{3,1},{4,2},{5,3},{6,4},{7,5},{8,6},{9,7},{10,... | collective-permute-start | bytes 589832 | tf_op jit(solution)/shard_map/ppermute | solution.py:20
  11.7 0.2 collective-permute-start.2
  11.8 0.9 %ask_high.1 = (bf16[128,1024]{1,0:T(8,128)(2,1)S(1)}, bf16[128,768]{1,0:T(8,128)(2,1)S(1)}, bf16[128,768]{1,0:T(8,128)(2,1)S(1)}) custom-call(s32[32,128]{1,0:T(8,128)S(1)} %get-tuple-element.19.inv_ref, bf16[120,1024]{1,0:T(8,128)(2,1)S(1)} %get-tuple-element.20.vw_ref, s32[1,4096]{1,0:T(1,128)S(1)} %get-tuple-element.21.table_ref), custom_call_target="tpu_custom_call" | custom-call | flops 2000000000 | bytes 1000000 | tf_op jit(solution)/shard_map/ask_high/pallas_call | solution.py:316
  12.7 0.4 collective-permute-start.4
  13.1 0.8 %collective-permute-start.6 = (bf16[128,768]{1,0:T(8,128)(2,1)S(1)}, bf16[128,768]{1,0:T(8,128)(2,1)S(1)}, u32[]{:S(2)}, u32[]{:S(2)}) collective-permute-start(bf16[128,768]{1,0:T(8,128)(2,1)S(1)} %get-tuple-element.28), channel_id=1, source_target_pairs={{0,2},{1,3},{2,4},{3,5},{4,6},{5,7},{6,8},{7,9},{8,10},{9,11},{10,... | collective-permute-start | bytes 589832 | tf_op jit(solution)/shard_map/ppermute | solution.py:20
  13.9 2.7 %own.1 = (f32[20520,128]{1,0:T(8,128)S(1)}, f32[16,1024]{1,0:T(8,128)S(1)}) custom-call(bf16[10,128,2048]{2,1,0:T(8,128)(2,1)S(1)} %get-tuple-element.18.state_ref, s32[1,4096]{1,0:T(1,128)} %table_hbm.3, bf16[128,1024]{1,0:T(8,128)(2,1)S(1)} %get-tuple-element.22.w_ref), custom_call_target="tpu_custom_call" | custom-call | flops 8000000000 | bytes 10000000 | tf_op jit(solution)/shard_map/own/pallas_call | solution.py:326
  16.6 0.0 collective-permute-done.refs_1_
  16.6 1.2 %answer.4.refs_2_ = f32[16,768]{1,0:T(8,128)S(1)} custom-call(f32[20520,128]{1,0:T(8,128)S(1)} %get-tuple-element.24.refs_0_, bf16[128,768]{1,0:T(8,128)(2,1)S(1)} %collective-permute-done.refs_1_, f32[16,1024]{1,0:T(8,128)S(1)} %get-tuple-element.23.refs_2_), custom_call_target="tpu_custom_call" | custom-call | flops 2000000000 | bytes 1000000 | tf_op jit(solution)/shard_map/answer/pallas_call | solution.py:349
  17.8 0.2 collective-permute-start.1
  18.0 0.0 collective-permute-done.2.refs_1_
  18.0 1.2 %answer.5.refs_2_ = f32[16,768]{1,0:T(8,128)S(1)} custom-call(f32[20520,128]{1,0:T(8,128)S(1)} %get-tuple-element.24.refs_0_, bf16[128,768]{1,0:T(8,128)(2,1)S(1)} %collective-permute-done.2.refs_1_, f32[16,768]{1,0:T(8,128)S(1)} %answer.4.refs_2_), custom_call_target="tpu_custom_call" | custom-call | flops 2000000000 | bytes 1000000 | tf_op jit(solution)/shard_map/answer/pallas_call | solution.py:351
  19.2 0.3 collective-permute-start.3
  19.4 2.9 %collective-permute-done.4.refs_1_ = bf16[128,768]{1,0:T(8,128)(2,1)S(1)} collective-permute-done((bf16[128,768]{1,0:T(8,128)(2,1)S(1)}, bf16[128,768]{1,0:T(8,128)(2,1)S(1)}, u32[]{:S(2)}, u32[]{:S(2)}) %collective-permute-start.4) | collective-permute-done | bytes 196640 | tf_op jit(solution)/shard_map/ppermute | solution.py:20
  22.4 1.2 %answer.6.refs_2_ = f32[16,768]{1,0:T(8,128)S(1)} custom-call(f32[20520,128]{1,0:T(8,128)S(1)} %get-tuple-element.24.refs_0_, bf16[128,768]{1,0:T(8,128)(2,1)S(1)} %collective-permute-done.4.refs_1_, f32[16,768]{1,0:T(8,128)S(1)} %answer.5.refs_2_), custom_call_target="tpu_custom_call" | custom-call | flops 2000000000 | bytes 1000000 | tf_op jit(solution)/shard_map/answer/pallas_call | solution.py:353
  23.6 0.0 copy-start.3
  23.6 0.0 copy-start.4
  23.6 2.3 %collective-permute-start.5 = (f32[16,768]{1,0:T(8,128)S(1)}, f32[16,768]{1,0:T(8,128)S(1)}, u32[]{:S(2)}, u32[]{:S(2)}) collective-permute-start(f32[16,768]{1,0:T(8,128)S(1)} %answer.6.refs_2_), channel_id=1, source_target_pairs={{0,63},{1,0},{2,1},{3,2},{4,3},{5,4},{6,5},{7,6},{8,7},{9,8},{10,9... | collective-permute-start | bytes 147464 | tf_op jit(solution)/shard_map/ppermute | solution.py:20
  25.9 0.0 collective-permute-done.6.refs_1_
  25.9 1.2 %answer.7 = f32[16,768]{1,0:T(8,128)S(1)} custom-call(f32[20520,128]{1,0:T(8,128)S(1)} %get-tuple-element.24.refs_0_, bf16[128,768]{1,0:T(8,128)(2,1)S(1)} %collective-permute-done.6.refs_1_, f32[16,768]{1,0:T(8,128)S(1)} %answer.6.refs_2_), custom_call_target="tpu_custom_call" | custom-call | flops 2000000000 | bytes 1000000 | tf_op jit(solution)/shard_map/answer/pallas_call | solution.py:355
  27.1 0.0 copy-start
  27.1 0.0 copy-start.1
  27.2 0.0 copy-start.2
  27.2 1.9 %collective-permute-start.7 = (f32[16,768]{1,0:T(8,128)S(1)}, f32[16,768]{1,0:T(8,128)S(1)}, u32[]{:S(2)}, u32[]{:S(2)}) collective-permute-start(f32[16,768]{1,0:T(8,128)S(1)} %answer.7), channel_id=1, source_target_pairs={{0,62},{1,63},{2,0},{3,1},{4,2},{5,3},{6,4},{7,5},{8,6},{9,7},{10,... | collective-permute-start | bytes 147464 | tf_op jit(solution)/shard_map/ppermute | solution.py:20
  29.0 0.0 collective-permute-done.3.refs_4_
  29.0 0.0 collective-permute-done.1.refs_3_
  29.0 0.0 copy-done.3
  29.1 0.0 copy-done.4
  29.1 1.0 %combine.2.refs_2_ = f32[8,1280]{1,0:T(8,128)S(1)} custom-call(s32[4,1024]{1,0:T(4,128)S(1)} %bitcast.12, f32[4,1024]{1,0:T(4,128)S(1)} %bitcast.14, f32[16,1024]{1,0:T(8,128)S(1)} %get-tuple-element.23.refs_2_, f32[16,768]{1,0:T(8,128)S(1)} %collective-permute-done.1.refs_3_, f32[16,768]{1,0:T(8,128)S(1)} %collective-permute-done.3.refs_4_), custom_call_target="tpu_custom_call" | custom-call | flops 1000000000 | bytes 1000000 | tf_op jit(solution)/shard_map/combine/pallas_call | solution.py:360
  30.1 1.3 %collective-permute-done.7.refs_4_ = f32[16,768]{1,0:T(8,128)S(1)} collective-permute-done((f32[16,768]{1,0:T(8,128)S(1)}, f32[16,768]{1,0:T(8,128)S(1)}, u32[]{:S(2)}, u32[]{:S(2)}) %collective-permute-start.7) | collective-permute-done | bytes 49184 | tf_op jit(solution)/shard_map/ppermute | solution.py:20
  31.3 0.0 collective-permute-done.5.refs_3_
  31.3 0.7 %combine.3.refs_0_ = f32[8,1280]{1,0:T(8,128)S(1)} custom-call(s32[4,1024]{1,0:T(4,128)S(1)} %bitcast.13, f32[4,1024]{1,0:T(4,128)S(1)} %bitcast.15, f32[8,1280]{1,0:T(8,128)S(1)} %combine.2.refs_2_, f32[16,768]{1,0:T(8,128)S(1)} %collective-permute-done.5.refs_3_, f32[16,768]{1,0:T(8,128)S(1)} %collective-permute-done.7.refs_4_), custom_call_target="tpu_custom_call" | custom-call | flops 1000000000 | bytes 1000000 | tf_op jit(solution)/shard_map/combine/pallas_call | solution.py:360
  32.0 0.6 %collective-permute-start.10 = (f32[8,1280]{1,0:T(8,128)S(1)}, f32[8,1280]{1,0:T(8,128)S(1)}, u32[]{:S(2)}, u32[]{:S(2)}) collective-permute-start(f32[8,1280]{1,0:T(8,128)S(1)} %combine.3.refs_0_), channel_id=1, source_target_pairs={{0,192},{64,128},{128,64},{192,0},{1,193},{65,129},{129,65},{193,1... | collective-permute-start | bytes 122888 | tf_op jit(solution)/shard_map/ppermute | solution.py:24
  32.6 2.7 %collective-permute-start.9 = (f32[8,1280]{1,0:T(8,128)S(1)}, f32[8,1280]{1,0:T(8,128)S(1)}, u32[]{:S(2)}, u32[]{:S(2)}) collective-permute-start(f32[8,1280]{1,0:T(8,128)S(1)} %combine.3.refs_0_), channel_id=1, source_target_pairs={{0,128},{64,192},{128,0},{192,64},{1,129},{65,193},{129,1},{193,65... | collective-permute-start | bytes 122888 | tf_op jit(solution)/shard_map/ppermute | solution.py:24
  35.4 0.8 %collective-permute-start.8 = (f32[8,1280]{1,0:T(8,128)S(1)}, f32[8,1280]{1,0:T(8,128)S(1)}, u32[]{:S(2)}, u32[]{:S(2)}) collective-permute-start(f32[8,1280]{1,0:T(8,128)S(1)} %combine.3.refs_0_), channel_id=1, source_target_pairs={{0,64},{64,0},{128,192},{192,128},{1,65},{65,1},{129,193},{193,129... | collective-permute-start | bytes 122888 | tf_op jit(solution)/shard_map/ppermute | solution.py:24
  36.2 0.0 collective-permute-done.10.refs_3_
  36.2 1.9 %collective-permute-done.9.refs_2_ = f32[8,1280]{1,0:T(8,128)S(1)} collective-permute-done((f32[8,1280]{1,0:T(8,128)S(1)}, f32[8,1280]{1,0:T(8,128)S(1)}, u32[]{:S(2)}, u32[]{:S(2)}) %collective-permute-start.9) | collective-permute-done | bytes 40992 | tf_op jit(solution)/shard_map/ppermute | solution.py:24
  38.2 1.2 %collective-permute-done.8.refs_1_ = f32[8,1280]{1,0:T(8,128)S(1)} collective-permute-done((f32[8,1280]{1,0:T(8,128)S(1)}, f32[8,1280]{1,0:T(8,128)S(1)}, u32[]{:S(2)}, u32[]{:S(2)}) %collective-permute-start.8) | collective-permute-done | bytes 40992 | tf_op jit(solution)/shard_map/ppermute | solution.py:24
  39.4 0.0 copy-done
  39.4 0.0 copy-done.1
  39.4 0.0 copy-done.2
  39.4 0.6 %cov.1 = (f32[80,64]{1,0:T(8,128)S(1)}, f32[80,64]{1,0:T(8,128)S(1)}, f32[80,64]{1,0:T(8,128)S(1)}) custom-call(f32[8,1280]{1,0:T(8,128)S(1)} %combine.3.refs_0_, f32[8,1280]{1,0:T(8,128)S(1)} %collective-permute-done.8.refs_1_, f32[8,1280]{1,0:T(8,128)S(1)} %collective-permute-done.9.refs_2_, f32[8,1280]{1,0:T(8,128)S(1)} %collective-permute-done.10.refs_3_, ...), custom_call_target="tpu_custom_call" | custom-call | tf_op jit(solution)/shard_map/cov/pallas_call | solution.py:374
  40.0 0.1 collective-permute-start.11
  40.1 5.1 %collective-permute-start.12 = (f32[80,64]{1,0:T(8,128)S(1)}, f32[80,64]{1,0:T(8,128)S(1)}, u32[]{:S(2)}, u32[]{:S(2)}) collective-permute-start(f32[80,64]{1,0:T(8,128)S(1)} %get-tuple-element.31), channel_id=1, source_target_pairs={{0,63},{1,0},{2,1},{3,2},{4,3},{5,4},{6,5},{7,6},{8,7},{9,8},{10,9... | collective-permute-start | bytes 61448 | tf_op jit(solution)/shard_map/ppermute | solution.py:20
  45.1 1.7 %collective-permute-done.11.a_ref = f32[80,64]{1,0:T(8,128)S(1)} collective-permute-done((f32[80,64]{1,0:T(8,128)S(1)}, f32[80,64]{1,0:T(8,128)S(1)}, u32[]{:S(2)}, u32[]{:S(2)}) %collective-permute-start.11) | collective-permute-done | bytes 20512 | tf_op jit(solution)/shard_map/ppermute | solution.py:20
  46.8 0.0 collective-permute-done.12.b_ref
  46.8 0.8 %final.1 = (f32[10,8,40]{2,1,0:T(8,128)}, f32[8,10]{1,0:T(8,128)}) custom-call(f32[80,64]{1,0:T(8,128)S(1)} %get-tuple-element.29.mid_ref, f32[80,64]{1,0:T(8,128)S(1)} %collective-permute-done.11.a_ref, f32[80,64]{1,0:T(8,128)S(1)} %collective-permute-done.12.b_ref), custom_call_target="tpu_custom_call" | custom-call | tf_op jit(solution)/shard_map/final/pallas_call | solution.py:384
Async XLA Ops:
  3.3 13.3 %collective-permute-start = (bf16[128,768]{1,0:T(8,128)(2,1)S(1)}, bf16[128,768]{1,0:T(8,128)(2,1)S(1)}, u32[]{:S(2)}, u32[]{:S(2)}) collective-permute-start(bf16[128,768]{1,0:T(8,128)(2,1)S(1)} %get-tuple-element.25), channel_id=1, source_target_pairs={{0,62},{1,63},{2,0},{3,1},{4,2},{5,3},{6,4},{7,5},{8,6},{9,7},{10,... | collective-permute-start | bytes 589832 | tf_op jit(solution)/shard_map/ppermute | solution.py:20
  11.7 6.3 %collective-permute-start.2 = (bf16[128,768]{1,0:T(8,128)(2,1)S(1)}, bf16[128,768]{1,0:T(8,128)(2,1)S(1)}, u32[]{:S(2)}, u32[]{:S(2)}) collective-permute-start(bf16[128,768]{1,0:T(8,128)(2,1)S(1)} %get-tuple-element.26), channel_id=1, source_target_pairs={{0,63},{1,0},{2,1},{3,2},{4,3},{5,4},{6,5},{7,6},{8,7},{9,8},{10,9... | collective-permute-start | bytes 589832 | tf_op jit(solution)/shard_map/ppermute | solution.py:20
  12.7 9.7 %collective-permute-start.4 = (bf16[128,768]{1,0:T(8,128)(2,1)S(1)}, bf16[128,768]{1,0:T(8,128)(2,1)S(1)}, u32[]{:S(2)}, u32[]{:S(2)}) collective-permute-start(bf16[128,768]{1,0:T(8,128)(2,1)S(1)} %get-tuple-element.27), channel_id=1, source_target_pairs={{0,1},{1,2},{2,3},{3,4},{4,5},{5,6},{6,7},{7,8},{8,9},{9,10},{10,1... | collective-permute-start | bytes 589832 | tf_op jit(solution)/shard_map/ppermute | solution.py:20
  13.1 12.8 %collective-permute-start.6 = (bf16[128,768]{1,0:T(8,128)(2,1)S(1)}, bf16[128,768]{1,0:T(8,128)(2,1)S(1)}, u32[]{:S(2)}, u32[]{:S(2)}) collective-permute-start(bf16[128,768]{1,0:T(8,128)(2,1)S(1)} %get-tuple-element.28), channel_id=1, source_target_pairs={{0,2},{1,3},{2,4},{3,5},{4,6},{5,7},{6,8},{7,9},{8,10},{9,11},{10,... | collective-permute-start | bytes 589832 | tf_op jit(solution)/shard_map/ppermute | solution.py:20
  17.8 11.3 %collective-permute-start.1 = (f32[16,768]{1,0:T(8,128)S(1)}, f32[16,768]{1,0:T(8,128)S(1)}, u32[]{:S(2)}, u32[]{:S(2)}) collective-permute-start(f32[16,768]{1,0:T(8,128)S(1)} %answer.4.refs_2_), channel_id=1, source_target_pairs={{0,2},{1,3},{2,4},{3,5},{4,6},{5,7},{6,8},{7,9},{8,10},{9,11},{10,... | collective-permute-start | bytes 147464 | tf_op jit(solution)/shard_map/ppermute | solution.py:20
  19.2 9.9 %collective-permute-start.3 = (f32[16,768]{1,0:T(8,128)S(1)}, f32[16,768]{1,0:T(8,128)S(1)}, u32[]{:S(2)}, u32[]{:S(2)}) collective-permute-start(f32[16,768]{1,0:T(8,128)S(1)} %answer.5.refs_2_), channel_id=1, source_target_pairs={{0,1},{1,2},{2,3},{3,4},{4,5},{5,6},{6,7},{7,8},{8,9},{9,10},{10,1... | collective-permute-start | bytes 147464 | tf_op jit(solution)/shard_map/ppermute | solution.py:20
  23.6 5.5 %copy-start.3 = (s32[1024,4]{0,1:T(4,128)S(1)}, s32[1024,4]{0,1:T(4,128)}, u32[]{:S(2)}) copy-start(s32[1024,4]{0,1:T(4,128)} %param.11) | copy-start | bytes 49156
  23.6 5.5 %copy-start.4 = (f32[1024,4]{0,1:T(4,128)S(1)}, f32[1024,4]{0,1:T(4,128)}, u32[]{:S(2)}) copy-start(f32[1024,4]{0,1:T(4,128)} %param.10) | copy-start | bytes 49156
  23.6 7.7 %collective-permute-start.5 = (f32[16,768]{1,0:T(8,128)S(1)}, f32[16,768]{1,0:T(8,128)S(1)}, u32[]{:S(2)}, u32[]{:S(2)}) collective-permute-start(f32[16,768]{1,0:T(8,128)S(1)} %answer.6.refs_2_), channel_id=1, source_target_pairs={{0,63},{1,0},{2,1},{3,2},{4,3},{5,4},{6,5},{7,6},{8,7},{9,8},{10,9... | collective-permute-start | bytes 147464 | tf_op jit(solution)/shard_map/ppermute | solution.py:20
  27.1 12.2 %copy-start = (f32[1024]{0:T(1024)S(1)}, f32[1024]{0:T(1024)}, u32[]{:S(2)}) copy-start(f32[1024]{0:T(1024)} %param.13) | copy-start | bytes 12292
  27.1 12.2 %copy-start.1 = (f32[1024]{0:T(1024)S(1)}, f32[1024]{0:T(1024)}, u32[]{:S(2)}) copy-start(f32[1024]{0:T(1024)} %param.14) | copy-start | bytes 12292
  27.2 12.2 %copy-start.2 = (s32[1024]{0:T(1024)S(1)}, s32[1024]{0:T(1024)}, u32[]{:S(2)}) copy-start(s32[1024]{0:T(1024)} %param.15) | copy-start | bytes 12292
  27.2 4.2 %collective-permute-start.7 = (f32[16,768]{1,0:T(8,128)S(1)}, f32[16,768]{1,0:T(8,128)S(1)}, u32[]{:S(2)}, u32[]{:S(2)}) collective-permute-start(f32[16,768]{1,0:T(8,128)S(1)} %answer.7), channel_id=1, source_target_pairs={{0,62},{1,63},{2,0},{3,1},{4,2},{5,3},{6,4},{7,5},{8,6},{9,7},{10,... | collective-permute-start | bytes 147464 | tf_op jit(solution)/shard_map/ppermute | solution.py:20
  32.0 4.2 %collective-permute-start.10 = (f32[8,1280]{1,0:T(8,128)S(1)}, f32[8,1280]{1,0:T(8,128)S(1)}, u32[]{:S(2)}, u32[]{:S(2)}) collective-permute-start(f32[8,1280]{1,0:T(8,128)S(1)} %combine.3.refs_0_), channel_id=1, source_target_pairs={{0,192},{64,128},{128,64},{192,0},{1,193},{65,129},{129,65},{193,1... | collective-permute-start | bytes 122888 | tf_op jit(solution)/shard_map/ppermute | solution.py:24
  32.6 5.5 %collective-permute-start.9 = (f32[8,1280]{1,0:T(8,128)S(1)}, f32[8,1280]{1,0:T(8,128)S(1)}, u32[]{:S(2)}, u32[]{:S(2)}) collective-permute-start(f32[8,1280]{1,0:T(8,128)S(1)} %combine.3.refs_0_), channel_id=1, source_target_pairs={{0,128},{64,192},{128,0},{192,64},{1,129},{65,193},{129,1},{193,65... | collective-permute-start | bytes 122888 | tf_op jit(solution)/shard_map/ppermute | solution.py:24
  35.4 4.0 %collective-permute-start.8 = (f32[8,1280]{1,0:T(8,128)S(1)}, f32[8,1280]{1,0:T(8,128)S(1)}, u32[]{:S(2)}, u32[]{:S(2)}) collective-permute-start(f32[8,1280]{1,0:T(8,128)S(1)} %combine.3.refs_0_), channel_id=1, source_target_pairs={{0,64},{64,0},{128,192},{192,128},{1,65},{65,1},{129,193},{193,129... | collective-permute-start | bytes 122888 | tf_op jit(solution)/shard_map/ppermute | solution.py:24
  40.0 6.8 %collective-permute-start.11 = (f32[80,64]{1,0:T(8,128)S(1)}, f32[80,64]{1,0:T(8,128)S(1)}, u32[]{:S(2)}, u32[]{:S(2)}) collective-permute-start(f32[80,64]{1,0:T(8,128)S(1)} %get-tuple-element.30), channel_id=1, source_target_pairs={{0,1},{1,2},{2,3},{3,4},{4,5},{5,6},{6,7},{7,8},{8,9},{9,10},{10,1... | collective-permute-start | bytes 61448 | tf_op jit(solution)/shard_map/ppermute | solution.py:20
  40.1 6.7 %collective-permute-start.12 = (f32[80,64]{1,0:T(8,128)S(1)}, f32[80,64]{1,0:T(8,128)S(1)}, u32[]{:S(2)}, u32[]{:S(2)}) collective-permute-start(f32[80,64]{1,0:T(8,128)S(1)} %get-tuple-element.31), channel_id=1, source_target_pairs={{0,63},{1,0},{2,1},{3,2},{4,3},{5,4},{6,5},{7,6},{8,7},{9,8},{10,9... | collective-permute-start | bytes 61448 | tf_op jit(solution)/shard_map/ppermute | solution.py:20

commit v7 on v6

--- a/solution.py
+++ b/solution.py
@@ -67,7 +67,8 @@
 
 def ask_low_kernel(slot_hbm, table_hbm, vw_hbm, state_hbm, inv_ref, vw_ref, table_ref, state_ref, *refs):
     *out_refs, slot_ref, sems = refs
-    members, levels, cells = state_hbm.shape
+    levels, cells = state_hbm.shape[1:]
+    members = state_ref.shape[0]
     pairs = [(slot_hbm, slot_ref), (vw_hbm, vw_ref), (table_hbm, table_ref)]
     for m in range(0, members, 2):
         pairs.append((state_hbm.at[pl.ds(m, 2)], state_ref.at[pl.ds(m, 2), pl.ds(0, levels), :]))
@@ -100,7 +101,7 @@
             out[:, part * TILE : (part + 1) * TILE] = slot_weights(inv_ref, vw_ref, tile, table_ref)
 
 
-def answer_tile(cell_of, w, turned_ref, cells_dim):
+def answer_tile(pair_of, w, turned_ref, cells_dim):
     S, rest = row_stride(cells_dim), member_row(cells_dim, 8)
     half = TILE // 2
     lane = lax.broadcasted_iota(jnp.int32, (8, 128), 1)
@@ -111,10 +112,11 @@
     parts = []
     for o in range(half // 8):
         sides = []
+        pairs = [pair_of(8 * o + j) for j in range(8)]
         for h in range(2):
             a_rows, b_rows = [], []
             for j in range(8):
-                c = cell_of(h * half + 8 * o + j)
+                c = pairs[j][h]
                 a_rows.append(turned_ref[pl.ds(c, 8, stride=S), :])
                 b_rows.append(turned_ref[pl.ds(c + rest, 2, stride=S), :])
             sides.append(jnp.concatenate(a_rows + b_rows, axis=0).astype(BF16))
@@ -136,16 +138,30 @@
     return jnp.concatenate([jnp.concatenate(out_a, axis=1), jnp.concatenate(out_b, axis=1)], axis=0)
 
 
-def own_kernel(state_ref, table_hbm, w_ref, turned_ref, eq_ref, cell_ref, cell_sem):
-    members, levels, cells = state_ref.shape
+def own_kernel(first_ref, state_hbm, table_hbm, w_ref, turned_ref, eq_ref, rest_ref, cell_ref, cell_sem, sems):
+    members, levels, cells = state_hbm.shape
+    early = first_ref.shape[0]
+    for m in range(members - early):
+        rest_ref[m, levels:, :] = jnp.zeros((rest_ref.shape[1] - levels, cells), BF16)
+    late = [
+        pltpu.make_async_copy(
+            state_hbm.at[pl.ds(m, 2)], rest_ref.at[pl.ds(m - early, 2), pl.ds(0, levels), :], sems.at[(m - early) // 2]
+        )
+        for m in range(early, members, 2)
+    ]
+    for each in late:
+        each.start()
     copy = pltpu.make_async_copy(table_hbm.at[:, pl.ds(0, eq_ref.shape[1])], cell_ref, cell_sem)
     copy.start()
     r = lax.broadcasted_iota(jnp.int32, (TILE, TILE), 0)
     eye = jnp.where(r == lax.broadcasted_iota(jnp.int32, (TILE, TILE), 1), 1.0, 0.0).astype(BF16)
     for m in range(0, members, 2):
+        state_ref, n = (first_ref, m) if m < early else (rest_ref, m - early)
+        if m >= early:
+            late[n // 2].wait()
         for part in range(cells // TILE):
             at = slice(part * TILE, (part + 1) * TILE)
-            block = jnp.concatenate([state_ref[m, :, at], state_ref[m + 1, :, at]], axis=0)
+            block = jnp.concatenate([state_ref[n, :, at], state_ref[n + 1, :, at]], axis=0)
             flat = lax.dot_general(eye, block, NT, preferred_element_type=F32)
             for i in range(2):
                 low = member_row(cells, m + i) + part * TILE
@@ -153,7 +169,12 @@
     copy.wait()
     for tile in range(eq_ref.shape[1] // TILE):
         at = slice(tile * TILE, (tile + 1) * TILE)
-        eq_ref[:, at] = answer_tile(lambda i: cell_ref[0, tile * TILE + i], w_ref[:, at], turned_ref, cells)
+        eq_ref[:, at] = answer_tile(
+            lambda i: (cell_ref[0, tile * TILE + i], cell_ref[0, tile * TILE + TILE // 2 + i]),
+            w_ref[:, at],
+            turned_ref,
+            cells,
+        )
 
 
 def answer_kernel(levels, cells, turned_ref, w_ref, before_ref, eq_ref):
@@ -165,7 +186,14 @@
         at = slice(tile * TILE, (tile + 1) * TILE)
         w = w_ref[:, at]
         w = jnp.where(keep, w, jnp.zeros_like(w))
-        eq_ref[:, at] = answer_tile(lambda j: words[0, tile * TILE + j], w, turned_ref, cells)
+        mid = tile * TILE + TILE // 2
+        both = words[:, tile * TILE : mid] + (words[:, mid : mid + TILE // 2] << 16)
+
+        def pair_of(j):
+            word = both[0, j]
+            return word & 0xFFFF, word >> 16
+
+        eq_ref[:, at] = answer_tile(pair_of, w, turned_ref, cells)
 
 
 def combine_kernel(firsts, slot_ref, hw_ref, *refs):
@@ -294,6 +322,7 @@
     far = lambda x: pltpu.with_memory_space_constraint(x, pltpu.HBM)
     params = pltpu.CompilerParams(vmem_limit_bytes=16 * 1024 * 1024)
 
+    early = mem_dev - 4
     w_shape = jax.ShapeDtypeStruct((128, halo), BF16)
     inv, vw_near, table, state_near, ask_m2, ask_m1 = pl.pallas_call(
         ask_low_kernel,
@@ -301,13 +330,13 @@
             pltpu.VMEM((neigh * obs // 128, 128), jnp.int32),
             pltpu.VMEM((levels, obs), BF16),
             pltpu.VMEM((1, neigh * obs), jnp.int32),
-            pltpu.VMEM((mem_dev, 128, cells), BF16),
+            pltpu.VMEM((early, 128, cells), BF16),
             w_shape,
             w_shape,
         ],
         in_specs=[ANY] * 4,
         out_specs=[VMEM] * 6,
-        scratch_shapes=[pltpu.VMEM((neigh, obs), jnp.int32), pltpu.SemaphoreType.DMA((3 + mem_dev // 2,))],
+        scratch_shapes=[pltpu.VMEM((neigh, obs), jnp.int32), pltpu.SemaphoreType.DMA((3 + early // 2,))],
         compiler_params=params,
         cost_estimate=pl.CostEstimate(flops=2_000_000_000, bytes_accessed=6_000_000, transcendentals=0),
         name="ask_low",
@@ -329,13 +358,18 @@
             pltpu.VMEM((mem_dev * row_stride(cells), 128), F32),
             pltpu.VMEM((16, obs), F32),
         ],
-        in_specs=[VMEM, ANY, VMEM],
+        in_specs=[VMEM, ANY, ANY, VMEM],
         out_specs=[VMEM] * 2,
-        scratch_shapes=[pltpu.SMEM((1, obs), jnp.int32), pltpu.SemaphoreType.DMA],
+        scratch_shapes=[
+            pltpu.VMEM((mem_dev - early, 128, cells), BF16),
+            pltpu.SMEM((1, obs), jnp.int32),
+            pltpu.SemaphoreType.DMA,
+            pltpu.SemaphoreType.DMA((2,)),
+        ],
         compiler_params=params,
         cost_estimate=pl.CostEstimate(flops=8_000_000_000, bytes_accessed=10_000_000, transcendentals=0),
         name="own",
-    )(state_near, far(request_cell), w_own)
+    )(state_near, far(state_t), far(request_cell), w_own)
     turned = pltpu.with_memory_space_constraint(turned, pltpu.VMEM)
     answer = pl.pallas_call(
         lambda *refs: answer_kernel(levels, cells, *refs),

time: 47.8 us -> 48.3 us (1.010)
  waiting for transfers between devices: 9.08 us -> 7.61 us
  starting transfers between devices: 23.7 us -> 24.9 us
  Pallas kernels: 14 us -> 14.8 us
    pallas_call x1, Pallas kernels: 2.67 us -> 4.24 us  [on_device(): pl.pallas_call(own_kernel, out_shape=[pltpu.VMEM((mem_dev * row_stride(ce...]
    ppermute x10, waiting for transfers between devices: 5.91 us -> 4.44 us  [passed_along(): lax.ppermute(x, axis, [(i, (i + by) % devices) for i in range(devices)])]
    ppermute x10, starting transfers between devices: 19.5 us -> 20.8 us  [passed_along(): lax.ppermute(x, axis, [(i, (i + by) % devices) for i in range(devices)])]
  transfers between devices with their start and end apart: 13 -> 13, of which waited for: 5 -> 5; matrix products, arithmetic and copies ran while one was open for 0% -> 0% of each run, Pallas kernels for 20% -> 22%
where the time goes in v7:
time: 48.3 us; the launch traced here: 48.1 us
  starting transfers between devices  24.9 us (52%)
  Pallas kernels  14.8 us (31%)
  waiting for transfers between devices  7.61 us (16%)
  between operations  0.77 us (2%)
    ppermute x10, starting transfers between devices, passed_along(): lax.ppermute(x, axis, [(i, (i + by) % devices) for i in range(devices)])  20.8 us
    ppermute x10, waiting for transfers between devices, passed_along(): lax.ppermute(x, axis, [(i, (i + by) % devices) for i in range(devices)])  4.44 us
    pallas_call x1, Pallas kernels, on_device(): pl.pallas_call(own_kernel, out_shape=[pltpu.VMEM((mem_dev * row_stride(ce...  4.24 us
    ppermute x3, starting transfers between devices, swapped(): lax.ppermute(x, axis, [(i, i ^ mask) for i in range(lax.axis_size(axis))])  4.18 us
    ppermute x3, waiting for transfers between devices, swapped(): lax.ppermute(x, axis, [(i, i ^ mask) for i in range(lax.axis_size(axis))])  3.17 us
    pallas_call x1, Pallas kernels, on_device(): pl.pallas_call(ask_low_kernel, out_shape=[pltpu.VMEM((neigh * obs // 128,...  2.34 us
    pallas_call x2, Pallas kernels, combine(): pl.pallas_call(lambda *refs: combine_kernel(firsts, *refs), out_shape=jax...  1.69 us
    pallas_call x1, Pallas kernels, on_device(): sent_m2 = answer(turned, w_m2, eq_own)  1.07 us
  transfers between devices with their start and end apart: 13, of which 5 were waited for; matrix products, arithmetic and copies ran while one was open for 0% of the time, Pallas kernels for 22%

profile of v7, /device:TPU:4, one launch (start us, length us, event | category | flops | bytes accessed | tf_op | source)
XLA Modules:
  0.0 48.1 jit_solution(13254676212577163743)
XLA Ops:
  0.6 2.3 %ask_low.1 = (s32[32,128]{1,0:T(8,128)S(1)}, bf16[120,1024]{1,0:T(8,128)(2,1)S(1)}, s32[1,4096]{1,0:T(1,128)S(1)}, bf16[6,128,2048]{2,1,0:T(8,128)(2,1)S(1)}, bf...) custom-call(s32[4,1024]{1,0:T(4,128)} %bitcast.11, s32[1,4096]{1,0:T(1,128)} %table_hbm.3, ...), custom_call_target="tpu_custom_call" | custom-call | flops 2000000000 | bytes 6000000 | tf_op jit(solution)/shard_map/ask_low/pallas_call | solution.py:327
  3.0 8.4 %collective-permute-start = (bf16[128,768]{1,0:T(8,128)(2,1)S(1)}, bf16[128,768]{1,0:T(8,128)(2,1)S(1)}, u32[]{:S(2)}, u32[]{:S(2)}) collective-permute-start(bf16[128,768]{1,0:T(8,128)(2,1)S(1)} %get-tuple-element.25), channel_id=1, source_target_pairs={{0,62},{1,63},{2,0},{3,1},{4,2},{5,3},{6,4},{7,5},{8,6},{9,7},{10,... | collective-permute-start | bytes 589832 | tf_op jit(solution)/shard_map/ppermute | solution.py:20
  11.4 0.2 collective-permute-start.2
  11.5 0.9 %ask_high.1 = (bf16[128,1024]{1,0:T(8,128)(2,1)S(1)}, bf16[128,768]{1,0:T(8,128)(2,1)S(1)}, bf16[128,768]{1,0:T(8,128)(2,1)S(1)}) custom-call(s32[32,128]{1,0:T(8,128)S(1)} %get-tuple-element.19.inv_ref, bf16[120,1024]{1,0:T(8,128)(2,1)S(1)} %get-tuple-element.20.vw_ref, s32[1,4096]{1,0:T(1,128)S(1)} %get-tuple-element.21.table_ref), custom_call_target="tpu_custom_call" | custom-call | flops 2000000000 | bytes 1000000 | tf_op jit(solution)/shard_map/ask_high/pallas_call | solution.py:345
  12.4 0.4 collective-permute-start.4
  12.8 0.8 %collective-permute-start.6 = (bf16[128,768]{1,0:T(8,128)(2,1)S(1)}, bf16[128,768]{1,0:T(8,128)(2,1)S(1)}, u32[]{:S(2)}, u32[]{:S(2)}) collective-permute-start(bf16[128,768]{1,0:T(8,128)(2,1)S(1)} %get-tuple-element.28), channel_id=1, source_target_pairs={{0,2},{1,3},{2,4},{3,5},{4,6},{5,7},{6,8},{7,9},{8,10},{9,11},{10,... | collective-permute-start | bytes 589832 | tf_op jit(solution)/shard_map/ppermute | solution.py:20
  13.6 4.2 %own.1 = (f32[20520,128]{1,0:T(8,128)S(1)}, f32[16,1024]{1,0:T(8,128)S(1)}) custom-call(bf16[6,128,2048]{2,1,0:T(8,128)(2,1)S(1)} %get-tuple-element.18.first_ref, bf16[10,120,2048]{2,1,0:T(8,128)(2,1)} %bitcast.17, s32[1,4096]{1,0:T(1,128)} %table_hbm.3, bf16[128,1024]{1,0:T(8,128)(2,1)S(1)} %get-tuple-element.22.w_ref), custom_call_target="tpu_custom_call" | custom-call | flops 8000000000 | bytes 10000000 | tf_op jit(solution)/shard_map/own/pallas_call | solution.py:355
  17.9 0.0 collective-permute-done.refs_1_
  17.9 1.1 %answer.4.refs_2_ = f32[16,768]{1,0:T(8,128)S(1)} custom-call(f32[20520,128]{1,0:T(8,128)S(1)} %get-tuple-element.24.refs_0_, bf16[128,768]{1,0:T(8,128)(2,1)S(1)} %collective-permute-done.refs_1_, f32[16,1024]{1,0:T(8,128)S(1)} %get-tuple-element.23.refs_2_), custom_call_target="tpu_custom_call" | custom-call | flops 2000000000 | bytes 1000000 | tf_op jit(solution)/shard_map/answer/pallas_call | solution.py:383
  18.9 0.1 collective-permute-start.1
  19.0 0.0 collective-permute-done.2.refs_1_
  19.0 1.1 %answer.5.refs_2_ = f32[16,768]{1,0:T(8,128)S(1)} custom-call(f32[20520,128]{1,0:T(8,128)S(1)} %get-tuple-element.24.refs_0_, bf16[128,768]{1,0:T(8,128)(2,1)S(1)} %collective-permute-done.2.refs_1_, f32[16,768]{1,0:T(8,128)S(1)} %answer.4.refs_2_), custom_call_target="tpu_custom_call" | custom-call | flops 2000000000 | bytes 1000000 | tf_op jit(solution)/shard_map/answer/pallas_call | solution.py:385
  20.1 0.3 collective-permute-start.3
  20.4 1.7 %collective-permute-done.4.refs_1_ = bf16[128,768]{1,0:T(8,128)(2,1)S(1)} collective-permute-done((bf16[128,768]{1,0:T(8,128)(2,1)S(1)}, bf16[128,768]{1,0:T(8,128)(2,1)S(1)}, u32[]{:S(2)}, u32[]{:S(2)}) %collective-permute-start.4) | collective-permute-done | bytes 196640 | tf_op jit(solution)/shard_map/ppermute | solution.py:20
  22.1 1.1 %answer.6.refs_2_ = f32[16,768]{1,0:T(8,128)S(1)} custom-call(f32[20520,128]{1,0:T(8,128)S(1)} %get-tuple-element.24.refs_0_, bf16[128,768]{1,0:T(8,128)(2,1)S(1)} %collective-permute-done.4.refs_1_, f32[16,768]{1,0:T(8,128)S(1)} %answer.5.refs_2_), custom_call_target="tpu_custom_call" | custom-call | flops 2000000000 | bytes 1000000 | tf_op jit(solution)/shard_map/answer/pallas_call | solution.py:387
  23.2 0.0 copy-start.3
  23.2 0.0 copy-start.4
  23.2 3.4 %collective-permute-start.5 = (f32[16,768]{1,0:T(8,128)S(1)}, f32[16,768]{1,0:T(8,128)S(1)}, u32[]{:S(2)}, u32[]{:S(2)}) collective-permute-start(f32[16,768]{1,0:T(8,128)S(1)} %answer.6.refs_2_), channel_id=1, source_target_pairs={{0,63},{1,0},{2,1},{3,2},{4,3},{5,4},{6,5},{7,6},{8,7},{9,8},{10,9... | collective-permute-start | bytes 147464 | tf_op jit(solution)/shard_map/ppermute | solution.py:20
  26.6 0.0 collective-permute-done.6.refs_1_
  26.6 1.1 %answer.7 = f32[16,768]{1,0:T(8,128)S(1)} custom-call(f32[20520,128]{1,0:T(8,128)S(1)} %get-tuple-element.24.refs_0_, bf16[128,768]{1,0:T(8,128)(2,1)S(1)} %collective-permute-done.6.refs_1_, f32[16,768]{1,0:T(8,128)S(1)} %answer.6.refs_2_), custom_call_target="tpu_custom_call" | custom-call | flops 2000000000 | bytes 1000000 | tf_op jit(solution)/shard_map/answer/pallas_call | solution.py:389
  27.7 0.0 copy-start
  27.7 0.0 copy-start.1
  27.7 0.0 copy-start.2
  27.7 2.1 %collective-permute-start.7 = (f32[16,768]{1,0:T(8,128)S(1)}, f32[16,768]{1,0:T(8,128)S(1)}, u32[]{:S(2)}, u32[]{:S(2)}) collective-permute-start(f32[16,768]{1,0:T(8,128)S(1)} %answer.7), channel_id=1, source_target_pairs={{0,62},{1,63},{2,0},{3,1},{4,2},{5,3},{6,4},{7,5},{8,6},{9,7},{10,... | collective-permute-start | bytes 147464 | tf_op jit(solution)/shard_map/ppermute | solution.py:20
  29.8 0.0 collective-permute-done.3.refs_4_
  29.8 0.0 collective-permute-done.1.refs_3_
  29.8 0.0 copy-done.3
  29.8 0.0 copy-done.4
  29.8 1.0 %combine.2.refs_2_ = f32[8,1280]{1,0:T(8,128)S(1)} custom-call(s32[4,1024]{1,0:T(4,128)S(1)} %bitcast.12, f32[4,1024]{1,0:T(4,128)S(1)} %bitcast.14, f32[16,1024]{1,0:T(8,128)S(1)} %get-tuple-element.23.refs_2_, f32[16,768]{1,0:T(8,128)S(1)} %collective-permute-done.1.refs_3_, f32[16,768]{1,0:T(8,128)S(1)} %collective-permute-done.3.refs_4_), custom_call_target="tpu_custom_call" | custom-call | flops 1000000000 | bytes 1000000 | tf_op jit(solution)/shard_map/combine/pallas_call | solution.py:394
  30.8 1.0 %collective-permute-done.7.refs_4_ = f32[16,768]{1,0:T(8,128)S(1)} collective-permute-done((f32[16,768]{1,0:T(8,128)S(1)}, f32[16,768]{1,0:T(8,128)S(1)}, u32[]{:S(2)}, u32[]{:S(2)}) %collective-permute-start.7) | collective-permute-done | bytes 49184 | tf_op jit(solution)/shard_map/ppermute | solution.py:20
  31.9 0.0 collective-permute-done.5.refs_3_
  31.9 0.7 %combine.3.refs_0_ = f32[8,1280]{1,0:T(8,128)S(1)} custom-call(s32[4,1024]{1,0:T(4,128)S(1)} %bitcast.13, f32[4,1024]{1,0:T(4,128)S(1)} %bitcast.15, f32[8,1280]{1,0:T(8,128)S(1)} %combine.2.refs_2_, f32[16,768]{1,0:T(8,128)S(1)} %collective-permute-done.5.refs_3_, f32[16,768]{1,0:T(8,128)S(1)} %collective-permute-done.7.refs_4_), custom_call_target="tpu_custom_call" | custom-call | flops 1000000000 | bytes 1000000 | tf_op jit(solution)/shard_map/combine/pallas_call | solution.py:394
  32.6 0.6 %collective-permute-start.10 = (f32[8,1280]{1,0:T(8,128)S(1)}, f32[8,1280]{1,0:T(8,128)S(1)}, u32[]{:S(2)}, u32[]{:S(2)}) collective-permute-start(f32[8,1280]{1,0:T(8,128)S(1)} %combine.3.refs_0_), channel_id=1, source_target_pairs={{0,192},{64,128},{128,64},{192,0},{1,193},{65,129},{129,65},{193,1... | collective-permute-start | bytes 122888 | tf_op jit(solution)/shard_map/ppermute | solution.py:24
  33.2 2.7 %collective-permute-start.9 = (f32[8,1280]{1,0:T(8,128)S(1)}, f32[8,1280]{1,0:T(8,128)S(1)}, u32[]{:S(2)}, u32[]{:S(2)}) collective-permute-start(f32[8,1280]{1,0:T(8,128)S(1)} %combine.3.refs_0_), channel_id=1, source_target_pairs={{0,128},{64,192},{128,0},{192,64},{1,129},{65,193},{129,1},{193,65... | collective-permute-start | bytes 122888 | tf_op jit(solution)/shard_map/ppermute | solution.py:24
  35.9 0.8 %collective-permute-start.8 = (f32[8,1280]{1,0:T(8,128)S(1)}, f32[8,1280]{1,0:T(8,128)S(1)}, u32[]{:S(2)}, u32[]{:S(2)}) collective-permute-start(f32[8,1280]{1,0:T(8,128)S(1)} %combine.3.refs_0_), channel_id=1, source_target_pairs={{0,64},{64,0},{128,192},{192,128},{1,65},{65,1},{129,193},{193,129... | collective-permute-start | bytes 122888 | tf_op jit(solution)/shard_map/ppermute | solution.py:24
  36.7 0.0 collective-permute-done.10.refs_3_
  36.7 1.9 %collective-permute-done.9.refs_2_ = f32[8,1280]{1,0:T(8,128)S(1)} collective-permute-done((f32[8,1280]{1,0:T(8,128)S(1)}, f32[8,1280]{1,0:T(8,128)S(1)}, u32[]{:S(2)}, u32[]{:S(2)}) %collective-permute-start.9) | collective-permute-done | bytes 40992 | tf_op jit(solution)/shard_map/ppermute | solution.py:24
  38.7 1.2 %collective-permute-done.8.refs_1_ = f32[8,1280]{1,0:T(8,128)S(1)} collective-permute-done((f32[8,1280]{1,0:T(8,128)S(1)}, f32[8,1280]{1,0:T(8,128)S(1)}, u32[]{:S(2)}, u32[]{:S(2)}) %collective-permute-start.8) | collective-permute-done | bytes 40992 | tf_op jit(solution)/shard_map/ppermute | solution.py:24
  39.9 0.0 copy-done
  39.9 0.0 copy-done.1
  39.9 0.0 copy-done.2
  39.9 0.6 %cov.1 = (f32[80,64]{1,0:T(8,128)S(1)}, f32[80,64]{1,0:T(8,128)S(1)}, f32[80,64]{1,0:T(8,128)S(1)}) custom-call(f32[8,1280]{1,0:T(8,128)S(1)} %combine.3.refs_0_, f32[8,1280]{1,0:T(8,128)S(1)} %collective-permute-done.8.refs_1_, f32[8,1280]{1,0:T(8,128)S(1)} %collective-permute-done.9.refs_2_, f32[8,1280]{1,0:T(8,128)S(1)} %collective-permute-done.10.refs_3_, ...), custom_call_target="tpu_custom_call" | custom-call | tf_op jit(solution)/shard_map/cov/pallas_call | solution.py:408
  40.5 0.1 collective-permute-start.11
  40.6 5.1 %collective-permute-start.12 = (f32[80,64]{1,0:T(8,128)S(1)}, f32[80,64]{1,0:T(8,128)S(1)}, u32[]{:S(2)}, u32[]{:S(2)}) collective-permute-start(f32[80,64]{1,0:T(8,128)S(1)} %get-tuple-element.31), channel_id=1, source_target_pairs={{0,63},{1,0},{2,1},{3,2},{4,3},{5,4},{6,5},{7,6},{8,7},{9,8},{10,9... | collective-permute-start | bytes 61448 | tf_op jit(solution)/shard_map/ppermute | solution.py:20
  45.7 1.7 %collective-permute-done.11.a_ref = f32[80,64]{1,0:T(8,128)S(1)} collective-permute-done((f32[80,64]{1,0:T(8,128)S(1)}, f32[80,64]{1,0:T(8,128)S(1)}, u32[]{:S(2)}, u32[]{:S(2)}) %collective-permute-start.11) | collective-permute-done | bytes 20512 | tf_op jit(solution)/shard_map/ppermute | solution.py:20
  47.3 0.0 collective-permute-done.12.b_ref
  47.3 0.8 %final.1 = (f32[10,8,40]{2,1,0:T(8,128)}, f32[8,10]{1,0:T(8,128)}) custom-call(f32[80,64]{1,0:T(8,128)S(1)} %get-tuple-element.29.mid_ref, f32[80,64]{1,0:T(8,128)S(1)} %collective-permute-done.11.a_ref, f32[80,64]{1,0:T(8,128)S(1)} %collective-permute-done.12.b_ref), custom_call_target="tpu_custom_call" | custom-call | tf_op jit(solution)/shard_map/final/pallas_call | solution.py:418
Async XLA Ops:
  3.0 14.9 %collective-permute-start = (bf16[128,768]{1,0:T(8,128)(2,1)S(1)}, bf16[128,768]{1,0:T(8,128)(2,1)S(1)}, u32[]{:S(2)}, u32[]{:S(2)}) collective-permute-start(bf16[128,768]{1,0:T(8,128)(2,1)S(1)} %get-tuple-element.25), channel_id=1, source_target_pairs={{0,62},{1,63},{2,0},{3,1},{4,2},{5,3},{6,4},{7,5},{8,6},{9,7},{10,... | collective-permute-start | bytes 589832 | tf_op jit(solution)/shard_map/ppermute | solution.py:20
  11.4 7.7 %collective-permute-start.2 = (bf16[128,768]{1,0:T(8,128)(2,1)S(1)}, bf16[128,768]{1,0:T(8,128)(2,1)S(1)}, u32[]{:S(2)}, u32[]{:S(2)}) collective-permute-start(bf16[128,768]{1,0:T(8,128)(2,1)S(1)} %get-tuple-element.26), channel_id=1, source_target_pairs={{0,63},{1,0},{2,1},{3,2},{4,3},{5,4},{6,5},{7,6},{8,7},{9,8},{10,9... | collective-permute-start | bytes 589832 | tf_op jit(solution)/shard_map/ppermute | solution.py:20
  12.4 9.7 %collective-permute-start.4 = (bf16[128,768]{1,0:T(8,128)(2,1)S(1)}, bf16[128,768]{1,0:T(8,128)(2,1)S(1)}, u32[]{:S(2)}, u32[]{:S(2)}) collective-permute-start(bf16[128,768]{1,0:T(8,128)(2,1)S(1)} %get-tuple-element.27), channel_id=1, source_target_pairs={{0,1},{1,2},{2,3},{3,4},{4,5},{5,6},{6,7},{7,8},{8,9},{9,10},{10,1... | collective-permute-start | bytes 589832 | tf_op jit(solution)/shard_map/ppermute | solution.py:20
  12.8 13.8 %collective-permute-start.6 = (bf16[128,768]{1,0:T(8,128)(2,1)S(1)}, bf16[128,768]{1,0:T(8,128)(2,1)S(1)}, u32[]{:S(2)}, u32[]{:S(2)}) collective-permute-start(bf16[128,768]{1,0:T(8,128)(2,1)S(1)} %get-tuple-element.28), channel_id=1, source_target_pairs={{0,2},{1,3},{2,4},{3,5},{4,6},{5,7},{6,8},{7,9},{8,10},{9,11},{10,... | collective-permute-start | bytes 589832 | tf_op jit(solution)/shard_map/ppermute | solution.py:20
  18.9 10.9 %collective-permute-start.1 = (f32[16,768]{1,0:T(8,128)S(1)}, f32[16,768]{1,0:T(8,128)S(1)}, u32[]{:S(2)}, u32[]{:S(2)}) collective-permute-start(f32[16,768]{1,0:T(8,128)S(1)} %answer.4.refs_2_), channel_id=1, source_target_pairs={{0,2},{1,3},{2,4},{3,5},{4,6},{5,7},{6,8},{7,9},{8,10},{9,11},{10,... | collective-permute-start | bytes 147464 | tf_op jit(solution)/shard_map/ppermute | solution.py:20
  20.1 9.7 %collective-permute-start.3 = (f32[16,768]{1,0:T(8,128)S(1)}, f32[16,768]{1,0:T(8,128)S(1)}, u32[]{:S(2)}, u32[]{:S(2)}) collective-permute-start(f32[16,768]{1,0:T(8,128)S(1)} %answer.5.refs_2_), channel_id=1, source_target_pairs={{0,1},{1,2},{2,3},{3,4},{4,5},{5,6},{6,7},{7,8},{8,9},{9,10},{10,1... | collective-permute-start | bytes 147464 | tf_op jit(solution)/shard_map/ppermute | solution.py:20
  23.2 6.6 %copy-start.3 = (s32[1024,4]{0,1:T(4,128)S(1)}, s32[1024,4]{0,1:T(4,128)}, u32[]{:S(2)}) copy-start(s32[1024,4]{0,1:T(4,128)} %param.11) | copy-start | bytes 49156
  23.2 6.6 %copy-start.4 = (f32[1024,4]{0,1:T(4,128)S(1)}, f32[1024,4]{0,1:T(4,128)}, u32[]{:S(2)}) copy-start(f32[1024,4]{0,1:T(4,128)} %param.10) | copy-start | bytes 49156
  23.2 8.7 %collective-permute-start.5 = (f32[16,768]{1,0:T(8,128)S(1)}, f32[16,768]{1,0:T(8,128)S(1)}, u32[]{:S(2)}, u32[]{:S(2)}) collective-permute-start(f32[16,768]{1,0:T(8,128)S(1)} %answer.6.refs_2_), channel_id=1, source_target_pairs={{0,63},{1,0},{2,1},{3,2},{4,3},{5,4},{6,5},{7,6},{8,7},{9,8},{10,9... | collective-permute-start | bytes 147464 | tf_op jit(solution)/shard_map/ppermute | solution.py:20
  27.7 12.2 %copy-start = (f32[1024]{0:T(1024)S(1)}, f32[1024]{0:T(1024)}, u32[]{:S(2)}) copy-start(f32[1024]{0:T(1024)} %param.13) | copy-start | bytes 12292
  27.7 12.2 %copy-start.1 = (f32[1024]{0:T(1024)S(1)}, f32[1024]{0:T(1024)}, u32[]{:S(2)}) copy-start(f32[1024]{0:T(1024)} %param.14) | copy-start | bytes 12292
  27.7 12.2 %copy-start.2 = (s32[1024]{0:T(1024)S(1)}, s32[1024]{0:T(1024)}, u32[]{:S(2)}) copy-start(s32[1024]{0:T(1024)} %param.15) | copy-start | bytes 12292
  27.7 4.2 %collective-permute-start.7 = (f32[16,768]{1,0:T(8,128)S(1)}, f32[16,768]{1,0:T(8,128)S(1)}, u32[]{:S(2)}, u32[]{:S(2)}) collective-permute-start(f32[16,768]{1,0:T(8,128)S(1)} %answer.7), channel_id=1, source_target_pairs={{0,62},{1,63},{2,0},{3,1},{4,2},{5,3},{6,4},{7,5},{8,6},{9,7},{10,... | collective-permute-start | bytes 147464 | tf_op jit(solution)/shard_map/ppermute | solution.py:20
  32.6 4.2 %collective-permute-start.10 = (f32[8,1280]{1,0:T(8,128)S(1)}, f32[8,1280]{1,0:T(8,128)S(1)}, u32[]{:S(2)}, u32[]{:S(2)}) collective-permute-start(f32[8,1280]{1,0:T(8,128)S(1)} %combine.3.refs_0_), channel_id=1, source_target_pairs={{0,192},{64,128},{128,64},{192,0},{1,193},{65,129},{129,65},{193,1... | collective-permute-start | bytes 122888 | tf_op jit(solution)/shard_map/ppermute | solution.py:24
  33.2 5.5 %collective-permute-start.9 = (f32[8,1280]{1,0:T(8,128)S(1)}, f32[8,1280]{1,0:T(8,128)S(1)}, u32[]{:S(2)}, u32[]{:S(2)}) collective-permute-start(f32[8,1280]{1,0:T(8,128)S(1)} %combine.3.refs_0_), channel_id=1, source_target_pairs={{0,128},{64,192},{128,0},{192,64},{1,129},{65,193},{129,1},{193,65... | collective-permute-start | bytes 122888 | tf_op jit(solution)/shard_map/ppermute | solution.py:24
  35.9 4.0 %collective-permute-start.8 = (f32[8,1280]{1,0:T(8,128)S(1)}, f32[8,1280]{1,0:T(8,128)S(1)}, u32[]{:S(2)}, u32[]{:S(2)}) collective-permute-start(f32[8,1280]{1,0:T(8,128)S(1)} %combine.3.refs_0_), channel_id=1, source_target_pairs={{0,64},{64,0},{128,192},{192,128},{1,65},{65,1},{129,193},{193,129... | collective-permute-start | bytes 122888 | tf_op jit(solution)/shard_map/ppermute | solution.py:24
  40.5 6.8 %collective-permute-start.11 = (f32[80,64]{1,0:T(8,128)S(1)}, f32[80,64]{1,0:T(8,128)S(1)}, u32[]{:S(2)}, u32[]{:S(2)}) collective-permute-start(f32[80,64]{1,0:T(8,128)S(1)} %get-tuple-element.30), channel_id=1, source_target_pairs={{0,1},{1,2},{2,3},{3,4},{4,5},{5,6},{6,7},{7,8},{8,9},{9,10},{10,1... | collective-permute-start | bytes 61448 | tf_op jit(solution)/shard_map/ppermute | solution.py:20
  40.6 6.7 %collective-permute-start.12 = (f32[80,64]{1,0:T(8,128)S(1)}, f32[80,64]{1,0:T(8,128)S(1)}, u32[]{:S(2)}, u32[]{:S(2)}) collective-permute-start(f32[80,64]{1,0:T(8,128)S(1)} %get-tuple-element.31), channel_id=1, source_target_pairs={{0,63},{1,0},{2,1},{3,2},{4,3},{5,4},{6,5},{7,6},{8,7},{9,8},{10,9... | collective-permute-start | bytes 61448 | tf_op jit(solution)/shard_map/ppermute | solution.py:20

commit v8 on v6

--- a/solution.py
+++ b/solution.py
@@ -100,7 +100,7 @@
             out[:, part * TILE : (part + 1) * TILE] = slot_weights(inv_ref, vw_ref, tile, table_ref)
 
 
-def answer_tile(cell_of, w, turned_ref, cells_dim):
+def answer_tile(pair_of, w, turned_ref, cells_dim):
     S, rest = row_stride(cells_dim), member_row(cells_dim, 8)
     half = TILE // 2
     lane = lax.broadcasted_iota(jnp.int32, (8, 128), 1)
@@ -111,10 +111,11 @@
     parts = []
     for o in range(half // 8):
         sides = []
+        pairs = [pair_of(8 * o + j) for j in range(8)]
         for h in range(2):
             a_rows, b_rows = [], []
             for j in range(8):
-                c = cell_of(h * half + 8 * o + j)
+                c = pairs[j][h]
                 a_rows.append(turned_ref[pl.ds(c, 8, stride=S), :])
                 b_rows.append(turned_ref[pl.ds(c + rest, 2, stride=S), :])
             sides.append(jnp.concatenate(a_rows + b_rows, axis=0).astype(BF16))
@@ -153,7 +154,12 @@
     copy.wait()
     for tile in range(eq_ref.shape[1] // TILE):
         at = slice(tile * TILE, (tile + 1) * TILE)
-        eq_ref[:, at] = answer_tile(lambda i: cell_ref[0, tile * TILE + i], w_ref[:, at], turned_ref, cells)
+        eq_ref[:, at] = answer_tile(
+            lambda i: (cell_ref[0, tile * TILE + i], cell_ref[0, tile * TILE + TILE // 2 + i]),
+            w_ref[:, at],
+            turned_ref,
+            cells,
+        )
 
 
 def answer_kernel(levels, cells, turned_ref, w_ref, before_ref, eq_ref):
@@ -165,7 +171,14 @@
         at = slice(tile * TILE, (tile + 1) * TILE)
         w = w_ref[:, at]
         w = jnp.where(keep, w, jnp.zeros_like(w))
-        eq_ref[:, at] = answer_tile(lambda j: words[0, tile * TILE + j], w, turned_ref, cells)
+        mid = tile * TILE + TILE // 2
+        both = words[:, tile * TILE : mid] + (words[:, mid : mid + TILE // 2] << 16)
+
+        def pair_of(j):
+            word = both[0, j]
+            return word & 0xFFFF, word >> 16
+
+        eq_ref[:, at] = answer_tile(pair_of, w, turned_ref, cells)
 
 
 def combine_kernel(firsts, slot_ref, hw_ref, *refs):

time: 47.8 us -> 47.4 us (level)
  waiting for transfers between devices: 9.08 us -> 9.7 us
  Pallas kernels: 14 us -> 13.5 us
  starting transfers between devices: 23.7 us -> 23.2 us
    ppermute x10, waiting for transfers between devices: 5.91 us -> 6.52 us  [passed_along(): lax.ppermute(x, axis, [(i, (i + by) % devices) for i in range(devices)])]
    ppermute x10, starting transfers between devices: 19.5 us -> 19 us  [passed_along(): lax.ppermute(x, axis, [(i, (i + by) % devices) for i in range(devices)])]
  transfers between devices with their start and end apart: 13 -> 13, of which waited for: 5 -> 7; matrix products, arithmetic and copies ran while one was open for 0% -> 0% of each run, Pallas kernels for 20% -> 19%
where the time goes in v8:
time: 47.4 us; the launch traced here: 47.2 us
  starting transfers between devices  23.2 us (49%)
  Pallas kernels  13.5 us (28%)
  waiting for transfers between devices  9.7 us (20%)
  between operations  0.77 us (2%)
    ppermute x10, starting transfers between devices, passed_along(): lax.ppermute(x, axis, [(i, (i + by) % devices) for i in range(devices)])  19 us
    ppermute x10, waiting for transfers between devices, passed_along(): lax.ppermute(x, axis, [(i, (i + by) % devices) for i in range(devices)])  6.52 us
    ppermute x3, starting transfers between devices, swapped(): lax.ppermute(x, axis, [(i, i ^ mask) for i in range(lax.axis_size(axis))])  4.18 us
    ppermute x3, waiting for transfers between devices, swapped(): lax.ppermute(x, axis, [(i, i ^ mask) for i in range(lax.axis_size(axis))])  3.18 us
    pallas_call x1, Pallas kernels, on_device(): pl.pallas_call(own_kernel, out_shape=[pltpu.VMEM((mem_dev * row_stride(ce...  2.68 us
    pallas_call x1, Pallas kernels, on_device(): pl.pallas_call(ask_low_kernel, out_shape=[pltpu.VMEM((neigh * obs // 128,...  2.63 us
    pallas_call x2, Pallas kernels, combine(): pl.pallas_call(lambda *refs: combine_kernel(firsts, *refs), out_shape=jax...  1.69 us
    pallas_call x1, Pallas kernels, on_device(): sent_p2 = answer(turned, w_p2, sent_p1)  1.07 us
  transfers between devices with their start and end apart: 13, of which 7 were waited for; matrix products, arithmetic and copies ran while one was open for 0% of the time, Pallas kernels for 19%

profile of v8, /device:TPU:4, one launch (start us, length us, event | category | flops | bytes accessed | tf_op | source)
XLA Modules:
  0.0 47.2 jit_solution(18325853585893881448)
XLA Ops:
  0.6 2.6 %ask_low.1 = (s32[32,128]{1,0:T(8,128)S(1)}, bf16[120,1024]{1,0:T(8,128)(2,1)S(1)}, s32[1,4096]{1,0:T(1,128)S(1)}, bf16[10,128,2048]{2,1,0:T(8,128)(2,1)S(1)}, b...) custom-call(s32[4,1024]{1,0:T(4,128)} %bitcast.11, s32[1,4096]{1,0:T(1,128)} %table_hbm.3, ...), custom_call_target="tpu_custom_call" | custom-call | flops 2000000000 | bytes 6000000 | tf_op jit(solution)/shard_map/ask_low/pallas_call | solution.py:311
  3.3 8.4 %collective-permute-start = (bf16[128,768]{1,0:T(8,128)(2,1)S(1)}, bf16[128,768]{1,0:T(8,128)(2,1)S(1)}, u32[]{:S(2)}, u32[]{:S(2)}) collective-permute-start(bf16[128,768]{1,0:T(8,128)(2,1)S(1)} %get-tuple-element.25), channel_id=1, source_target_pairs={{0,62},{1,63},{2,0},{3,1},{4,2},{5,3},{6,4},{7,5},{8,6},{9,7},{10,... | collective-permute-start | bytes 589832 | tf_op jit(solution)/shard_map/ppermute | solution.py:20
  11.7 0.2 collective-permute-start.2
  11.8 0.9 %ask_high.1 = (bf16[128,1024]{1,0:T(8,128)(2,1)S(1)}, bf16[128,768]{1,0:T(8,128)(2,1)S(1)}, bf16[128,768]{1,0:T(8,128)(2,1)S(1)}) custom-call(s32[32,128]{1,0:T(8,128)S(1)} %get-tuple-element.19.inv_ref, bf16[120,1024]{1,0:T(8,128)(2,1)S(1)} %get-tuple-element.20.vw_ref, s32[1,4096]{1,0:T(1,128)S(1)} %get-tuple-element.21.table_ref), custom_call_target="tpu_custom_call" | custom-call | flops 2000000000 | bytes 1000000 | tf_op jit(solution)/shard_map/ask_high/pallas_call | solution.py:329
  12.7 0.4 collective-permute-start.4
  13.1 0.8 %collective-permute-start.6 = (bf16[128,768]{1,0:T(8,128)(2,1)S(1)}, bf16[128,768]{1,0:T(8,128)(2,1)S(1)}, u32[]{:S(2)}, u32[]{:S(2)}) collective-permute-start(bf16[128,768]{1,0:T(8,128)(2,1)S(1)} %get-tuple-element.28), channel_id=1, source_target_pairs={{0,2},{1,3},{2,4},{3,5},{4,6},{5,7},{6,8},{7,9},{8,10},{9,11},{10,... | collective-permute-start | bytes 589832 | tf_op jit(solution)/shard_map/ppermute | solution.py:20
  13.9 2.7 %own.1 = (f32[20520,128]{1,0:T(8,128)S(1)}, f32[16,1024]{1,0:T(8,128)S(1)}) custom-call(bf16[10,128,2048]{2,1,0:T(8,128)(2,1)S(1)} %get-tuple-element.18.state_ref, s32[1,4096]{1,0:T(1,128)} %table_hbm.3, bf16[128,1024]{1,0:T(8,128)(2,1)S(1)} %get-tuple-element.22.w_ref), custom_call_target="tpu_custom_call" | custom-call | flops 8000000000 | bytes 10000000 | tf_op jit(solution)/shard_map/own/pallas_call | solution.py:339
  16.6 0.0 collective-permute-done.refs_1_
  16.6 1.1 %answer.4.refs_2_ = f32[16,768]{1,0:T(8,128)S(1)} custom-call(f32[20520,128]{1,0:T(8,128)S(1)} %get-tuple-element.24.refs_0_, bf16[128,768]{1,0:T(8,128)(2,1)S(1)} %collective-permute-done.refs_1_, f32[16,1024]{1,0:T(8,128)S(1)} %get-tuple-element.23.refs_2_), custom_call_target="tpu_custom_call" | custom-call | flops 2000000000 | bytes 1000000 | tf_op jit(solution)/shard_map/answer/pallas_call | solution.py:362
  17.7 0.1 collective-permute-start.1
  17.8 0.1 collective-permute-done.2.refs_1_
  17.9 1.1 %answer.5.refs_2_ = f32[16,768]{1,0:T(8,128)S(1)} custom-call(f32[20520,128]{1,0:T(8,128)S(1)} %get-tuple-element.24.refs_0_, bf16[128,768]{1,0:T(8,128)(2,1)S(1)} %collective-permute-done.2.refs_1_, f32[16,768]{1,0:T(8,128)S(1)} %answer.4.refs_2_), custom_call_target="tpu_custom_call" | custom-call | flops 2000000000 | bytes 1000000 | tf_op jit(solution)/shard_map/answer/pallas_call | solution.py:364
  19.0 0.1 collective-permute-start.3
  19.1 3.3 %collective-permute-done.4.refs_1_ = bf16[128,768]{1,0:T(8,128)(2,1)S(1)} collective-permute-done((bf16[128,768]{1,0:T(8,128)(2,1)S(1)}, bf16[128,768]{1,0:T(8,128)(2,1)S(1)}, u32[]{:S(2)}, u32[]{:S(2)}) %collective-permute-start.4) | collective-permute-done | bytes 196640 | tf_op jit(solution)/shard_map/ppermute | solution.py:20
  22.4 1.1 %answer.6.refs_2_ = f32[16,768]{1,0:T(8,128)S(1)} custom-call(f32[20520,128]{1,0:T(8,128)S(1)} %get-tuple-element.24.refs_0_, bf16[128,768]{1,0:T(8,128)(2,1)S(1)} %collective-permute-done.4.refs_1_, f32[16,768]{1,0:T(8,128)S(1)} %answer.5.refs_2_), custom_call_target="tpu_custom_call" | custom-call | flops 2000000000 | bytes 1000000 | tf_op jit(solution)/shard_map/answer/pallas_call | solution.py:366
  23.5 0.0 copy-start.3
  23.5 0.0 copy-start.4
  23.5 2.2 %collective-permute-start.5 = (f32[16,768]{1,0:T(8,128)S(1)}, f32[16,768]{1,0:T(8,128)S(1)}, u32[]{:S(2)}, u32[]{:S(2)}) collective-permute-start(f32[16,768]{1,0:T(8,128)S(1)} %answer.6.refs_2_), channel_id=1, source_target_pairs={{0,63},{1,0},{2,1},{3,2},{4,3},{5,4},{6,5},{7,6},{8,7},{9,8},{10,9... | collective-permute-start | bytes 147464 | tf_op jit(solution)/shard_map/ppermute | solution.py:20
  25.7 0.0 collective-permute-done.6.refs_1_
  25.7 1.1 %answer.7 = f32[16,768]{1,0:T(8,128)S(1)} custom-call(f32[20520,128]{1,0:T(8,128)S(1)} %get-tuple-element.24.refs_0_, bf16[128,768]{1,0:T(8,128)(2,1)S(1)} %collective-permute-done.6.refs_1_, f32[16,768]{1,0:T(8,128)S(1)} %answer.6.refs_2_), custom_call_target="tpu_custom_call" | custom-call | flops 2000000000 | bytes 1000000 | tf_op jit(solution)/shard_map/answer/pallas_call | solution.py:368
  26.7 0.0 copy-start
  26.7 0.0 copy-start.1
  26.8 0.0 copy-start.2
  26.8 1.7 %collective-permute-start.7 = (f32[16,768]{1,0:T(8,128)S(1)}, f32[16,768]{1,0:T(8,128)S(1)}, u32[]{:S(2)}, u32[]{:S(2)}) collective-permute-start(f32[16,768]{1,0:T(8,128)S(1)} %answer.7), channel_id=1, source_target_pairs={{0,62},{1,63},{2,0},{3,1},{4,2},{5,3},{6,4},{7,5},{8,6},{9,7},{10,... | collective-permute-start | bytes 147464 | tf_op jit(solution)/shard_map/ppermute | solution.py:20
  28.5 0.0 collective-permute-done.3.refs_4_
  28.5 0.0 collective-permute-done.1.refs_3_
  28.5 0.0 copy-done.3
  28.5 0.0 copy-done.4
  28.5 1.0 %combine.2.refs_2_ = f32[8,1280]{1,0:T(8,128)S(1)} custom-call(s32[4,1024]{1,0:T(4,128)S(1)} %bitcast.12, f32[4,1024]{1,0:T(4,128)S(1)} %bitcast.14, f32[16,1024]{1,0:T(8,128)S(1)} %get-tuple-element.23.refs_2_, f32[16,768]{1,0:T(8,128)S(1)} %collective-permute-done.1.refs_3_, f32[16,768]{1,0:T(8,128)S(1)} %collective-permute-done.3.refs_4_), custom_call_target="tpu_custom_call" | custom-call | flops 1000000000 | bytes 1000000 | tf_op jit(solution)/shard_map/combine/pallas_call | solution.py:373
  29.5 1.4 %collective-permute-done.7.refs_4_ = f32[16,768]{1,0:T(8,128)S(1)} collective-permute-done((f32[16,768]{1,0:T(8,128)S(1)}, f32[16,768]{1,0:T(8,128)S(1)}, u32[]{:S(2)}, u32[]{:S(2)}) %collective-permute-start.7) | collective-permute-done | bytes 49184 | tf_op jit(solution)/shard_map/ppermute | solution.py:20
  30.9 0.0 collective-permute-done.5.refs_3_
  30.9 0.7 %combine.3.refs_0_ = f32[8,1280]{1,0:T(8,128)S(1)} custom-call(s32[4,1024]{1,0:T(4,128)S(1)} %bitcast.13, f32[4,1024]{1,0:T(4,128)S(1)} %bitcast.15, f32[8,1280]{1,0:T(8,128)S(1)} %combine.2.refs_2_, f32[16,768]{1,0:T(8,128)S(1)} %collective-permute-done.5.refs_3_, f32[16,768]{1,0:T(8,128)S(1)} %collective-permute-done.7.refs_4_), custom_call_target="tpu_custom_call" | custom-call | flops 1000000000 | bytes 1000000 | tf_op jit(solution)/shard_map/combine/pallas_call | solution.py:373
  31.6 0.6 %collective-permute-start.10 = (f32[8,1280]{1,0:T(8,128)S(1)}, f32[8,1280]{1,0:T(8,128)S(1)}, u32[]{:S(2)}, u32[]{:S(2)}) collective-permute-start(f32[8,1280]{1,0:T(8,128)S(1)} %combine.3.refs_0_), channel_id=1, source_target_pairs={{0,192},{64,128},{128,64},{192,0},{1,193},{65,129},{129,65},{193,1... | collective-permute-start | bytes 122888 | tf_op jit(solution)/shard_map/ppermute | solution.py:24
  32.3 2.7 %collective-permute-start.9 = (f32[8,1280]{1,0:T(8,128)S(1)}, f32[8,1280]{1,0:T(8,128)S(1)}, u32[]{:S(2)}, u32[]{:S(2)}) collective-permute-start(f32[8,1280]{1,0:T(8,128)S(1)} %combine.3.refs_0_), channel_id=1, source_target_pairs={{0,128},{64,192},{128,0},{192,64},{1,129},{65,193},{129,1},{193,65... | collective-permute-start | bytes 122888 | tf_op jit(solution)/shard_map/ppermute | solution.py:24
  35.0 0.8 %collective-permute-start.8 = (f32[8,1280]{1,0:T(8,128)S(1)}, f32[8,1280]{1,0:T(8,128)S(1)}, u32[]{:S(2)}, u32[]{:S(2)}) collective-permute-start(f32[8,1280]{1,0:T(8,128)S(1)} %combine.3.refs_0_), channel_id=1, source_target_pairs={{0,64},{64,0},{128,192},{192,128},{1,65},{65,1},{129,193},{193,129... | collective-permute-start | bytes 122888 | tf_op jit(solution)/shard_map/ppermute | solution.py:24
  35.8 0.1 collective-permute-done.10.refs_3_
  35.9 1.9 %collective-permute-done.9.refs_2_ = f32[8,1280]{1,0:T(8,128)S(1)} collective-permute-done((f32[8,1280]{1,0:T(8,128)S(1)}, f32[8,1280]{1,0:T(8,128)S(1)}, u32[]{:S(2)}, u32[]{:S(2)}) %collective-permute-start.9) | collective-permute-done | bytes 40992 | tf_op jit(solution)/shard_map/ppermute | solution.py:24
  37.8 1.2 %collective-permute-done.8.refs_1_ = f32[8,1280]{1,0:T(8,128)S(1)} collective-permute-done((f32[8,1280]{1,0:T(8,128)S(1)}, f32[8,1280]{1,0:T(8,128)S(1)}, u32[]{:S(2)}, u32[]{:S(2)}) %collective-permute-start.8) | collective-permute-done | bytes 40992 | tf_op jit(solution)/shard_map/ppermute | solution.py:24
  39.0 0.0 copy-done
  39.0 0.0 copy-done.1
  39.0 0.0 copy-done.2
  39.0 0.6 %cov.1 = (f32[80,64]{1,0:T(8,128)S(1)}, f32[80,64]{1,0:T(8,128)S(1)}, f32[80,64]{1,0:T(8,128)S(1)}) custom-call(f32[8,1280]{1,0:T(8,128)S(1)} %combine.3.refs_0_, f32[8,1280]{1,0:T(8,128)S(1)} %collective-permute-done.8.refs_1_, f32[8,1280]{1,0:T(8,128)S(1)} %collective-permute-done.9.refs_2_, f32[8,1280]{1,0:T(8,128)S(1)} %collective-permute-done.10.refs_3_, ...), custom_call_target="tpu_custom_call" | custom-call | tf_op jit(solution)/shard_map/cov/pallas_call | solution.py:387
  39.6 0.1 collective-permute-start.11
  39.7 5.1 %collective-permute-start.12 = (f32[80,64]{1,0:T(8,128)S(1)}, f32[80,64]{1,0:T(8,128)S(1)}, u32[]{:S(2)}, u32[]{:S(2)}) collective-permute-start(f32[80,64]{1,0:T(8,128)S(1)} %get-tuple-element.31), channel_id=1, source_target_pairs={{0,63},{1,0},{2,1},{3,2},{4,3},{5,4},{6,5},{7,6},{8,7},{9,8},{10,9... | collective-permute-start | bytes 61448 | tf_op jit(solution)/shard_map/ppermute | solution.py:20
  44.7 1.7 %collective-permute-done.11.a_ref = f32[80,64]{1,0:T(8,128)S(1)} collective-permute-done((f32[80,64]{1,0:T(8,128)S(1)}, f32[80,64]{1,0:T(8,128)S(1)}, u32[]{:S(2)}, u32[]{:S(2)}) %collective-permute-start.11) | collective-permute-done | bytes 20512 | tf_op jit(solution)/shard_map/ppermute | solution.py:20
  46.4 0.0 collective-permute-done.12.b_ref
  46.4 0.8 %final.1 = (f32[10,8,40]{2,1,0:T(8,128)}, f32[8,10]{1,0:T(8,128)}) custom-call(f32[80,64]{1,0:T(8,128)S(1)} %get-tuple-element.29.mid_ref, f32[80,64]{1,0:T(8,128)S(1)} %collective-permute-done.11.a_ref, f32[80,64]{1,0:T(8,128)S(1)} %collective-permute-done.12.b_ref), custom_call_target="tpu_custom_call" | custom-call | tf_op jit(solution)/shard_map/final/pallas_call | solution.py:397
Async XLA Ops:
  3.3 13.3 %collective-permute-start = (bf16[128,768]{1,0:T(8,128)(2,1)S(1)}, bf16[128,768]{1,0:T(8,128)(2,1)S(1)}, u32[]{:S(2)}, u32[]{:S(2)}) collective-permute-start(bf16[128,768]{1,0:T(8,128)(2,1)S(1)} %get-tuple-element.25), channel_id=1, source_target_pairs={{0,62},{1,63},{2,0},{3,1},{4,2},{5,3},{6,4},{7,5},{8,6},{9,7},{10,... | collective-permute-start | bytes 589832 | tf_op jit(solution)/shard_map/ppermute | solution.py:20
  11.7 6.3 %collective-permute-start.2 = (bf16[128,768]{1,0:T(8,128)(2,1)S(1)}, bf16[128,768]{1,0:T(8,128)(2,1)S(1)}, u32[]{:S(2)}, u32[]{:S(2)}) collective-permute-start(bf16[128,768]{1,0:T(8,128)(2,1)S(1)} %get-tuple-element.26), channel_id=1, source_target_pairs={{0,63},{1,0},{2,1},{3,2},{4,3},{5,4},{6,5},{7,6},{8,7},{9,8},{10,9... | collective-permute-start | bytes 589832 | tf_op jit(solution)/shard_map/ppermute | solution.py:20
  12.7 9.7 %collective-permute-start.4 = (bf16[128,768]{1,0:T(8,128)(2,1)S(1)}, bf16[128,768]{1,0:T(8,128)(2,1)S(1)}, u32[]{:S(2)}, u32[]{:S(2)}) collective-permute-start(bf16[128,768]{1,0:T(8,128)(2,1)S(1)} %get-tuple-element.27), channel_id=1, source_target_pairs={{0,1},{1,2},{2,3},{3,4},{4,5},{5,6},{6,7},{7,8},{8,9},{9,10},{10,1... | collective-permute-start | bytes 589832 | tf_op jit(solution)/shard_map/ppermute | solution.py:20
  13.1 12.5 %collective-permute-start.6 = (bf16[128,768]{1,0:T(8,128)(2,1)S(1)}, bf16[128,768]{1,0:T(8,128)(2,1)S(1)}, u32[]{:S(2)}, u32[]{:S(2)}) collective-permute-start(bf16[128,768]{1,0:T(8,128)(2,1)S(1)} %get-tuple-element.28), channel_id=1, source_target_pairs={{0,2},{1,3},{2,4},{3,5},{4,6},{5,7},{6,8},{7,9},{8,10},{9,11},{10,... | collective-permute-start | bytes 589832 | tf_op jit(solution)/shard_map/ppermute | solution.py:20
  17.7 10.9 %collective-permute-start.1 = (f32[16,768]{1,0:T(8,128)S(1)}, f32[16,768]{1,0:T(8,128)S(1)}, u32[]{:S(2)}, u32[]{:S(2)}) collective-permute-start(f32[16,768]{1,0:T(8,128)S(1)} %answer.4.refs_2_), channel_id=1, source_target_pairs={{0,2},{1,3},{2,4},{3,5},{4,6},{5,7},{6,8},{7,9},{8,10},{9,11},{10,... | collective-permute-start | bytes 147464 | tf_op jit(solution)/shard_map/ppermute | solution.py:20
  19.0 9.5 %collective-permute-start.3 = (f32[16,768]{1,0:T(8,128)S(1)}, f32[16,768]{1,0:T(8,128)S(1)}, u32[]{:S(2)}, u32[]{:S(2)}) collective-permute-start(f32[16,768]{1,0:T(8,128)S(1)} %answer.5.refs_2_), channel_id=1, source_target_pairs={{0,1},{1,2},{2,3},{3,4},{4,5},{5,6},{6,7},{7,8},{8,9},{9,10},{10,1... | collective-permute-start | bytes 147464 | tf_op jit(solution)/shard_map/ppermute | solution.py:20
  23.5 5.1 %copy-start.3 = (s32[1024,4]{0,1:T(4,128)S(1)}, s32[1024,4]{0,1:T(4,128)}, u32[]{:S(2)}) copy-start(s32[1024,4]{0,1:T(4,128)} %param.11) | copy-start | bytes 49156
  23.5 5.1 %copy-start.4 = (f32[1024,4]{0,1:T(4,128)S(1)}, f32[1024,4]{0,1:T(4,128)}, u32[]{:S(2)}) copy-start(f32[1024,4]{0,1:T(4,128)} %param.10) | copy-start | bytes 49156
  23.5 7.5 %collective-permute-start.5 = (f32[16,768]{1,0:T(8,128)S(1)}, f32[16,768]{1,0:T(8,128)S(1)}, u32[]{:S(2)}, u32[]{:S(2)}) collective-permute-start(f32[16,768]{1,0:T(8,128)S(1)} %answer.6.refs_2_), channel_id=1, source_target_pairs={{0,63},{1,0},{2,1},{3,2},{4,3},{5,4},{6,5},{7,6},{8,7},{9,8},{10,9... | collective-permute-start | bytes 147464 | tf_op jit(solution)/shard_map/ppermute | solution.py:20
  26.7 12.3 %copy-start = (f32[1024]{0:T(1024)S(1)}, f32[1024]{0:T(1024)}, u32[]{:S(2)}) copy-start(f32[1024]{0:T(1024)} %param.13) | copy-start | bytes 12292
  26.7 12.2 %copy-start.1 = (f32[1024]{0:T(1024)S(1)}, f32[1024]{0:T(1024)}, u32[]{:S(2)}) copy-start(f32[1024]{0:T(1024)} %param.14) | copy-start | bytes 12292
  26.8 12.2 %copy-start.2 = (s32[1024]{0:T(1024)S(1)}, s32[1024]{0:T(1024)}, u32[]{:S(2)}) copy-start(s32[1024]{0:T(1024)} %param.15) | copy-start | bytes 12292
  26.8 4.2 %collective-permute-start.7 = (f32[16,768]{1,0:T(8,128)S(1)}, f32[16,768]{1,0:T(8,128)S(1)}, u32[]{:S(2)}, u32[]{:S(2)}) collective-permute-start(f32[16,768]{1,0:T(8,128)S(1)} %answer.7), channel_id=1, source_target_pairs={{0,62},{1,63},{2,0},{3,1},{4,2},{5,3},{6,4},{7,5},{8,6},{9,7},{10,... | collective-permute-start | bytes 147464 | tf_op jit(solution)/shard_map/ppermute | solution.py:20
  31.6 4.3 %collective-permute-start.10 = (f32[8,1280]{1,0:T(8,128)S(1)}, f32[8,1280]{1,0:T(8,128)S(1)}, u32[]{:S(2)}, u32[]{:S(2)}) collective-permute-start(f32[8,1280]{1,0:T(8,128)S(1)} %combine.3.refs_0_), channel_id=1, source_target_pairs={{0,192},{64,128},{128,64},{192,0},{1,193},{65,129},{129,65},{193,1... | collective-permute-start | bytes 122888 | tf_op jit(solution)/shard_map/ppermute | solution.py:24
  32.3 5.5 %collective-permute-start.9 = (f32[8,1280]{1,0:T(8,128)S(1)}, f32[8,1280]{1,0:T(8,128)S(1)}, u32[]{:S(2)}, u32[]{:S(2)}) collective-permute-start(f32[8,1280]{1,0:T(8,128)S(1)} %combine.3.refs_0_), channel_id=1, source_target_pairs={{0,128},{64,192},{128,0},{192,64},{1,129},{65,193},{129,1},{193,65... | collective-permute-start | bytes 122888 | tf_op jit(solution)/shard_map/ppermute | solution.py:24
  35.0 4.0 %collective-permute-start.8 = (f32[8,1280]{1,0:T(8,128)S(1)}, f32[8,1280]{1,0:T(8,128)S(1)}, u32[]{:S(2)}, u32[]{:S(2)}) collective-permute-start(f32[8,1280]{1,0:T(8,128)S(1)} %combine.3.refs_0_), channel_id=1, source_target_pairs={{0,64},{64,0},{128,192},{192,128},{1,65},{65,1},{129,193},{193,129... | collective-permute-start | bytes 122888 | tf_op jit(solution)/shard_map/ppermute | solution.py:24
  39.6 6.8 %collective-permute-start.11 = (f32[80,64]{1,0:T(8,128)S(1)}, f32[80,64]{1,0:T(8,128)S(1)}, u32[]{:S(2)}, u32[]{:S(2)}) collective-permute-start(f32[80,64]{1,0:T(8,128)S(1)} %get-tuple-element.30), channel_id=1, source_target_pairs={{0,1},{1,2},{2,3},{3,4},{4,5},{5,6},{6,7},{7,8},{8,9},{9,10},{10,1... | collective-permute-start | bytes 61448 | tf_op jit(solution)/shard_map/ppermute | solution.py:20
  39.7 6.7 %collective-permute-start.12 = (f32[80,64]{1,0:T(8,128)S(1)}, f32[80,64]{1,0:T(8,128)S(1)}, u32[]{:S(2)}, u32[]{:S(2)}) collective-permute-start(f32[80,64]{1,0:T(8,128)S(1)} %get-tuple-element.31), channel_id=1, source_target_pairs={{0,63},{1,0},{2,1},{3,2},{4,3},{5,4},{6,5},{7,6},{8,7},{9,8},{10,9... | collective-permute-start | bytes 61448 | tf_op jit(solution)/shard_map/ppermute | solution.py:20
